TPU v7x, 32 devices: a whole 2x2x4 slice. The times are simulated.
32 devices in a mesh: dp: 4 (over x, core), expert: 8 (over z, y).
Axes of the slice: x: 2, y: 2, z: 4, core: 2. Of those that a mesh axis runs over, the one named last changes fastest.
Arguments:
- tokens: bfloat16 [32768, 512], P(('dp', 'expert')), may hold values from -6 to 6
- cotangent: bfloat16 [32768, 512], P(('dp', 'expert')), may hold values from -6 to 6
- valid: int32 [128, 256], P(('dp', 'expert')), may hold values from 0 to 1, as said below
- routes: int32 [2, 32768, 2], P(None, ('dp', 'expert')), may hold values from 0 to 7, all different within a row
- priority: int32 [64, 512], P(('dp', 'expert')), may hold values from 0 to 511, each once within a row
- step: int32 [], replicated, may hold values from 1 to 20
- dense_master: float32 [2, 2064, 512], P(None, 'dp'), may hold values from -2 to 2
- dense_first: float32 [2, 2064, 512], P(None, 'dp'), may hold values from -0.00024414062 to 0.00024414062
- dense_second: float32 [2, 2064, 512], P(None, 'dp'), may hold values from 1.4194222e-09 to 1.4194222e-07
- expert_master: float32 [2, 8, 1024, 2048], P(None, 'expert', 'dp'), may hold values from -0.494974747 to 0.494974747
- expert_first: float32 [2, 8, 1024, 2048], P(None, 'expert', 'dp'), may hold values from -0.00024414062 to 0.00024414062
- expert_second: float32 [2, 8, 1024, 2048], P(None, 'expert', 'dp'), may hold values from 2.8004202e-10 to 8.40126e-09
- shift_master: float32 [2, 8, 2560], P(None, 'expert', 'dp'), may hold values from -5.6 to 5.6
- shift_first: float32 [2, 8, 2560], P(None, 'expert', 'dp'), may hold values from -0.00024414062 to 0.00024414062
- shift_second: float32 [2, 8, 2560], P(None, 'expert', 'dp'), may hold values from 2.8004202e-10 to 8.40126e-09
Outputs:
- output: float32 [32768, 512], P(('dp', 'expert'))
- grad_tokens: float32 [32768, 512], P(('dp', 'expert'))
- grad_norm: float32 [], replicated
- dense_grad: float32 [2, 2064, 512], P(None, 'dp')
- dense_update: float32 [2, 2064, 512], P(None, 'dp')
- dense_first_new: float32 [2, 2064, 512], P(None, 'dp')
- dense_second_new: float32 [2, 2064, 512], P(None, 'dp')
- expert_grad: float32 [2, 8, 1024, 2048], P(None, 'expert', 'dp')
- expert_update: float32 [2, 8, 1024, 2048], P(None, 'expert', 'dp')
- expert_first_new: float32 [2, 8, 1024, 2048], P(None, 'expert', 'dp')
- expert_second_new: float32 [2, 8, 1024, 2048], P(None, 'expert', 'dp')
- shift_grad: float32 [2, 8, 2560], P(None, 'expert', 'dp')
- shift_update: float32 [2, 8, 2560], P(None, 'expert', 'dp')
- shift_first_new: float32 [2, 8, 2560], P(None, 'expert', 'dp')
- shift_second_new: float32 [2, 8, 2560], P(None, 'expert', 'dp')
Inputs may be any that keep to these rules, and one draw needn't show every extreme that they name: `valid`: each image's row is 0 everywhere, or 1 exactly in its first 197 slots. `routes`: each token names two different experts. `priority`: each row holds every rank of 0 to 511 once.
All inputs are finite; a program needn't handle non-finite values.
Results may differ from a plain program's by a relative error of at most 0.022.
Values may be sent and summed in bfloat16 or wider, within the bound.
A program may use at most 320 MiB of HBM per device.

v0:
```python
import jax
import jax.numpy as jnp
from jax import lax
from jax.sharding import PartitionSpec as P

HEADS = 8
PATCHES = 197


NORM_EPS = 1e-06
NEG_FILL = -1e30
CLIP_NORM = 1.0
BETA_ONE = 0.9
BETA_TWO = 0.95
STEP_RATE = 0.01
DECAY_RATE = 0.1
ADAM_EPS = 1e-08


def norm_rows(values, gain_row, shift_row):
    centred = values - jnp.mean(values, axis=-1, keepdims=True)
    spread = jnp.mean(centred * centred, axis=-1, keepdims=True)
    return centred * lax.rsqrt(spread + NORM_EPS) * gain_row + shift_row


def erf_gelu(values):
    return jax.nn.gelu(values, approximate=False)


def dot_rows(left_side, right_side):
    return lax.dot_general(
        left_side, right_side, (((1,), (1,)), ((), ())), preferred_element_type=jnp.float32
    )


def placement(routed, ranking, usable, experts, capacity):
    tok_count = routed.shape[0]
    positions = jnp.arange(tok_count, dtype=jnp.int32)
    ordering = jnp.zeros((tok_count,), jnp.int32).at[ranking].set(positions)
    labels = jnp.arange(experts, dtype=jnp.int32)
    one_hot = (routed[ordering][:, :, None] == labels).astype(jnp.int32) * usable[ordering][
        :, None, None
    ]
    earlier = jnp.cumsum(one_hot, axis=0) - one_hot
    first_total = jnp.sum(one_hot[:, 0], axis=0)
    pos_first = jnp.sum(earlier[:, 0] * one_hot[:, 0], axis=-1)
    pos_second = jnp.sum((earlier[:, 1] + first_total[None, :]) * one_hot[:, 1], axis=-1)
    ranked = jnp.stack([pos_first, pos_second], axis=-1)
    position = ranked[ranking]
    keeping = (position < capacity) & (usable[:, None] > 0)
    slot_index = jnp.where(keeping, routed * capacity + position, experts * capacity)
    slot_source = jnp.full((experts * capacity + 1,), tok_count, jnp.int32)
    slot_source = (
        slot_source.at[slot_index[:, 0]].set(positions).at[slot_index[:, 1]].set(positions)
    )
    return (slot_index, keeping.astype(jnp.float32), slot_source)


def split_rows(row_block, model_width, experts):
    qkv_rows = row_block[: 3 * model_width]
    out_rows = row_block[3 * model_width : 4 * model_width]
    router_rows = row_block[4 * model_width : 4 * model_width + experts]
    vectors = row_block[4 * model_width + experts :].astype(jnp.float32)
    return (qkv_rows, out_rows, router_rows, vectors)


def forward_layer(
    inputs, key_ok, tok_ok, routed, ranking, row_block, mat_block, shift_block, experts, capacity
):
    tok_count, model_width = inputs.shape
    images, slots_img = key_ok.shape
    head_size = model_width // HEADS
    scale_qk = head_size ** (-0.5)
    qkv_rows, out_rows, router_rows, vectors = split_rows(row_block, model_width, experts)
    normed_a = norm_rows(inputs, vectors[0], vectors[1]).astype(jnp.bfloat16)
    qkv_low = (dot_rows(normed_a, qkv_rows) + vectors[2:5].reshape(-1)).astype(jnp.bfloat16)
    qkv_parts = qkv_low.reshape(images, slots_img, 3, HEADS, head_size)
    scores = (
        jnp.einsum(
            "bqhd,bkhd->bhqk",
            qkv_parts[:, :, 0],
            qkv_parts[:, :, 1],
            preferred_element_type=jnp.float32,
        )
        * scale_qk
    )
    scores = jnp.where(key_ok[:, None, None, :], scores, NEG_FILL)
    row_peak = jnp.max(scores, axis=-1, keepdims=True)
    exponent = jnp.exp(scores - row_peak)
    totals = jnp.sum(exponent, axis=-1, keepdims=True)
    weights = exponent / totals
    log_total = row_peak + jnp.log(totals)
    attended = jnp.einsum(
        "bhqk,bkhd->bqhd",
        weights.astype(jnp.bfloat16),
        qkv_parts[:, :, 2],
        preferred_element_type=jnp.float32,
    )
    attended = attended.reshape(tok_count, model_width).astype(jnp.bfloat16)
    x_mid = inputs + (jnp.dot(attended, out_rows, preferred_element_type=jnp.float32) + vectors[5])
    normed_c = norm_rows(x_mid, vectors[6], vectors[7]).astype(jnp.bfloat16)
    router = jax.nn.softmax(dot_rows(normed_c, router_rows), axis=-1)
    choose = (routed[:, :, None] == jnp.arange(experts, dtype=jnp.int32)).astype(jnp.float32)
    gate_values = jnp.sum(router[:, None, :] * choose, axis=-1)
    slot_index, keeping, slot_source = placement(routed, ranking, tok_ok, experts, capacity)
    groups = lax.axis_size("expert")
    local_exp = mat_block.shape[0]
    hidden = mat_block.shape[2]
    padded = jnp.concatenate([normed_c, jnp.zeros((1, model_width), jnp.bfloat16)], axis=0)
    buffer = padded[slot_source[: experts * capacity]].reshape(
        groups, local_exp, capacity, model_width
    )
    weight_in = mat_block[:, :model_width]
    weight_out = mat_block[:, model_width:]
    shift_in = shift_block[:, :hidden].astype(jnp.float32)
    shift_out = shift_block[:, hidden:].astype(jnp.float32)
    received = lax.all_to_all(buffer, "expert", split_axis=0, concat_axis=0, tiled=True)
    hidden_pre = (
        jnp.einsum("sjcd,jdf->sjcf", received, weight_in, preferred_element_type=jnp.float32)
        + shift_in[None, :, None, :]
    )
    active = erf_gelu(hidden_pre).astype(jnp.bfloat16)
    produced = (
        jnp.einsum("sjcf,jdf->sjcd", active, weight_out, preferred_element_type=jnp.float32)
        + shift_out[None, :, None, :]
    )
    returned = lax.all_to_all(
        produced.astype(jnp.bfloat16), "expert", split_axis=0, concat_axis=0, tiled=True
    )
    returned, received, hidden_pre = (returned, received, hidden_pre)
    flat_rows = jnp.concatenate(
        [
            returned.reshape(experts * capacity, model_width),
            jnp.zeros((1, model_width), jnp.bfloat16),
        ],
        axis=0,
    )
    picked = flat_rows[slot_index].astype(jnp.float32)
    mixing = keeping * gate_values
    x_out = x_mid + jnp.sum(mixing[:, :, None] * picked, axis=1)
    kept_state = (
        inputs,
        key_ok,
        routed,
        normed_a,
        qkv_low,
        log_total,
        attended,
        x_mid,
        normed_c,
        router,
        gate_values,
        slot_index,
        keeping,
        slot_source,
        picked,
        received,
        hidden_pre,
    )
    return (x_out, kept_state)


def backward_layer(grad_out, kept_state, row_block, mat_block, experts, capacity):
    (
        inputs,
        key_ok,
        routed,
        normed_a,
        qkv_low,
        log_total,
        attended,
        x_mid,
        normed_c,
        router,
        gate_values,
        slot_index,
        keeping,
        slot_source,
        picked,
        received,
        hidden_pre,
    ) = kept_state
    tok_count, model_width = inputs.shape
    images, slots_img = key_ok.shape
    head_size = model_width // HEADS
    scale_qk = head_size ** (-0.5)
    qkv_rows, out_rows, router_rows, vectors = split_rows(row_block, model_width, experts)
    groups = lax.axis_size("expert")
    local_exp = mat_block.shape[0]
    slot_total = experts * capacity
    weight_in = mat_block[:, :model_width]
    weight_out = mat_block[:, model_width:]
    mixing = keeping * gate_values
    grad_gates = keeping * jnp.sum(grad_out[:, None, :] * picked, axis=-1)
    slot_gate = (
        jnp.zeros((slot_total + 1,), jnp.float32).at[slot_index.reshape(-1)].set(mixing.reshape(-1))
    )
    grad_pad = jnp.concatenate([grad_out, jnp.zeros((1, model_width), jnp.float32)], axis=0)
    slot_grad = (grad_pad[slot_source[:slot_total]] * slot_gate[:slot_total, None]).astype(
        jnp.bfloat16
    )
    slot_grad = slot_grad.reshape(groups, local_exp, capacity, model_width)
    grad_recv = lax.all_to_all(slot_grad, "expert", split_axis=0, concat_axis=0, tiled=True)
    active = erf_gelu(hidden_pre).astype(jnp.bfloat16)
    grad_active = jnp.einsum(
        "sjcd,jdf->sjcf", grad_recv, weight_out, preferred_element_type=jnp.float32
    )
    gelu_out, gelu_pull = jax.vjp(erf_gelu, hidden_pre)
    grad_pre = gelu_pull(grad_active)[0].astype(jnp.bfloat16)
    grad_sent = jnp.einsum(
        "sjcf,jdf->sjcd", grad_pre, weight_in, preferred_element_type=jnp.float32
    ).astype(jnp.bfloat16)
    grad_back = lax.all_to_all(grad_sent, "expert", split_axis=0, concat_axis=0, tiled=True)
    grad_w_in = jnp.einsum("sjcd,sjcf->jdf", received, grad_pre, preferred_element_type=jnp.float32)
    grad_w_out = jnp.einsum("sjcd,sjcf->jdf", grad_recv, active, preferred_element_type=jnp.float32)
    grad_s_in = jnp.sum(grad_pre, axis=(0, 2), dtype=jnp.float32)
    grad_s_out = jnp.sum(grad_recv, axis=(0, 2), dtype=jnp.float32)
    mats_grad = jnp.concatenate([grad_w_in, grad_w_out], axis=1)
    shift_grad = jnp.concatenate([grad_s_in, grad_s_out], axis=-1)
    back_flat = jnp.concatenate(
        [grad_back.reshape(slot_total, model_width), jnp.zeros((1, model_width), jnp.bfloat16)],
        axis=0,
    )
    grad_c = jnp.sum(keeping[:, :, None] * back_flat[slot_index].astype(jnp.float32), axis=1)
    choose = (routed[:, :, None] == jnp.arange(experts, dtype=jnp.int32)).astype(jnp.float32)
    grad_router = jnp.sum(grad_gates[:, :, None] * choose, axis=1)
    grad_logits = (
        router * (grad_router - jnp.sum(grad_router * router, axis=-1, keepdims=True))
    ).astype(jnp.bfloat16)
    router_grad = jnp.einsum("ne,nd->ed", grad_logits, normed_c, preferred_element_type=jnp.float32)
    grad_c = grad_c + jnp.dot(grad_logits, router_rows, preferred_element_type=jnp.float32)
    second_out, second_pull = jax.vjp(norm_rows, x_mid, vectors[6], vectors[7])
    grad_mid_n, grad_gain2, grad_shift2 = second_pull(grad_c)
    grad_mid = grad_out + grad_mid_n
    grad_branch = grad_mid.astype(jnp.bfloat16)
    grad_bias_o = jnp.sum(grad_branch, axis=0, dtype=jnp.float32)
    out_grad = jnp.einsum("nd,ne->de", attended, grad_branch, preferred_element_type=jnp.float32)
    grad_att = (
        dot_rows(grad_branch, out_rows)
        .astype(jnp.bfloat16)
        .reshape(images, slots_img, HEADS, head_size)
    )
    qkv_parts = qkv_low.reshape(images, slots_img, 3, HEADS, head_size)
    queries = qkv_parts[:, :, 0]
    keys_all = qkv_parts[:, :, 1]
    values_all = qkv_parts[:, :, 2]
    scores = (
        jnp.einsum("bqhd,bkhd->bhqk", queries, keys_all, preferred_element_type=jnp.float32)
        * scale_qk
    )
    weights = jnp.where(key_ok[:, None, None, :], jnp.exp(scores - log_total), 0.0)
    grad_weights = jnp.einsum(
        "bqhd,bkhd->bhqk", grad_att, values_all, preferred_element_type=jnp.float32
    )
    grad_values = jnp.einsum(
        "bhqk,bqhd->bkhd",
        weights.astype(jnp.bfloat16),
        grad_att,
        preferred_element_type=jnp.float32,
    )
    grad_scores = weights * (grad_weights - jnp.sum(grad_weights * weights, axis=-1, keepdims=True))
    grad_scores = jnp.where(key_ok[:, None, None, :], grad_scores, 0.0).astype(jnp.bfloat16)
    grad_queries = (
        jnp.einsum("bhqk,bkhd->bqhd", grad_scores, keys_all, preferred_element_type=jnp.float32)
        * scale_qk
    )
    grad_keys = (
        jnp.einsum("bhqk,bqhd->bkhd", grad_scores, queries, preferred_element_type=jnp.float32)
        * scale_qk
    )
    grad_qkv = (
        jnp.stack([grad_queries, grad_keys, grad_values], axis=2)
        .reshape(tok_count, 3 * model_width)
        .astype(jnp.bfloat16)
    )
    grad_bias_qkv = jnp.sum(grad_qkv, axis=0, dtype=jnp.float32)
    qkv_grad = jnp.einsum("nj,nd->jd", grad_qkv, normed_a, preferred_element_type=jnp.float32)
    grad_a = jnp.dot(grad_qkv, qkv_rows, preferred_element_type=jnp.float32)
    first_out, first_pull = jax.vjp(norm_rows, inputs, vectors[0], vectors[1])
    grad_in_n, grad_gain1, grad_shift1 = first_pull(grad_a)
    grad_in = grad_mid + grad_in_n
    vector_grad = jnp.concatenate(
        [
            grad_gain1[None],
            grad_shift1[None],
            grad_bias_qkv.reshape(3, model_width),
            grad_bias_o[None],
            grad_gain2[None],
            grad_shift2[None],
        ],
        axis=0,
    )
    rows_grad = jnp.concatenate([qkv_grad, out_grad, router_grad, vector_grad], axis=0)
    return (grad_in, rows_grad, mats_grad, shift_grad)


def adam_update(master, first_mom, second_mom, gradient, clip_scale, step_float):
    clipped = gradient * clip_scale
    first_new = BETA_ONE * first_mom + (1.0 - BETA_ONE) * clipped
    second_new = BETA_TWO * second_mom + (1.0 - BETA_TWO) * clipped * clipped
    first_hat = first_new / (1.0 - BETA_ONE**step_float)
    second_hat = second_new / (1.0 - BETA_TWO**step_float)
    change = -STEP_RATE * (first_hat / (jnp.sqrt(second_hat) + ADAM_EPS) + DECAY_RATE * master)
    return (change, first_new, second_new)


def local(
    tokens,
    cotangent,
    valid,
    routes,
    priority,
    step,
    dense_master,
    dense_first,
    dense_second,
    expert_master,
    expert_first,
    expert_second,
    shift_master,
    shift_first,
    shift_second,
):
    layer_count = dense_master.shape[0]
    micro_count = priority.shape[0]
    group_tok = priority.shape[1]
    slots_img = valid.shape[1]
    images_mb = group_tok // slots_img
    local_exp = expert_master.shape[1]
    experts = local_exp * lax.axis_size("expert")
    capacity = (9 * images_mb * PATCHES + 4 * experts - 1) // (4 * experts)
    expert_low, shift_low = (
        lax.all_gather(expert_master.astype(jnp.bfloat16), "dp", axis=2, tiled=True),
        lax.all_gather(shift_master.astype(jnp.bfloat16), "dp", axis=2, tiled=True),
    )
    dense_low = dense_master.astype(jnp.bfloat16)

    def dense_layer(layer_id):
        return lax.all_gather(dense_low[layer_id], "dp", axis=0, tiled=True)

    dense_sums = []
    mats_sums = []
    shift_sums = []
    outputs = []
    input_grads = []
    for micro_id in range(micro_count):
        row_start = micro_id * group_tok
        image_rows = valid[micro_id * images_mb : (micro_id + 1) * images_mb]
        key_ok = image_rows > 0
        tok_ok = image_rows.reshape(-1)
        ranking = priority[micro_id]
        current = tokens[row_start : row_start + group_tok].astype(jnp.float32)
        kept_all = []
        for layer_id in range(layer_count):
            routed = routes[layer_id, row_start : row_start + group_tok]
            current, kept_state = forward_layer(
                current,
                key_ok,
                tok_ok,
                routed,
                ranking,
                dense_layer(layer_id),
                expert_low[layer_id],
                shift_low[layer_id],
                experts,
                capacity,
            )
            kept_all.append(kept_state)
        outputs.append(jnp.where(tok_ok[:, None] > 0, current, 0.0))
        grad_state = jnp.where(
            tok_ok[:, None] > 0,
            cotangent[row_start : row_start + group_tok].astype(jnp.float32),
            0.0,
        )
        for layer_id in reversed(range(layer_count)):
            grad_state, rows_grad, mats_grad, shift_grad = backward_layer(
                grad_state,
                kept_all[layer_id],
                dense_layer(layer_id),
                expert_low[layer_id],
                experts,
                capacity,
            )
            if micro_id == 0:
                dense_sums.insert(0, rows_grad)
                mats_sums.insert(0, mats_grad)
                shift_sums.insert(0, shift_grad)
            else:
                dense_sums[layer_id] = dense_sums[layer_id] + rows_grad
                mats_sums[layer_id] = mats_sums[layer_id] + mats_grad
                shift_sums[layer_id] = shift_sums[layer_id] + shift_grad
        input_grads.append(grad_state)
    dense_grad = jnp.stack(dense_sums)
    mats_grad = jnp.stack(mats_sums)
    shift_grad = jnp.stack(shift_sums)
    dense_total = lax.psum(dense_grad.astype(jnp.bfloat16), "expert")
    dense_shard = lax.psum_scatter(dense_total, "dp", scatter_dimension=1, tiled=True).astype(
        jnp.float32
    )
    expert_shard, shift_shard = (
        lax.psum_scatter(
            mats_grad.astype(jnp.bfloat16), "dp", scatter_dimension=2, tiled=True
        ).astype(jnp.float32),
        lax.psum_scatter(
            shift_grad.astype(jnp.bfloat16), "dp", scatter_dimension=2, tiled=True
        ).astype(jnp.float32),
    )
    first_replica = (lax.axis_index("expert") == 0).astype(jnp.float32)
    dense_square = jnp.sum(dense_shard * dense_shard) * first_replica
    expert_square = jnp.sum(expert_shard * expert_shard) + jnp.sum(shift_shard * shift_shard)
    dense_sq_all, expert_sq_all = lax.psum((dense_square, expert_square), ("dp", "expert"))
    grad_norm = jnp.sqrt(dense_sq_all + expert_sq_all)
    clip_scale = CLIP_NORM / jnp.maximum(grad_norm, CLIP_NORM)
    step_float = step.astype(jnp.float32)
    dense_new = adam_update(
        dense_master, dense_first, dense_second, dense_shard, clip_scale, step_float
    )
    expert_new = adam_update(
        expert_master, expert_first, expert_second, expert_shard, clip_scale, step_float
    )
    shift_new = adam_update(
        shift_master, shift_first, shift_second, shift_shard, clip_scale, step_float
    )
    return (
        jnp.concatenate(outputs, axis=0),
        jnp.concatenate(input_grads, axis=0),
        grad_norm,
        dense_shard,
        dense_new[0],
        dense_new[1],
        dense_new[2],
        expert_shard,
        expert_new[0],
        expert_new[1],
        expert_new[2],
        shift_shard,
        shift_new[0],
        shift_new[1],
        shift_new[2],
    )


def solution(mesh):
    placed = (
        P(("dp", "expert"), None),
        P(("dp", "expert"), None),
        P(("dp", "expert"), None),
        P(None, ("dp", "expert"), None),
        P(("dp", "expert"), None),
        P(),
        P(None, "dp", None),
        P(None, "dp", None),
        P(None, "dp", None),
        P(None, "expert", "dp", None),
        P(None, "expert", "dp", None),
        P(None, "expert", "dp", None),
        P(None, "expert", "dp"),
        P(None, "expert", "dp"),
        P(None, "expert", "dp"),
    )
    return jax.shard_map(
        local,
        mesh=mesh,
        in_specs=placed,
        out_specs=(
            P(("dp", "expert"), None),
            P(("dp", "expert"), None),
            P(),
            P(None, "dp", None),
            P(None, "dp", None),
            P(None, "dp", None),
            P(None, "dp", None),
            P(None, "expert", "dp", None),
            P(None, "expert", "dp", None),
            P(None, "expert", "dp", None),
            P(None, "expert", "dp", None),
            P(None, "expert", "dp"),
            P(None, "expert", "dp"),
            P(None, "expert", "dp"),
            P(None, "expert", "dp"),
        ),
        check_vma=False,
    )
```

profile of v0, /device:TPU:0, one launch (start us, length us, event | category | flops | bytes accessed | tf_op | source)
XLA Modules:
  0.0 1394.3 jit_solution(14457680251476159607)
XLA Ops:
  66.1 6.3 all_gather.20
  145.5 5.1 reshape.3033
  163.2 5.2 reshape.3035
  204.0 6.6 all-to-all-start.4
  223.7 6.1 slice_bitcast_fusion
  245.0 17.4 %fusion.378 = bf16[8,1,111,512]{3,2,1,0:T(8,128)(2,1)} fusion(bf16[1,1024,2048]{2,1,0:T(8,128)(2,1)S(1)} %copy-done.90, f32[512]{0:T(512)S(1)} %bitcast.1467, f32[8,111,2048]{2,1,0:T(8,128)S(1)} %fusion.312, f32[2048]{0:T(1024)S(1)} %bitcast.1419), kind=kOutput, calls=%fused_computation.456 | convolution fusion | flops 1983209472 | bytes 10356736 | tf_op jit(solution)/shard_map/sjcf,jdf->sjcd/dot_general | solution.py:124
  262.3 6.1 all-to-all-start.5
  275.4 17.3 %fusion.376 = bf16[8,1,111,512]{3,2,1,0:T(8,128)(2,1)} fusion(bf16[1,1024,2048]{2,1,0:T(8,128)(2,1)S(1)} %copy-done.91, f32[512]{0:T(512)S(1)} %bitcast.1468, f32[8,111,2048]{2,1,0:T(8,128)S(1)} %fusion.313, f32[2048]{0:T(1024)S(1)} %bitcast.1420), kind=kOutput, calls=%fused_computation.454 | convolution fusion | flops 1983209472 | bytes 10356736 | tf_op jit(solution)/shard_map/sjcf,jdf->sjcd/dot_general | solution.py:124
  292.7 6.0 all-to-all-start.1
  299.0 5.1 gather_fusion.13
  314.6 5.0 reshape.3036
  334.1 5.1 gather_fusion.4
  350.5 5.0 reshape.3034
  386.3 6.0 all-to-all-start.6
  407.5 6.7 all-to-all-done.6
  425.0 17.3 %fusion.379 = bf16[8,1,111,512]{3,2,1,0:T(8,128)(2,1)} fusion(bf16[1,1024,2048]{2,1,0:T(8,128)(2,1)S(1)} %copy-done.94, f32[512]{0:T(512)S(1)} %bitcast.1465, f32[8,111,2048]{2,1,0:T(8,128)S(1)} %fusion.314, f32[2048]{0:T(1024)S(1)} %bitcast.1425), kind=kOutput, calls=%fused_computation.457 | convolution fusion | flops 1983209472 | bytes 10356736 | tf_op jit(solution)/shard_map/sjcf,jdf->sjcd/dot_general | solution.py:124
  442.3 6.1 all-to-all-start.12
  455.2 17.1 %fusion.377 = bf16[8,1,111,512]{3,2,1,0:T(8,128)(2,1)} fusion(bf16[1,1024,2048]{2,1,0:T(8,128)(2,1)S(1)} %copy-done.95, f32[512]{0:T(512)S(1)} %bitcast.1466, f32[8,111,2048]{2,1,0:T(8,128)S(1)} %fusion.315, f32[2048]{0:T(1024)S(1)} %bitcast.1426), kind=kOutput, calls=%fused_computation.455 | convolution fusion | flops 1983209472 | bytes 10356736 | tf_op jit(solution)/shard_map/sjcf,jdf->sjcd/dot_general | solution.py:124
  472.3 6.0 all-to-all-start.7
  478.3 21.1 %convert_reduce_fusion = (f32[2048]{0:T(1024)}, bf16[8,1,111,2048]{3,2,0,1:T(8,128)(2,1)S(1)}) fusion(bf16[1,1024,2048]{2,1,0:T(8,128)(2,1)} %get-tuple-element.152, bf16[8,1,111,512]{3,2,1,0:T(8,128)(2,1)S(1)} %all-to-all-done.12, f32[2048]{0:T(1024)S(1)} %bitcast.1427, f32[8,111,2048]{2,1,0:T(8,128)} %copy-done.342), kind=kOutput, calls=%fused_computation.125 | convolution fusion | flops 1998665728 | bytes 14000128 | tf_op jit(solution)/shard_map/sjcd,jdf->sjcf/dot_general | solution.py:205
  499.4 22.3 %convolution_bitcast_fusion = f32[1,512,2048]{2,1,0:T(8,128)} fusion(bf16[8,1,111,512]{3,2,1,0:T(8,128)(2,1)S(1)} %all-to-all-done.12, f32[8,111,2048]{2,1,0:T(8,128)} %copy-done.342, f32[2048]{0:T(1024)S(1)} %bitcast.1428), kind=kOutput, calls=%fused_computation.253 | convolution fusion | flops 1982300160 | bytes 12386304 | tf_op jit(solution)/shard_map/sjcd,sjcf->jdf/dot_general | solution.py:215
  525.5 6.4 all-to-all-start.13
  532.0 6.6 fusion.131
  545.3 6.5 multiply_reduce_fusion.8
  553.3 5.0 all-to-all-start.3
  588.1 9.2 fusion.331
  597.3 9.2 fusion.337
  613.1 6.3 all-to-all-start.8
  627.3 6.6 multiply_reduce_fusion.12
  649.6 10.8 concatenate.425
  661.4 21.4 %convert_reduce_fusion.1 = (f32[2048]{0:T(1024)S(1)}, bf16[8,1,111,2048]{3,2,0,1:T(8,128)(2,1)S(1)}) fusion(bf16[1,1024,2048]{2,1,0:T(8,128)(2,1)} %get-tuple-element.152, bf16[8,1,111,512]{3,2,1,0:T(8,128)(2,1)} %all-to-all-done.8, f32[2048]{0:T(1024)S(1)} %bitcast.1429, f32[8,111,2048]{2,1,0:T(8,128)} %copy-done.341), kind=kOutput, calls=%fused_computation.126 | convolution fusion | flops 1998665728 | bytes 14008320 | tf_op jit(solution)/shard_map/sjcd,jdf->sjcf/dot_general | solution.py:205
  687.7 6.2 all-to-all-start.9
  693.9 21.0 %convolution_bitcast_fusion.1 = f32[1,512,2048]{2,1,0:T(8,128)} fusion(bf16[8,1,111,512]{3,2,1,0:T(8,128)(2,1)} %all-to-all-done.8, f32[8,111,2048]{2,1,0:T(8,128)} %copy-done.341, f32[2048]{0:T(1024)S(1)} %bitcast.1430), kind=kOutput, calls=%fused_computation.254 | convolution fusion | flops 1982300160 | bytes 12386304 | tf_op jit(solution)/shard_map/sjcd,sjcf->jdf/dot_general | solution.py:215
  719.5 5.1 gather_fusion.19
  751.2 8.9 fusion.355
  760.2 9.0 fusion.361
  793.5 6.1 all-to-all-start.10
  802.1 12.5 concatenate.415
  823.5 21.5 %convert_reduce_fusion.3 = (f32[2048]{0:T(1024)}, bf16[8,1,111,2048]{3,2,0,1:T(8,128)(2,1)S(1)}) fusion(bf16[1,1024,2048]{2,1,0:T(8,128)(2,1)} %get-tuple-element.153, bf16[8,1,111,512]{3,2,1,0:T(8,128)(2,1)} %all-to-all-done.10, f32[2048]{0:T(1024)S(1)} %bitcast.1421, f32[8,111,2048]{2,1,0:T(8,128)} %copy-done.340), kind=kOutput, calls=%fused_computation.128 | convolution fusion | flops 1998665728 | bytes 14008320 | tf_op jit(solution)/shard_map/sjcd,jdf->sjcf/dot_general | solution.py:205
  849.7 6.2 all-to-all-start.11
  856.0 20.6 %convert_reduce_fusion.2 = (f32[2048]{0:T(1024)S(1)}, bf16[8,1,111,2048]{3,2,0,1:T(8,128)(2,1)S(1)}) fusion(bf16[1,1024,2048]{2,1,0:T(8,128)(2,1)} %get-tuple-element.153, bf16[8,1,111,512]{3,2,1,0:T(8,128)(2,1)S(1)} %all-to-all-done.14, f32[2048]{0:T(1024)S(1)} %bitcast.1422, f32[8,111,2048]{2,1,0:T(8,128)} %copy-done.339), kind=kOutput, calls=%fused_computation.127 | convolution fusion | flops 1998665728 | bytes 14000128 | tf_op jit(solution)/shard_map/sjcd,jdf->sjcf/dot_general | solution.py:205
  881.4 6.0 all-to-all-start.15
  887.4 5.5 add_convert_fusion
  909.4 5.1 gather_fusion.25
  938.3 8.4 fusion.319
  946.7 8.4 fusion.325
  972.7 9.0 fusion.343
  981.6 9.0 fusion.349
  1002.2 12.5 concatenate.405
  1014.8 12.9 concatenate.395
  1032.4 19.2 %copy.434 = bf16[2,2064,512]{2,0,1:T(2,128)(2,1)} copy(bf16[2,2064,512]{2,1,0:T(8,128)(2,1)S(1)} %pad_maximum_fusion.1) | data formatting | bytes 8454144 | tf_op jit(solution)/shard_map/stack | solution.py:393
  1064.0 14.4 %bitcast_reduce_fusion = bf16[2560,2]{1,0:T(8,128)(2,1)} fusion(bf16[2,1,2560]{1,0,2:T(2,128)(2,1)S(1)} %copy.451), kind=kLoop, calls=%fused_computation.458 | loop fusion | bytes 20480
  1078.5 21.4 %convolution_bitcast_fusion.3 = f32[1,512,2048]{2,1,0:T(8,128)} fusion(bf16[8,1,111,512]{3,2,1,0:T(8,128)(2,1)} %all-to-all-done.10, f32[8,111,2048]{2,1,0:T(8,128)} %copy-done.340, f32[2048]{0:T(1024)S(1)} %bitcast.1423), kind=kOutput, calls=%fused_computation.256 | convolution fusion | flops 1982300160 | bytes 12386304 | tf_op jit(solution)/shard_map/sjcd,sjcf->jdf/dot_general | solution.py:215
  1104.3 20.8 %convolution_bitcast_fusion.2 = f32[1,512,2048]{2,1,0:T(8,128)} fusion(bf16[8,1,111,512]{3,2,1,0:T(8,128)(2,1)S(1)} %copy-done.100, f32[8,111,2048]{2,1,0:T(8,128)} %copy-done.339, f32[2048]{0:T(1024)S(1)} %bitcast.1424), kind=kOutput, calls=%fused_computation.255 | convolution fusion | flops 1982300160 | bytes 12386304 | tf_op jit(solution)/shard_map/sjcd,sjcf->jdf/dot_general | solution.py:215
  1125.1 11.4 all-reduce.22.cloned.1.call-done
  1139.7 4.9 fusion.134
  1149.4 6.2 pad_maximum_fusion
  1168.3 76.0 %all-reduce.20.cloned.1.call-done = bf16[2,516,512]{2,0,1:T(2,128)(2,1)} async-done(((bf16[2,516,512]{2,0,1:T(2,128)(2,1)}), bf16[2,516,512]{2,0,1:T(2,128)(2,1)}) %all-reduce.20.cloned.1.call-update) | async-done | bytes 1056784 | tf_op jit(solution)/shard_map/psum | solution.py:396
  1244.4 5.3 multiply_reduce_fusion.5
  1250.3 67.6 %reduce-scatter.5.cloned.1.call-done = bf16[2,1,256,2048]{3,2,1,0:T(8,128)(2,1)} async-done(((bf16[2,1,1024,2048]{3,2,1,0:T(8,128)(2,1)}), bf16[2,1,256,2048]{3,2,1,0:T(8,128)(2,1)}) %reduce-scatter.5.cloned.1.call-update) | async-done | bytes 2097168 | tf_op jit(solution)/shard_map/reduce_scatter | solution.py:401
  1317.9 5.2 multiply_reduce_fusion
  1327.2 39.5 %psum.24 = f32[]{:T(128)} all-reduce(f32[]{:T(128)S(6)} %add.1004), channel_id=1, replica_groups=mesh['dp'=4,'expert'=8] {'dp','expert'}, use_global_device_ids=true, to_apply=%region_137.138 | all-reduce | flops 1 | bytes 8 | tf_op jit(solution)/shard_map/psum | solution.py:411
  1368.1 10.6 add_multiply_fusion.1
  1378.7 7.3 add_multiply_fusion
  (1215 shorter events, 578.4 us)
Async XLA Ops:
  7.2 126.0 %all-gather.8.cloned.1.call-start = ((), (), s32[]{:S(2)}) async-start(), calls=%async_computation.20 | async-start | bytes 5283840 | tf_op jit(solution)/shard_map/all_gather | solution.py:339
  12.1 122.1 %all-gather.10.cloned.1.call-start = ((), (), s32[]{:S(2)}) async-start(), calls=%async_computation.21 | async-start | bytes 5283840 | tf_op jit(solution)/shard_map/all_gather | solution.py:339
  12.8 210.8 %all-gather.6.cloned.1.call-start = ((), (), s32[]{:S(2)}) async-start(), calls=%async_computation.18 | async-start | bytes 10485760 | tf_op jit(solution)/shard_map/all_gather | solution.py:333
  16.8 45.6 %copy-start.215 = (pred[512]{0:T(512)(128)(4,1)}, pred[512]{0:T(512)(128)(4,1)S(1)}, u32[]{:S(2)}) copy-start(pred[512]{0:T(512)(128)(4,1)S(1)} %broadcast_compare_fusion.1) | copy-start | bytes 1540
  23.4 174.5 %copy-start.200 = (s32[512,2]{0,1:T(2,128)}, s32[512,2]{0,1:T(2,128)S(1)}, u32[]{:S(2)}) copy-start(s32[512,2]{0,1:T(2,128)S(1)} %copy.332) | copy-start | bytes 12292
  27.8 22.7 %copy-start.218 = (pred[512]{0:T(512)(128)(4,1)}, pred[512]{0:T(512)(128)(4,1)S(1)}, u32[]{:S(2)}) copy-start(pred[512]{0:T(512)(128)(4,1)S(1)} %broadcast_compare_fusion) | copy-start | bytes 1540
  51.5 140.0 %copy-start.131 = (pred[512,2]{1,0:T(8,128)(4,1)}, pred[512,2]{1,0:T(8,128)(4,1)S(1)}, u32[]{:S(2)}) copy-start(pred[512,2]{1,0:T(8,128)(4,1)S(1)} %get-tuple-element.236) | copy-start | bytes 3076
  58.8 40.0 %copy-start.70 = (s32[512,2]{1,0:T(8,128)}, s32[512,2]{1,0:T(8,128)S(1)}, u32[]{:S(2)}) copy-start(s32[512,2]{1,0:T(8,128)S(1)} %gather_fusion.2) | copy-start | bytes 12292
  60.7 41.5 %copy-start.71 = (s32[512,2]{1,0:T(8,128)}, s32[512,2]{1,0:T(8,128)S(1)}, u32[]{:S(2)}) copy-start(s32[512,2]{1,0:T(8,128)S(1)} %gather_fusion.6) | copy-start | bytes 12292
  63.4 41.4 %copy-start.133 = (pred[512,2]{1,0:T(8,128)(4,1)}, pred[512,2]{1,0:T(8,128)(4,1)S(1)}, u32[]{:S(2)}) copy-start(pred[512,2]{1,0:T(8,128)(4,1)S(1)} %get-tuple-element.232) | copy-start | bytes 3076
  128.3 53.2 %copy-start.248 = (pred[2,256]{1,0:T(4,128)(4,1)}, pred[2,256]{1,0:T(4,128)(4,1)S(1)}, u32[]{:S(2)}) copy-start(pred[2,256]{1,0:T(4,128)(4,1)S(1)} %get-tuple-element.215) | copy-start | bytes 1540
  128.3 57.3 %copy-start.244 = (pred[2,256]{1,0:T(4,128)(4,1)}, pred[2,256]{1,0:T(4,128)(4,1)S(1)}, u32[]{:S(2)}) copy-start(pred[2,256]{1,0:T(4,128)(4,1)S(1)} %get-tuple-element.214) | copy-start | bytes 1540
  134.1 62.9 %copy-start.163 = (bf16[1,8,512]{2,0,1:T(2,128)(2,1)}, bf16[1,8,512]{2,0,1:T(2,128)(2,1)S(1)}, u32[]{:S(2)}) copy-start(bf16[1,8,512]{2,0,1:T(2,128)(2,1)S(1)} %get-tuple-element.156) | copy-start | bytes 24580
  138.7 49.7 %copy-start.75 = (bf16[1,512,512]{2,1,0:T(8,128)(2,1)}, bf16[1,512,512]{2,1,0:T(8,128)(2,1)S(1)}, u32[]{:S(2)}) copy-start(bf16[1,512,512]{2,1,0:T(8,128)(2,1)S(1)} %copy.526) | copy-start | bytes 1572868
  143.2 46.1 %copy-start.222 = (f32[1,1,512]{2,0,1:T(1,128)}, f32[1,1,512]{2,0,1:T(1,128)S(1)}, u32[]{:S(2)}) copy-start(f32[1,1,512]{2,0,1:T(1,128)S(1)} %get-tuple-element.189) | copy-start | bytes 6148
  158.1 25.4 %copy-start.106 = (bf16[2,256,1,8,64]{1,4,3,0,2:T(8,128)(2,1)}, bf16[2,256,1,8,64]{1,4,3,0,2:T(8,128)(2,1)S(1)}, u32[]{:S(2)}) copy-start(bf16[2,256,1,8,64]{1,4,3,0,2:T(8,128)(2,1)S(1)} %copy.471) | copy-start | bytes 1572868
  188.1 123.0 %copy-start.14 = (f32[512,512]{1,0:T(8,128)}, f32[512,512]{1,0:T(8,128)S(1)}, u32[]{:S(2)}) copy-start(f32[512,512]{1,0:T(8,128)S(1)} %get-tuple-element.244) | copy-start | bytes 3145732
  204.0 30.2 %all-to-all-start.4 = ((bf16[8,1,111,512]{3,2,1,0:T(8,128)(2,1)}), bf16[8,1,111,512]{3,2,1,0:T(8,128)(2,1)}, u32[]{:S(2)}, u32[]{:S(2)}) async-start(bf16[8,1,111,512]{3,2,1,0:T(8,128)(2,1)} %bitcast.101), calls=%async_computation.4 | async-start | bytes 1835008 | tf_op jit(solution)/shard_map/all_to_all | solution.py:117
  222.4 125.3 %copy-start.286 = (f32[1,1,512]{2,0,1:T(1,128)}, f32[1,1,512]{2,0,1:T(1,128)S(1)}, u32[]{:S(2)}) copy-start(f32[1,1,512]{2,0,1:T(1,128)S(1)} %get-tuple-element.187) | copy-start | bytes 6148
  222.4 125.3 %copy-start.329 = (f32[1,1,512]{2,0,1:T(1,128)}, f32[1,1,512]{2,0,1:T(1,128)S(1)}, u32[]{:S(2)}) copy-start(f32[1,1,512]{2,0,1:T(1,128)S(1)} %get-tuple-element.186) | copy-start | bytes 6148
  234.2 28.1 %all-to-all-start = ((bf16[8,1,111,512]{3,2,1,0:T(8,128)(2,1)}), bf16[8,1,111,512]{3,2,1,0:T(8,128)(2,1)S(1)}, u32[]{:S(2)}, u32[]{:S(2)}) async-start(bf16[8,1,111,512]{3,2,1,0:T(8,128)(2,1)} %bitcast.23), calls=%async_computation | async-start | bytes 1835008 | tf_op jit(solution)/shard_map/all_to_all | solution.py:117
  262.3 30.3 %all-to-all-start.5 = ((bf16[8,1,111,512]{3,2,1,0:T(8,128)(2,1)}), bf16[8,1,111,512]{3,2,1,0:T(8,128)(2,1)S(1)}, u32[]{:S(2)}, u32[]{:S(2)}) async-start(bf16[8,1,111,512]{3,2,1,0:T(8,128)(2,1)} %fusion.378), calls=%async_computation.5 | async-start | bytes 1835008 | tf_op jit(solution)/shard_map/all_to_all | solution.py:127
  275.4 23.7 %copy-start = (s32[1024]{0:T(1024)S(1)}, s32[1024]{0:T(1024)}, u32[]{:S(2)}) copy-start(s32[1024]{0:T(1024)} %broadcast_clamp_fusion.1) | copy-start | bytes 12292
  292.7 39.8 %all-to-all-start.1 = ((bf16[8,1,111,512]{3,2,1,0:T(8,128)(2,1)}), bf16[8,1,111,512]{3,2,1,0:T(8,128)(2,1)}, u32[]{:S(2)}, u32[]{:S(2)}) async-start(bf16[8,1,111,512]{3,2,1,0:T(8,128)(2,1)} %fusion.376), calls=%async_computation.1 | async-start | bytes 1835008 | tf_op jit(solution)/shard_map/all_to_all | solution.py:127
  332.1 40.3 %copy-start.12 = (f32[512,512]{1,0:T(8,128)}, f32[512,512]{1,0:T(8,128)S(1)}, u32[]{:S(2)}) copy-start(f32[512,512]{1,0:T(8,128)S(1)} %get-tuple-element.256) | copy-start | bytes 3145732
  332.2 40.3 %copy-start.181 = (f32[512]{0:T(512)}, f32[512]{0:T(512)S(1)}, u32[]{:S(2)}) copy-start(f32[512]{0:T(512)S(1)} %broadcast_multiply_fusion.4) | copy-start | bytes 6148
  332.4 40.0 %copy-start.213 = (f32[512]{0:T(512)}, f32[512]{0:T(512)S(1)}, u32[]{:S(2)}) copy-start(f32[512]{0:T(512)S(1)} %fusion.540) | copy-start | bytes 6148
  347.4 24.2 %copy-start.33 = (f32[512,512]{1,0:T(8,128)}, f32[512,512]{1,0:T(8,128)S(1)}, u32[]{:S(2)}) copy-start(f32[512,512]{1,0:T(8,128)S(1)} %get-tuple-element.149) | copy-start | bytes 3145732
  386.3 27.8 %all-to-all-start.6 = ((bf16[8,1,111,512]{3,2,1,0:T(8,128)(2,1)}), bf16[8,1,111,512]{3,2,1,0:T(8,128)(2,1)}, u32[]{:S(2)}, u32[]{:S(2)}) async-start(bf16[8,1,111,512]{3,2,1,0:T(8,128)(2,1)} %bitcast.1343), calls=%async_computation.6 | async-start | bytes 1835008 | tf_op jit(solution)/shard_map/all_to_all | solution.py:117
  414.1 28.2 %all-to-all-start.2 = ((bf16[8,1,111,512]{3,2,1,0:T(8,128)(2,1)}), bf16[8,1,111,512]{3,2,1,0:T(8,128)(2,1)S(1)}, u32[]{:S(2)}, u32[]{:S(2)}) async-start(bf16[8,1,111,512]{3,2,1,0:T(8,128)(2,1)} %bitcast.65), calls=%async_computation.2 | async-start | bytes 1835008 | tf_op jit(solution)/shard_map/all_to_all | solution.py:117
  442.3 30.0 %all-to-all-start.12 = ((bf16[8,1,111,512]{3,2,1,0:T(8,128)(2,1)}), bf16[8,1,111,512]{3,2,1,0:T(8,128)(2,1)S(1)}, u32[]{:S(2)}, u32[]{:S(2)}) async-start(bf16[8,1,111,512]{3,2,1,0:T(8,128)(2,1)} %fusion.404), calls=%async_computation.12 | async-start | bytes 1835008 | tf_op jit(solution)/shard_map/all_to_all | solution.py:203
  472.3 53.2 %all-to-all-start.7 = ((bf16[8,1,111,512]{3,2,1,0:T(8,128)(2,1)}), bf16[8,1,111,512]{3,2,1,0:T(8,128)(2,1)S(1)}, u32[]{:S(2)}, u32[]{:S(2)}) async-start(bf16[8,1,111,512]{3,2,1,0:T(8,128)(2,1)} %fusion.379), calls=%async_computation.7 | async-start | bytes 1835008 | tf_op jit(solution)/shard_map/all_to_all | solution.py:127
  499.4 23.0 %copy-start.337 = (bf16[8,1,111,2048]{3,2,0,1:T(8,128)(2,1)}, bf16[8,1,111,2048]{3,2,0,1:T(8,128)(2,1)S(1)}, u32[]{:S(2)}) copy-start(bf16[8,1,111,2048]{3,2,0,1:T(8,128)(2,1)S(1)} %get-tuple-element.270) | copy-start | bytes 10911748
  499.4 23.0 %copy-start.96 = (bf16[1,1024,2048]{2,1,0:T(8,128)(2,1)S(1)}, bf16[1,1024,2048]{2,1,0:T(8,128)(2,1)}, u32[]{:S(2)}) copy-start(bf16[1,1024,2048]{2,1,0:T(8,128)(2,1)} %get-tuple-element.152) | copy-start | bytes 12582916
  525.5 27.8 %all-to-all-start.13 = ((bf16[8,1,111,512]{3,2,1,0:T(8,128)(2,1)}), bf16[8,1,111,512]{3,2,1,0:T(8,128)(2,1)}, u32[]{:S(2)}, u32[]{:S(2)}) async-start(bf16[8,1,111,512]{3,2,1,0:T(8,128)(2,1)} %fusion.367), calls=%async_computation.13 | async-start | bytes 1835008 | tf_op jit(solution)/shard_map/all_to_all | solution.py:213
  553.3 59.8 %all-to-all-start.3 = ((bf16[8,1,111,512]{3,2,1,0:T(8,128)(2,1)}), bf16[8,1,111,512]{3,2,1,0:T(8,128)(2,1)}, u32[]{:S(2)}, u32[]{:S(2)}) async-start(bf16[8,1,111,512]{3,2,1,0:T(8,128)(2,1)} %fusion.377), calls=%async_computation.3 | async-start | bytes 1835008 | tf_op jit(solution)/shard_map/all_to_all | solution.py:127
  613.1 48.3 %all-to-all-start.8 = ((bf16[8,1,111,512]{3,2,1,0:T(8,128)(2,1)}), bf16[8,1,111,512]{3,2,1,0:T(8,128)(2,1)}, u32[]{:S(2)}, u32[]{:S(2)}) async-start(bf16[8,1,111,512]{3,2,1,0:T(8,128)(2,1)} %fusion.402), calls=%async_computation.8 | async-start | bytes 1835008 | tf_op jit(solution)/shard_map/all_to_all | solution.py:203
  661.4 23.3 %copy-start.97 = (bf16[1,1024,2048]{2,1,0:T(8,128)(2,1)S(1)}, bf16[1,1024,2048]{2,1,0:T(8,128)(2,1)}, u32[]{:S(2)}) copy-start(bf16[1,1024,2048]{2,1,0:T(8,128)(2,1)} %get-tuple-element.152) | copy-start | bytes 12582916
  687.7 29.3 %all-to-all-start.9 = ((bf16[8,1,111,512]{3,2,1,0:T(8,128)(2,1)}), bf16[8,1,111,512]{3,2,1,0:T(8,128)(2,1)S(1)}, u32[]{:S(2)}, u32[]{:S(2)}) async-start(bf16[8,1,111,512]{3,2,1,0:T(8,128)(2,1)} %fusion.373), calls=%async_computation.9 | async-start | bytes 1835008 | tf_op jit(solution)/shard_map/all_to_all | solution.py:213
  693.9 22.4 %copy-start.313 = (f32[512]{0:T(512)S(1)}, f32[512]{0:T(512)}, u32[]{:S(2)}) copy-start(f32[512]{0:T(512)} %convert_reduce_fusion.8) | copy-start | bytes 6148
  693.9 22.4 %copy-start.319 = (f32[2048]{0:T(1024)S(1)}, f32[2048]{0:T(1024)}, u32[]{:S(2)}) copy-start(f32[2048]{0:T(1024)} %get-tuple-element.269) | copy-start | bytes 24580
  792.3 22.4 %copy-start.63 = (bf16[512,512]{1,0:T(8,128)(2,1)S(1)}, bf16[512,512]{1,0:T(8,128)(2,1)}, u32[]{:S(2)}) copy-start(bf16[512,512]{1,0:T(8,128)(2,1)} %copy-done.62) | copy-start | bytes 1572868
  792.3 23.2 %copy-start.61 = (bf16[512,512]{1,0:T(8,128)(2,1)S(1)}, bf16[512,512]{1,0:T(8,128)(2,1)}, u32[]{:S(2)}) copy-start(bf16[512,512]{1,0:T(8,128)(2,1)} %copy-done.60) | copy-start | bytes 1572868
  793.5 22.9 %copy-start.69 = (f32[8,1,111,512]{3,2,0,1:T(8,128)S(1)}, f32[8,1,111,512]{3,2,0,1:T(8,128)}, u32[]{:S(2)}) copy-start(f32[8,1,111,512]{3,2,0,1:T(8,128)} %gather.139) | copy-start | bytes 5455876
  793.5 22.9 %copy-start.296 = (f32[8,111]{1,0:T(8,128)S(1)}, f32[8,111]{1,0:T(8,128)}, u32[]{:S(2)}) copy-start(f32[8,111]{1,0:T(8,128)} %mul.1532) | copy-start | bytes 10660
  793.5 25.9 %all-to-all-start.10 = ((bf16[8,1,111,512]{3,2,1,0:T(8,128)(2,1)}), bf16[8,1,111,512]{3,2,1,0:T(8,128)(2,1)}, u32[]{:S(2)}, u32[]{:S(2)}) async-start(bf16[8,1,111,512]{3,2,1,0:T(8,128)(2,1)} %fusion.403), calls=%async_computation.10 | async-start | bytes 1835008 | tf_op jit(solution)/shard_map/all_to_all | solution.py:203
  819.4 30.4 %all-to-all-start.14 = ((bf16[8,1,111,512]{3,2,1,0:T(8,128)(2,1)}), bf16[8,1,111,512]{3,2,1,0:T(8,128)(2,1)S(1)}, u32[]{:S(2)}, u32[]{:S(2)}) async-start(bf16[8,1,111,512]{3,2,1,0:T(8,128)(2,1)} %fusion.405), calls=%async_computation.14 | async-start | bytes 1835008 | tf_op jit(solution)/shard_map/all_to_all | solution.py:203
  823.5 23.3 %copy-start.92 = (bf16[1,1024,2048]{2,1,0:T(8,128)(2,1)S(1)}, bf16[1,1024,2048]{2,1,0:T(8,128)(2,1)}, u32[]{:S(2)}) copy-start(bf16[1,1024,2048]{2,1,0:T(8,128)(2,1)} %get-tuple-element.153) | copy-start | bytes 12582916
  849.7 26.9 %copy-start.98 = (bf16[8,1,111,512]{3,2,1,0:T(8,128)(2,1)}, bf16[8,1,111,512]{3,2,1,0:T(8,128)(2,1)S(1)}, u32[]{:S(2)}) copy-start(bf16[8,1,111,512]{3,2,1,0:T(8,128)(2,1)S(1)} %all-to-all-done.14) | copy-start | bytes 2727940
  849.7 31.6 %all-to-all-start.11 = ((bf16[8,1,111,512]{3,2,1,0:T(8,128)(2,1)}), bf16[8,1,111,512]{3,2,1,0:T(8,128)(2,1)S(1)}, u32[]{:S(2)}, u32[]{:S(2)}) async-start(bf16[8,1,111,512]{3,2,1,0:T(8,128)(2,1)} %fusion.370), calls=%async_computation.11 | async-start | bytes 1835008 | tf_op jit(solution)/shard_map/all_to_all | solution.py:213
  855.9 22.4 %copy-start.93 = (bf16[1,1024,2048]{2,1,0:T(8,128)(2,1)S(1)}, bf16[1,1024,2048]{2,1,0:T(8,128)(2,1)}, u32[]{:S(2)}) copy-start(bf16[1,1024,2048]{2,1,0:T(8,128)(2,1)} %get-tuple-element.153) | copy-start | bytes 12582916
  881.4 26.4 %all-to-all-start.15 = ((bf16[8,1,111,512]{3,2,1,0:T(8,128)(2,1)}), bf16[8,1,111,512]{3,2,1,0:T(8,128)(2,1)}, u32[]{:S(2)}, u32[]{:S(2)}) async-start(bf16[8,1,111,512]{3,2,1,0:T(8,128)(2,1)} %fusion.364), calls=%async_computation.15 | async-start | bytes 1835008 | tf_op jit(solution)/shard_map/all_to_all | solution.py:213
  887.4 249.1 %all-reduce.22.cloned.1.call-start = ((), (), s32[]{:S(2)}) async-start(), calls=%async_computation.24 | async-start | bytes 8454144
  958.7 42.4 %copy-start.52 = (f32[512,512]{1,0:T(8,128)}, f32[512,512]{1,0:T(8,128)S(1)}, u32[]{:S(2)}) copy-start(f32[512,512]{1,0:T(8,128)S(1)} %fusion.644) | copy-start | bytes 3145732
  1001.0 26.6 %copy-start.87 = (f32[512,512]{1,0:T(8,128)}, f32[512,512]{1,0:T(8,128)S(1)}, u32[]{:S(2)}) copy-start(f32[512,512]{1,0:T(8,128)S(1)} %get-tuple-element.266) | copy-start | bytes 3145732
  1051.6 110.5 %reduce-scatter.7.cloned.1.call-start = ((), (), s32[]{:S(2)}) async-start(), calls=%async_computation.23 | async-start | bytes 819200
  1078.4 165.9 %all-reduce.20.cloned.1.call-start = ((), (), s32[]{:S(2)}) async-start(), calls=%async_computation.22 | async-start | bytes 2113536 | tf_op jit(solution)/shard_map/psum | solution.py:396
  1139.5 178.4 %reduce-scatter.5.cloned.1.call-start = ((), (), s32[]{:S(2)}) async-start(), calls=%async_computation.19 | async-start | bytes 10485760 | tf_op jit(solution)/shard_map/reduce_scatter | solution.py:401
  1164.6 202.8 %copy-start.253 = (f32[2,1,640]{2,1,0:T(1,128)}, f32[2,1,640]{2,1,0:T(1,128)S(1)}, u32[]{:S(2)}) copy-start(f32[2,1,640]{2,1,0:T(1,128)S(1)} %get-tuple-element.107) | copy-start | bytes 15364
  1168.3 156.2 %copy-start.89 = (f32[512,512]{1,0:T(8,128)S(1)}, f32[512,512]{1,0:T(8,128)}, u32[]{:S(2)}) copy-start(f32[512,512]{1,0:T(8,128)} %get-tuple-element.172) | copy-start | bytes 3145732
  1168.3 199.1 %copy-start.252 = (f32[2,1,640]{2,1,0:T(1,128)S(1)}, f32[2,1,640]{2,1,0:T(1,128)}, u32[]{:S(2)}) copy-start(f32[2,1,640]{2,1,0:T(1,128)} %param.27) | copy-start | bytes 15364
  1168.3 199.1 %copy-start.324 = (f32[2,1,640]{2,1,0:T(1,128)S(1)}, f32[2,1,640]{2,1,0:T(1,128)}, u32[]{:S(2)}) copy-start(f32[2,1,640]{2,1,0:T(1,128)} %param.29) | copy-start | bytes 15364
  1168.3 199.1 %copy-start.325 = (f32[2,1,640]{2,1,0:T(1,128)S(1)}, f32[2,1,640]{2,1,0:T(1,128)}, u32[]{:S(2)}) copy-start(f32[2,1,640]{2,1,0:T(1,128)} %param.28) | copy-start | bytes 15364
  1168.3 199.7 %copy-start.59 = (f32[2,516,512]{2,0,1:T(2,128)S(1)}, f32[2,516,512]{2,0,1:T(2,128)}, u32[]{:S(2)}) copy-start(f32[2,516,512]{2,0,1:T(2,128)} %param.21) | copy-start | bytes 6340612
  (306 other events, 2500.3 us)
Sparse Core Ops, SparseCore 0:
  12.2 37.3 all-gather.7
  51.7 34.7 all-gather.9
  88.7 58.2 all-gather.5
  1051.7 84.7 all-reduce.21
  1139.4 22.5 reduce-scatter.6
  1166.0 78.3 all-reduce.19
  1246.9 70.9 reduce-scatter.4
where the time goes:
time: 1400 us; the launch traced here: 1390 us
  matrix products  451 us (32%)
  local copies, waits for them, and re-layouts  416 us (30%)
  other arithmetic  188 us (13%)
  waiting for transfers between devices  177 us (13%)
  starting transfers between devices  91.1 us (7%)
  blocking collectives  45.7 us (3%)
  between operations  25.1 us (2%)
    dot_general x4, matrix products, backward_layer(): jnp.einsum('sjcd,sjcf->jdf', grad_recv, active, preferred_element_type=jn...  85.5 us
    dot_general x4, matrix products, backward_layer(): jnp.einsum('sjcd,jdf->sjcf', grad_recv, weight_out, preferred_element_typ...  84.7 us
    unnamed x723, local copies, waits for them, and re-layouts  77.6 us
    psum x1, waiting for transfers between devices, local(): dense_total = lax.psum(dense_grad.astype(jnp.bfloat16), 'expert')  76 us
    dot_general x4, matrix products, forward_layer(): jnp.einsum('sjcf,jdf->sjcd', active, weight_out, preferred_element_type=j...  69.1 us
    reduce_scatter x1, waiting for transfers between devices, local(): lax.psum_scatter(mats_grad.astype(jnp.bfloat16), 'dp', scatter_dimension=...  67.6 us
    concatenate x8, local copies, waits for them, and re-layouts, backward_layer(): jnp.concatenate([qkv_grad, out_grad, router_grad, vector_grad], axis=0)  49 us
    psum x1, blocking collectives, local(): lax.psum((dense_square, expert_square), ('dp', 'expert'))  39.5 us
  transfers between devices with their start and end apart: 23, of which 9 were waited for; matrix products, arithmetic and copies ran while one was open for 50% of the time, Pallas kernels for 0%

commit v1 on v0

v1 whole, which is shorter than its diff:
```python
import functools

import jax
import jax.numpy as jnp
from jax import lax
from jax.experimental import pallas as pl
from jax.experimental.pallas import tpu as pltpu
from jax.sharding import PartitionSpec as P

HEADS = 8
PATCHES = 197


NORM_EPS = 1e-06
NEG_FILL = -1e30
CLIP_NORM = 1.0
BETA_ONE = 0.9
BETA_TWO = 0.95
STEP_RATE = 0.01
DECAY_RATE = 0.1
ADAM_EPS = 1e-08
LANES = 128
MESH = pl.DeviceIdType.MESH
VMEM_LIMIT = 60 * 1024 * 1024
F32 = jnp.float32
BF16 = jnp.bfloat16
INV_SQRT2 = 0.7071067811865476
INV_SQRT2PI = 0.3989422804014327


def up_to(count, step):
    return -(-count // step) * step


def dot_nn(left, right):
    return lax.dot_general(left, right, (((1,), (0,)), ((), ())), preferred_element_type=F32)


def dot_nt(left, right):
    return lax.dot_general(left, right, (((1,), (1,)), ((), ())), preferred_element_type=F32)


def dot_tn(left, right):
    return lax.dot_general(left, right, (((0,), (0,)), ((), ())), preferred_element_type=F32)


def lane_ids(rows, cols=LANES):
    return lax.broadcasted_iota(jnp.int32, (rows, cols), 1)


def one_where(mask):
    return jnp.where(mask, 1.0, 0.0).astype(BF16)


def normalise(values):
    centred = values - jnp.mean(values, axis=-1, keepdims=True)
    spread = jnp.mean(centred * centred, axis=-1, keepdims=True)
    scale = lax.rsqrt(spread + NORM_EPS)
    return centred * scale, scale


def norm_back(grad_hat, hat, scale):
    return scale * (
        grad_hat
        - jnp.mean(grad_hat, axis=-1, keepdims=True)
        - hat * jnp.mean(grad_hat * hat, axis=-1, keepdims=True)
    )


def dense_parts(dense_ref, experts):
    width = dense_ref.shape[-1]
    tail = dense_ref[4 * width :, :].astype(F32)
    vectors = tail[experts : experts + 8]
    router_rows = jnp.concatenate(
        [tail[:experts], jnp.zeros((LANES - experts, width), F32)], axis=0
    ).astype(BF16)
    return router_rows, vectors


def routing_kernel(capacity, slots_each, experts, layers, meta_ref, cols_ref, slot_col_ref, slot_row_ref):
    toks = meta_ref.shape[-1]
    meta = meta_ref[...]
    cols = cols_ref[...]
    rank_row, rank_col = meta[0:1], cols[:, 0:1]
    ok_row, ok_col = meta[1:2], cols[:, 1:2]
    before = one_where(rank_row < rank_col)
    before_t = one_where(rank_col < rank_row)
    lanes = lane_ids(toks)
    subs = lax.broadcasted_iota(jnp.int32, (LANES, toks), 0)
    col_out = [None] * 16
    row_out = [None] * 8
    for layer in range(layers):
        counts, ones, counts_t, ones_t, totals, totals_t = [], [], [], [], [], []
        for k in range(2):
            named = cols[:, 2 + 2 * layer + k : 3 + 2 * layer + k]
            hot = jnp.where((lanes == named) & (ok_col > 0), 1.0, 0.0)
            ones.append(hot)
            counts.append(dot_nn(before, hot.astype(BF16)))
            totals.append(jnp.sum(hot, axis=0, keepdims=True))
            named_t = meta[2 + 2 * layer + k : 3 + 2 * layer + k]
            hot_t = jnp.where((subs == named_t) & (ok_row > 0), 1.0, 0.0)
            ones_t.append(hot_t)
            counts_t.append(dot_nn(hot_t.astype(BF16), before_t))
            totals_t.append(jnp.sum(hot_t, axis=1, keepdims=True))
        for k in range(2):
            extra = totals[0] if k else 0.0
            place = jnp.sum((counts[k] + extra) * ones[k], axis=1, keepdims=True).astype(jnp.int32)
            named = cols[:, 2 + 2 * layer + k : 3 + 2 * layer + k]
            held = (place < capacity) & (ok_col > 0)
            col_out[2 * layer + k] = jnp.where(held, named * slots_each + place, -1)
            col_out[4 + 2 * layer + k] = named
            extra_t = totals_t[0] if k else 0.0
            place_t = jnp.sum((counts_t[k] + extra_t) * ones_t[k], axis=0, keepdims=True).astype(jnp.int32)
            named_t = meta[2 + 2 * layer + k : 3 + 2 * layer + k]
            held_t = (place_t < capacity) & (ok_row > 0)
            row_out[2 * layer + k] = jnp.where(held_t, named_t * slots_each + place_t, -1)
    col_out[8] = ok_col
    full = jnp.zeros((toks, LANES), jnp.int32)
    for at, value in enumerate(col_out):
        if value is not None:
            full = jnp.where(lanes == at, value, full)
    slot_col_ref[...] = full
    eight = lax.broadcasted_iota(jnp.int32, (8, toks), 0)
    rows = jnp.zeros((8, toks), jnp.int32)
    for at, value in enumerate(row_out):
        if value is not None:
            rows = jnp.where(eight == at, value, rows)
    slot_row_ref[...] = rows


def routing(meta, cols, capacity, slots_each, experts, layers):
    micros, _, toks = meta.shape
    return pl.pallas_call(
        functools.partial(routing_kernel, capacity, slots_each, experts, layers),
        grid=(micros,),
        in_specs=[
            pl.BlockSpec((None, 8, toks), lambda m: (m, 0, 0)),
            pl.BlockSpec((None, toks, 8), lambda m: (m, 0, 0)),
        ],
        out_specs=[
            pl.BlockSpec((None, toks, LANES), lambda m: (m, 0, 0)),
            pl.BlockSpec((None, 8, toks), lambda m: (m, 0, 0)),
        ],
        out_shape=[
            jax.ShapeDtypeStruct((micros, toks, LANES), jnp.int32),
            jax.ShapeDtypeStruct((micros, 8, toks), jnp.int32),
        ],
        compiler_params=pltpu.CompilerParams(vmem_limit_bytes=VMEM_LIMIT),
        name="routing",
    )(meta, cols)


def gates(router, slot_col, layer):
    lanes = lane_ids(router.shape[0])
    out = []
    for k in range(2):
        named = slot_col[:, 4 + 2 * layer + k : 5 + 2 * layer + k]
        value = jnp.sum(jnp.where(lanes == named, router, 0.0), axis=1, keepdims=True)
        held = slot_col[:, 2 * layer + k : 2 * layer + k + 1] >= 0
        out.append(jnp.where(held, value, 0.0))
    return out


def pick_mask(slot_col, layer, k, slots):
    toks = slot_col.shape[0]
    return lax.broadcasted_iota(jnp.int32, (toks, slots), 1) == slot_col[:, 2 * layer + k : 2 * layer + k + 1]


def place_mask(slot_row, layer, k, slots):
    toks = slot_row.shape[1]
    return lax.broadcasted_iota(jnp.int32, (slots, toks), 0) == slot_row[2 * layer + k : 2 * layer + k + 1]


def half_mask(rows, half):
    lanes = lane_ids(rows)
    return (lanes >= LANES // 2) if half else (lanes < LANES // 2)


def attention_forward(x, layer, images, experts, dense_ref, slot_col, slot_row, qkv_ref, a_ref, o_ref, x1_ref, c_ref, router_ref, send_ref):
    toks, width = x.shape
    rows = toks // images
    router_rows, vec = dense_parts(dense_ref, experts)
    hat, _ = normalise(x)
    a = (hat * vec[0:1] + vec[1:2]).astype(BF16)
    a_ref[...] = a
    for part in range(3):
        at = slice(part * width, (part + 1) * width)
        qkv_ref[:, at] = (dot_nt(a, dense_ref[at, :]) + vec[2 + part : 3 + part]).astype(BF16)
    key_dead = lane_ids(rows, rows) >= PATCHES
    scale = (width // HEADS) ** (-0.5)
    for image in range(images):
        at = slice(image * rows, (image + 1) * rows)
        for pair in range(width // LANES):
            q2 = qkv_ref[at, pair * LANES : (pair + 1) * LANES]
            k2 = qkv_ref[at, width + pair * LANES : width + (pair + 1) * LANES]
            v2 = qkv_ref[at, 2 * width + pair * LANES : 2 * width + (pair + 1) * LANES]
            both = []
            for half in range(2):
                q_half = jnp.where(half_mask(rows, half), q2, jnp.zeros_like(q2))
                s = jnp.where(key_dead, NEG_FILL, dot_nt(q_half, k2) * scale)
                e = jnp.exp(s - jnp.max(s, axis=1, keepdims=True))
                p = e * (1.0 / jnp.sum(e, axis=1, keepdims=True))
                both.append(dot_nn(p.astype(BF16), v2))
            o2 = jnp.where(half_mask(rows, 0), both[0], both[1])
            o_ref[at, pair * LANES : (pair + 1) * LANES] = o2.astype(BF16)
    x1 = x + (dot_nn(o_ref[...], dense_ref[3 * width : 4 * width, :]) + vec[5:6])
    x1_ref[...] = x1
    hat, _ = normalise(x1)
    c = (hat * vec[6:7] + vec[7:8]).astype(BF16)
    c_ref[...] = c
    logits = jnp.where(lane_ids(toks) < experts, dot_nt(c, router_rows), NEG_FILL)
    e = jnp.exp(logits - jnp.max(logits, axis=1, keepdims=True))
    router_ref[...] = e / jnp.sum(e, axis=1, keepdims=True)
    slots = send_ref.shape[0] * send_ref.shape[1]
    place = one_where(place_mask(slot_row, layer, 0, slots) | place_mask(slot_row, layer, 1, slots))
    send_ref[...] = dot_nn(place, c).astype(BF16).reshape(send_ref.shape)


def combine(x1, router, slot_col, layer, back, picked_ref):
    slots = back.shape[0] * back.shape[1]
    y = back.reshape(slots, back.shape[2])
    g = gates(router, slot_col, layer)
    total = x1
    for k in range(2):
        picked = dot_nn(one_where(pick_mask(slot_col, layer, k, slots)), y)
        picked_ref[k] = picked.astype(BF16)
        total = total + g[k] * picked
    return total


def combine_back(dx2, router, slot_col, slot_row, layer, picked_ref, dg_ref, send_ref):
    slots = send_ref.shape[0] * send_ref.shape[1]
    toks = dx2.shape[0]
    g = gates(router, slot_col, layer)
    lanes = lane_ids(toks)
    out = jnp.zeros((toks, LANES), F32)
    total = None
    for k in range(2):
        held = slot_col[:, 2 * layer + k : 2 * layer + k + 1] >= 0
        dg = jnp.sum(dx2 * picked_ref[k].astype(F32), axis=1, keepdims=True)
        named = slot_col[:, 4 + 2 * layer + k : 5 + 2 * layer + k]
        out = out + jnp.where((lanes == named) & held, dg, 0.0)
        part = dot_nn(one_where(place_mask(slot_row, layer, k, slots)), (g[k] * dx2).astype(BF16))
        total = part if total is None else total + part
    dg_ref[...] = out
    send_ref[...] = total.astype(BF16).reshape(send_ref.shape)


def attention_back(layer, images, experts, dense_ref, slot_col, back_ref, dx2, dr, router, x, x1, c, o_ref, qkv_ref, a_ref, acc_ref, dqkv_ref, do_ref):
    toks, width = x.shape
    rows = toks // images
    slots = back_ref.shape[0] * back_ref.shape[1]
    router_rows, vec = dense_parts(dense_ref, experts)
    dlog = (router * (dr - jnp.sum(dr * router, axis=1, keepdims=True))).astype(BF16)
    pick = one_where(pick_mask(slot_col, layer, 0, slots) | pick_mask(slot_col, layer, 1, slots))
    dc = dot_nn(pick, back_ref[...].reshape(slots, width)) + dot_nn(dlog, router_rows)
    acc_ref[4 * width : 4 * width + experts, :] += dot_tn(dlog, c)[:experts]
    hat, scale2 = normalise(x1)
    dgain2 = jnp.sum(dc * hat, axis=0, keepdims=True)
    dshift2 = jnp.sum(dc, axis=0, keepdims=True)
    dx1 = dx2 + norm_back(dc * vec[6:7], hat, scale2)
    dz = dx1.astype(BF16)
    dbo = jnp.sum(dz.astype(F32), axis=0, keepdims=True)
    acc_ref[3 * width : 4 * width, :] += dot_tn(o_ref[...], dz)
    do_ref[...] = dot_nt(dz, dense_ref[3 * width : 4 * width, :]).astype(BF16)
    key_dead = lax.broadcasted_iota(jnp.int32, (rows, rows), 0) >= PATCHES
    scale = (width // HEADS) ** (-0.5)
    first = half_mask(rows, 0)
    for image in range(images):
        at = slice(image * rows, (image + 1) * rows)
        for pair in range(width // LANES):
            cut = slice(pair * LANES, (pair + 1) * LANES)
            q2 = qkv_ref[at, cut]
            k2 = qkv_ref[at, width + pair * LANES : width + (pair + 1) * LANES]
            v2 = qkv_ref[at, 2 * width + pair * LANES : 2 * width + (pair + 1) * LANES]
            do2 = do_ref[at, cut]
            dqs, dks, dvs = [], [], []
            for half in range(2):
                keep = half_mask(rows, half)
                q_half = jnp.where(keep, q2, jnp.zeros_like(q2))
                do_half = jnp.where(keep, do2, jnp.zeros_like(do2))
                s = jnp.where(key_dead, NEG_FILL, dot_nt(k2, q_half) * scale)
                e = jnp.exp(s - jnp.max(s, axis=0, keepdims=True))
                p = e * (1.0 / jnp.sum(e, axis=0, keepdims=True))
                dp = dot_nt(v2, do_half)
                ds = (p * (dp - jnp.sum(dp * p, axis=0, keepdims=True))).astype(BF16)
                dvs.append(dot_nn(p.astype(BF16), do2))
                dks.append(dot_nn(ds, q2))
                dqs.append(dot_tn(ds, k2))
            dqkv_ref[at, cut] = (jnp.where(first, dqs[0], dqs[1]) * scale).astype(BF16)
            dqkv_ref[at, width + pair * LANES : width + (pair + 1) * LANES] = (
                jnp.where(first, dks[0], dks[1]) * scale
            ).astype(BF16)
            dqkv_ref[at, 2 * width + pair * LANES : 2 * width + (pair + 1) * LANES] = jnp.where(
                first, dvs[0], dvs[1]
            ).astype(BF16)
    a = a_ref[...]
    da = None
    biases = []
    for part in range(3):
        at = slice(part * width, (part + 1) * width)
        dq = dqkv_ref[:, at]
        acc_ref[at, :] += dot_tn(dq, a)
        biases.append(jnp.sum(dq.astype(F32), axis=0, keepdims=True))
        piece = dot_nn(dq, dense_ref[at, :])
        da = piece if da is None else da + piece
    hat, scale1 = normalise(x)
    dgain1 = jnp.sum(da * hat, axis=0, keepdims=True)
    dshift1 = jnp.sum(da, axis=0, keepdims=True)
    acc_ref[4 * width + experts : 4 * width + experts + 8, :] += jnp.concatenate(
        [dgain1, dshift1, *biases, dbo, dgain2, dshift2], axis=0
    )
    return dx1 + norm_back(da * vec[0:1], hat, scale1)


def pack_rows(block, images, rows):
    each = block.shape[0] // images
    return jnp.concatenate([block[i * each : i * each + rows] for i in range(images)], axis=0)


def unpack_rows(packed, images, each):
    rows = packed.shape[0] // images
    fill = jnp.zeros((each - rows, packed.shape[1]), packed.dtype)
    parts = []
    for i in range(images):
        parts += [packed[i * rows : (i + 1) * rows], fill]
    return jnp.concatenate(parts, axis=0)


def first_kernel(sizes, tok_ref, dense_ref, col_ref, row_ref, *outs):
    images, rows, experts = sizes
    x_ref, qkv_ref, a_ref, o_ref, x1_ref, c_ref, router_ref, send_ref = outs
    x = pack_rows(tok_ref[...].astype(F32), images, rows)
    x_ref[...] = x
    attention_forward(x, 0, images, experts, dense_ref, col_ref[...], row_ref[...], qkv_ref, a_ref, o_ref, x1_ref, c_ref, router_ref, send_ref)


def middle_kernel(sizes, layer, back_ref, x1_old, router_old, dense_ref, col_ref, row_ref, picked_ref, *outs):
    images, rows, experts = sizes
    x_ref, qkv_ref, a_ref, o_ref, x1_ref, c_ref, router_ref, send_ref = outs
    x = combine(x1_old[...], router_old[...], col_ref[...], layer - 1, back_ref[...], picked_ref)
    x_ref[...] = x
    attention_forward(x, layer, images, experts, dense_ref, col_ref[...], row_ref[...], qkv_ref, a_ref, o_ref, x1_ref, c_ref, router_ref, send_ref)


def turn_kernel(sizes, layer, back_ref, x1_old, router_old, cot_ref, col_ref, row_ref, out_ref, dx_ref, dg_ref, send_ref, picked_ref):
    images, rows, experts = sizes
    each = out_ref.shape[0] // images
    col = col_ref[...]
    x = combine(x1_old[...], router_old[...], col, layer, back_ref[...], picked_ref)
    ok = col[:, 8:9] > 0
    out_ref[...] = unpack_rows(jnp.where(ok, x, 0.0), images, each)
    dx = jnp.where(ok, pack_rows(cot_ref[...].astype(F32), images, rows), 0.0)
    dx_ref[...] = dx
    combine_back(dx, router_old[...], col, row_ref[...], layer, picked_ref, dg_ref, send_ref)


def flush_dense(acc_ref, dense_out):
    @pl.when(pl.program_id(0) == pl.num_programs(0) - 1)
    def _():
        rows = dense_out.shape[1]
        shard = acc_ref.shape[0] // dense_out.shape[0]
        for at in range(dense_out.shape[0]):
            dense_out[at, :shard, :] = acc_ref[at * shard : (at + 1) * shard, :].astype(BF16)
            if rows > shard:
                dense_out[at, shard:, :] = jnp.zeros((rows - shard, acc_ref.shape[1]), BF16)


def back_common(sizes, layer, refs):
    images, rows, experts = sizes
    (back_ref, dx_ref, dg_ref, router_ref, x_ref, x1_ref, c_ref, o_ref, qkv_ref, a_ref, dense_ref, col_ref, acc_ref, dqkv_ref, do_ref) = refs

    @pl.when(pl.program_id(0) == 0)
    def _():
        acc_ref[...] = jnp.zeros_like(acc_ref)

    return attention_back(layer, images, experts, dense_ref, col_ref[...], back_ref, dx_ref[...], dg_ref[...], router_ref[...], x_ref[...], x1_ref[...], c_ref[...], o_ref, qkv_ref, a_ref, acc_ref, dqkv_ref, do_ref)


def back_kernel(sizes, layer, *refs):
    (back_ref, dx_ref, dg_ref, router_ref, x_ref, x1_ref, c_ref, o_ref, qkv_ref, a_ref, dense_ref, col_ref, row_ref, router_low, picked_low, dx_out, dg_out, send_ref, dense_out, acc_ref, dqkv_ref, do_ref) = refs
    dx = back_common(sizes, layer, (back_ref, dx_ref, dg_ref, router_ref, x_ref, x1_ref, c_ref, o_ref, qkv_ref, a_ref, dense_ref, col_ref, acc_ref, dqkv_ref, do_ref))
    dx_out[...] = dx
    combine_back(dx, router_low[...], col_ref[...], row_ref[...], layer - 1, picked_low, dg_out, send_ref)
    flush_dense(acc_ref, dense_out)


def last_kernel(sizes, *refs):
    (back_ref, dx_ref, dg_ref, router_ref, x_ref, x1_ref, c_ref, o_ref, qkv_ref, a_ref, dense_ref, col_ref, dx_out, dense_out, acc_ref, dqkv_ref, do_ref) = refs
    dx = back_common(sizes, 0, (back_ref, dx_ref, dg_ref, router_ref, x_ref, x1_ref, c_ref, o_ref, qkv_ref, a_ref, dense_ref, col_ref, acc_ref, dqkv_ref, do_ref))
    dx_out[...] = unpack_rows(dx, sizes[0], dx_out.shape[0] // sizes[0])
    flush_dense(acc_ref, dense_out)


class Shapes:
    def __init__(self, micros, images, rows, each, width, hidden, experts, slots_each, dense_rows, shards):
        self.micros, self.images, self.rows, self.each = micros, images, rows, each
        self.width, self.hidden, self.experts, self.slots_each = width, hidden, experts, slots_each
        self.dense_rows, self.shards = dense_rows, shards
        self.toks = images * rows
        self.sizes = (images, rows, experts)

    def per_micro(self, *shape, dtype=F32):
        full = (self.micros, *shape)
        spec = pl.BlockSpec((None, *shape), lambda m: (m, *([0] * len(shape))))
        return spec, jax.ShapeDtypeStruct(full, dtype)

    def exchange(self):
        full = (self.experts, self.micros, self.slots_each, self.width)
        spec = pl.BlockSpec((self.experts, None, self.slots_each, self.width), lambda m: (0, m, 0, 0))
        return spec, jax.ShapeDtypeStruct(full, BF16)

    def token_block(self, dtype):
        per = self.images * self.each
        return pl.BlockSpec((per, self.width), lambda m: (m, 0)), jax.ShapeDtypeStruct((self.micros * per, self.width), dtype)

    def whole(self, *shape, dtype=BF16):
        spec = pl.BlockSpec(shape, lambda m: (0,) * len(shape), pipeline_mode=pl.Buffered(1))
        return spec, jax.ShapeDtypeStruct(shape, dtype)

    def forward_outs(self):
        t, w = self.toks, self.width
        return [
            self.per_micro(t, w),
            self.per_micro(t, 3 * w, dtype=BF16),
            self.per_micro(t, w, dtype=BF16),
            self.per_micro(t, w, dtype=BF16),
            self.per_micro(t, w),
            self.per_micro(t, w, dtype=BF16),
            self.per_micro(t, LANES),
            self.exchange(),
        ]

    def picked(self):
        return self.per_micro(2, self.toks, self.width, dtype=BF16)

    def cols(self):
        return self.per_micro(self.toks, LANES, dtype=jnp.int32)

    def row(self):
        return self.per_micro(8, self.toks, dtype=jnp.int32)

    def dense(self):
        return self.whole(self.dense_rows, self.width)

    def dense_out(self):
        return self.whole(self.shards, up_to(self.dense_rows // self.shards, 16), self.width)

    def scratch(self):
        return [
            pltpu.VMEM((self.dense_rows, self.width), F32),
            pltpu.VMEM((self.toks, 3 * self.width), BF16),
            pltpu.VMEM((self.toks, self.width), BF16),
        ]

    def saved_ins(self):
        t, w = self.toks, self.width
        return [self.exchange(), self.per_micro(t, w), self.per_micro(t, LANES), self.per_micro(t, LANES)] + self.forward_outs()[0:1] + [
            self.per_micro(t, w),
            self.per_micro(t, w, dtype=BF16),
            self.per_micro(t, w, dtype=BF16),
            self.per_micro(t, 3 * w, dtype=BF16),
            self.per_micro(t, w, dtype=BF16),
            self.dense(),
            self.cols(),
        ]

    def call(self, kernel, ins, outs, args, name, scratch=()):
        return pl.pallas_call(
            kernel,
            grid=(self.micros,),
            in_specs=[spec for spec, _ in ins],
            out_specs=[spec for spec, _ in outs],
            out_shape=[shape for _, shape in outs],
            scratch_shapes=list(scratch),
            compiler_params=pltpu.CompilerParams(vmem_limit_bytes=VMEM_LIMIT),
            name=name,
        )(*args)


def first_stage(shp, tokens, dense, cols, rows):
    return shp.call(
        functools.partial(first_kernel, shp.sizes),
        [shp.token_block(BF16), shp.dense(), shp.cols(), shp.row()],
        shp.forward_outs(),
        (tokens, dense, cols, rows),
        "attn_first",
    )


def middle_stage(shp, layer, back, x1, router, dense, cols, rows):
    t, w = shp.toks, shp.width
    return shp.call(
        functools.partial(middle_kernel, shp.sizes, layer),
        [shp.exchange(), shp.per_micro(t, w), shp.per_micro(t, LANES), shp.dense(), shp.cols(), shp.row()],
        [shp.picked(), *shp.forward_outs()],
        (back, x1, router, dense, cols, rows),
        "attn_next",
    )


def turn_stage(shp, layer, back, x1, router, cotangent, cols, rows):
    t, w = shp.toks, shp.width
    return shp.call(
        functools.partial(turn_kernel, shp.sizes, layer),
        [shp.exchange(), shp.per_micro(t, w), shp.per_micro(t, LANES), shp.token_block(BF16), shp.cols(), shp.row()],
        [shp.token_block(F32), shp.per_micro(t, w), shp.per_micro(t, LANES), shp.exchange()],
        (back, x1, router, cotangent, cols, rows),
        "turn",
        scratch=[pltpu.VMEM((2, t, w), BF16)],
    )


def back_stage(shp, layer, back, dx, dg, saved, dense, cols, rows, router_low, picked_low):
    t, w = shp.toks, shp.width
    x, qkv, a, o, x1, c, router = saved
    return shp.call(
        functools.partial(back_kernel, shp.sizes, layer),
        [*shp.saved_ins(), shp.row(), shp.per_micro(t, LANES), shp.picked()],
        [shp.per_micro(t, w), shp.per_micro(t, LANES), shp.exchange(), shp.dense_out()],
        (back, dx, dg, router, x, x1, c, o, qkv, a, dense, cols, rows, router_low, picked_low),
        "attn_back",
        scratch=shp.scratch(),
    )


def last_stage(shp, back, dx, dg, saved, dense, cols):
    x, qkv, a, o, x1, c, router = saved
    return shp.call(
        functools.partial(last_kernel, shp.sizes),
        shp.saved_ins(),
        [shp.token_block(F32), shp.dense_out()],
        (back, dx, dg, router, x, x1, c, o, qkv, a, dense, cols),
        "attn_last",
        scratch=shp.scratch(),
    )


def gelu_parts(h):
    cdf = 0.5 * (1.0 + lax.erf(h * INV_SQRT2))
    slope = cdf + h * (INV_SQRT2PI * jnp.exp(-0.5 * (h * h)))
    return (h * cdf).astype(BF16), slope.astype(BF16)


def expert_forward_kernel(x_ref, mats_ref, shift_ref, y_ref, act_ref, slope_ref):
    width, hidden = x_ref.shape[1], mats_ref.shape[1]
    shift = shift_ref[...].astype(F32)
    y = None
    for at in range(0, hidden, 512):
        cut = slice(at, at + 512)
        h = dot_nn(x_ref[...], mats_ref[:width, cut]) + shift[:, cut]
        act, slope = gelu_parts(h)
        act_ref[:, cut] = act
        slope_ref[:, cut] = slope
        piece = dot_nt(act, mats_ref[width:, cut])
        y = piece if y is None else y + piece
    y_ref[...] = (y + shift[:, hidden:]).astype(BF16)


def expert_forward(x, mats, shift):
    rows, width = x.shape
    hidden = mats.shape[1]
    block = 256
    return pl.pallas_call(
        expert_forward_kernel,
        grid=(rows // block,),
        in_specs=[
            pl.BlockSpec((block, width), lambda r: (r, 0)),
            pl.BlockSpec(mats.shape, lambda r: (0, 0), pipeline_mode=pl.Buffered(1)),
            pl.BlockSpec(shift.shape, lambda r: (0, 0)),
        ],
        out_specs=[
            pl.BlockSpec((block, width), lambda r: (r, 0)),
            pl.BlockSpec((block, hidden), lambda r: (r, 0)),
            pl.BlockSpec((block, hidden), lambda r: (r, 0)),
        ],
        out_shape=[
            jax.ShapeDtypeStruct((rows, width), BF16),
            jax.ShapeDtypeStruct((rows, hidden), BF16),
            jax.ShapeDtypeStruct((rows, hidden), BF16),
        ],
        compiler_params=pltpu.CompilerParams(vmem_limit_bytes=VMEM_LIMIT),
        name="expert_forward",
    )(x, mats, shift)


def expert_back_kernel(dy_ref, x_ref, act_ref, slope_ref, w_in_ref, w_out_ref, dx_ref, dw_ref, db_ref, xt_ref, dyt_ref, total_ref):
    step = pl.program_id(0)
    width = x_ref.shape[1]

    @pl.when(step == 0)
    def _():
        xt_ref[...] = x_ref[...].T
        dyt_ref[...] = dy_ref[...].T
        total_ref[...] = jnp.zeros_like(total_ref)

    dh = (dot_nn(dy_ref[...], w_out_ref[...]) * slope_ref[...].astype(F32)).astype(BF16)
    db_ref[...] = jnp.sum(dh.astype(F32), axis=0, keepdims=True)
    dw_ref[:width, :] = dot_nn(xt_ref[...], dh).astype(BF16)
    dw_ref[width:, :] = dot_nn(dyt_ref[...], act_ref[...]).astype(BF16)
    total_ref[...] += dot_nt(dh, w_in_ref[...])

    @pl.when(step == pl.num_programs(0) - 1)
    def _():
        dx_ref[...] = total_ref[...].astype(BF16)


def expert_back(dy, x, act, slope, mats):
    rows, width = x.shape
    hidden = mats.shape[1]
    block = 256
    full = lambda f: (0, 0)
    return pl.pallas_call(
        expert_back_kernel,
        grid=(hidden // block,),
        in_specs=[
            pl.BlockSpec((rows, width), full, pipeline_mode=pl.Buffered(1)),
            pl.BlockSpec((rows, width), full, pipeline_mode=pl.Buffered(1)),
            pl.BlockSpec((rows, block), lambda f: (0, f)),
            pl.BlockSpec((rows, block), lambda f: (0, f)),
            pl.BlockSpec((width, block), lambda f: (0, f)),
            pl.BlockSpec((width, block), lambda f: (1, f)),
        ],
        out_specs=[
            pl.BlockSpec((rows, width), full, pipeline_mode=pl.Buffered(1)),
            pl.BlockSpec((2 * width, block), lambda f: (0, f)),
            pl.BlockSpec((1, block), lambda f: (0, f)),
        ],
        out_shape=[
            jax.ShapeDtypeStruct((rows, width), BF16),
            jax.ShapeDtypeStruct((2 * width, hidden), BF16),
            jax.ShapeDtypeStruct((1, hidden), F32),
        ],
        scratch_shapes=[
            pltpu.VMEM((width, rows), BF16),
            pltpu.VMEM((width, rows), BF16),
            pltpu.VMEM((rows, width), F32),
        ],
        compiler_params=pltpu.CompilerParams(vmem_limit_bytes=VMEM_LIMIT),
        name="expert_back",
    )(dy, x, act, slope, mats, mats)


def adam_update(master, first_mom, second_mom, gradient, clip_scale, step_float):
    clipped = gradient * clip_scale
    first_new = BETA_ONE * first_mom + (1.0 - BETA_ONE) * clipped
    second_new = BETA_TWO * second_mom + (1.0 - BETA_TWO) * clipped * clipped
    first_hat = first_new / (1.0 - BETA_ONE**step_float)
    second_hat = second_new / (1.0 - BETA_TWO**step_float)
    change = -STEP_RATE * (first_hat / (jnp.sqrt(second_hat) + ADAM_EPS) + DECAY_RATE * master)
    return (change, first_new, second_new)


def local(
    tokens,
    cotangent,
    valid,
    routes,
    priority,
    step,
    dense_master,
    dense_first,
    dense_second,
    expert_master,
    expert_first,
    expert_second,
    shift_master,
    shift_first,
    shift_second,
):
    layer_count, shard_rows, width = dense_master.shape
    micros, group_tok = priority.shape
    each = valid.shape[1]
    images = group_tok // each
    hidden = expert_master.shape[3]
    groups = lax.axis_size("expert")
    shards = lax.axis_size("dp")
    experts = expert_master.shape[1] * groups
    capacity = (9 * images * PATCHES + 4 * experts - 1) // (4 * experts)
    slots_each = up_to(capacity, 16)
    rows = up_to(PATCHES, 16)
    shp = Shapes(micros, images, rows, each, width, hidden, experts, slots_each, shard_rows * shards, shards)

    dense_low = dense_master.astype(BF16)
    dense = [lax.all_gather(dense_low[i], "dp", axis=0, tiled=True) for i in range(layer_count)]
    expert_low = expert_master.astype(BF16)
    shift_low = shift_master.astype(BF16)
    mats = [lax.all_gather(expert_low[i, 0], "dp", axis=0, tiled=True) for i in range(layer_count)]
    shift = lax.all_gather(shift_low, "dp", axis=2, tiled=True)

    def cut(values):
        return values.reshape(micros, images, each)[:, :, :rows].reshape(micros, images * rows)

    planes = [cut(priority), cut(valid)]
    for i in range(layer_count):
        planes += [cut(routes[i, :, 0]), cut(routes[i, :, 1])]
    planes += [jnp.zeros_like(planes[0])] * (8 - len(planes))
    meta = jnp.stack(planes, axis=1)
    slot_col, slot_row = routing(meta, jnp.swapaxes(meta, 1, 2), capacity, slots_each, experts, layer_count)

    def exchange(values):
        return lax.all_to_all(values, "expert", split_axis=0, concat_axis=0, tiled=True)

    flat = (experts * micros * slots_each, width)
    saved, kept, picks = [], [], []
    for i in range(layer_count):
        if i == 0:
            outs = first_stage(shp, tokens, dense[0], slot_col, slot_row)
        else:
            picked, *outs = middle_stage(shp, i, back, saved[i - 1][4], saved[i - 1][6], dense[i], slot_col, slot_row)
            picks.append(picked)
        *state, send = outs
        saved.append(state)
        received = exchange(send).reshape(flat)
        produced, act, slope = expert_forward(received, mats[i], shift[i])
        kept.append((received, act, slope))
        back = exchange(produced.reshape(send.shape))
    top = layer_count - 1
    output, dx, dg, send = turn_stage(shp, top, back, saved[top][4], saved[top][6], cotangent, slot_col, slot_row)
    dense_grads, mats_grads, shift_grads = [None] * layer_count, [None] * layer_count, [None] * layer_count
    for i in reversed(range(layer_count)):
        received, act, slope = kept[i]
        dy = exchange(send).reshape(flat)
        dsent, dmats, dshift_in = expert_back(dy, received, act, slope, mats[i])
        mats_grads[i] = dmats
        shift_grads[i] = jnp.concatenate([dshift_in[0], jnp.sum(dy, axis=0, dtype=F32)])
        back = exchange(dsent.reshape(send.shape))
        if i:
            dx, dg, send, dense_grads[i] = back_stage(
                shp, i, back, dx, dg, saved[i], dense[i], slot_col, slot_row, saved[i - 1][6], picks[i - 1]
            )
        else:
            grad_tokens, dense_grads[i] = last_stage(shp, back, dx, dg, saved[i], dense[i], slot_col)
    dense_parts_sum = [
        lax.psum(lax.psum_scatter(g, "dp", scatter_dimension=0, tiled=False), "expert") for g in dense_grads
    ]
    dense_shard = jnp.stack([g[:shard_rows] for g in dense_parts_sum]).astype(F32)
    expert_shard = jnp.stack(
        [lax.psum_scatter(g, "dp", scatter_dimension=0, tiled=True) for g in mats_grads]
    ).astype(F32)[:, None]
    shift_shard = lax.psum_scatter(
        jnp.stack(shift_grads)[:, None].astype(BF16), "dp", scatter_dimension=2, tiled=True
    ).astype(F32)
    first_replica = (lax.axis_index("expert") == 0).astype(F32)
    square = (
        jnp.sum(dense_shard * dense_shard) * first_replica
        + jnp.sum(expert_shard * expert_shard)
        + jnp.sum(shift_shard * shift_shard)
    )
    grad_norm = jnp.sqrt(lax.psum(square, ("dp", "expert")))
    clip_scale = CLIP_NORM / jnp.maximum(grad_norm, CLIP_NORM)
    step_float = step.astype(F32)
    dense_new = adam_update(dense_master, dense_first, dense_second, dense_shard, clip_scale, step_float)
    expert_new = adam_update(expert_master, expert_first, expert_second, expert_shard, clip_scale, step_float)
    shift_new = adam_update(shift_master, shift_first, shift_second, shift_shard, clip_scale, step_float)
    return (output, grad_tokens, grad_norm, dense_shard, *dense_new, expert_shard, *expert_new, shift_shard, *shift_new)


def solution(mesh):
    split = P(("dp", "expert"), None)
    dense = P(None, "dp", None)
    mats = P(None, "expert", "dp", None)
    shift = P(None, "expert", "dp")
    placed = (split, split, split, P(None, ("dp", "expert"), None), split, P()) + (dense,) * 3 + (mats,) * 3 + (shift,) * 3
    return jax.shard_map(
        local,
        mesh=mesh,
        in_specs=placed,
        out_specs=(split, split, P()) + (dense,) * 4 + (mats,) * 4 + (shift,) * 4,
        check_vma=False,
    )
```

time: 1400 us -> 927 us (0.66)
  matrix products: 451 us -> 0 us
  local copies, waits for them, and re-layouts: 416 us -> 52.6 us
  waiting for transfers between devices: 177 us -> 387 us
  Pallas kernels: 0 us -> 186 us
  blocking collectives: 45.7 us -> 231 us
  other arithmetic: 188 us -> 24.3 us
  starting transfers between devices: 91.1 us -> 17.4 us
    dot_general x84 -> x0, matrix products: 451 us -> none  [the longest x4 85.5 us: backward_layer(): jnp.einsum('sjcd,sjcf->jdf', grad_recv, active, preferred_element_type=jn...]
    pallas_call x0 -> x10, Pallas kernels: none -> 186 us  [the longest x5 87.4 us: call(): pl.pallas_call(kernel, grid=(self.micros,), in_specs=[spec for spec, _ in...]
    all_to_all x0 -> x4, blocking collectives: none -> 186 us  [exchange(): lax.all_to_all(values, 'expert', split_axis=0, concat_axis=0, tiled=True)]
    all_to_all x16 -> x4, waiting for transfers between devices: 18.9 us -> 150 us  [exchange(): lax.all_to_all(values, 'expert', split_axis=0, concat_axis=0, tiled=True)]
    gather x38 -> x0, local copies, waits for them, and re-layouts: 93.4 us -> none  [the longest x8 23.7 us: backward_layer(): grad_pad[slot_source[:slot_total]] * slot_gate[:slot_total, None]]
    reduce_sum x67 -> x4, other arithmetic: 83.2 us -> 8.48 us  [the longest x1 5.2 us: local(): jnp.sum(expert_shard * expert_shard)]
    all_to_all x16 -> x4, starting transfers between devices: 90.6 us -> 16.4 us  [exchange(): lax.all_to_all(values, 'expert', split_axis=0, concat_axis=0, tiled=True)]
    concatenate x24 -> x0, local copies, waits for them, and re-layouts: 51.1 us -> none  [the longest x8 49 us: backward_layer(): jnp.concatenate([qkv_grad, out_grad, router_grad, vector_grad], axis=0)]
  transfers between devices with their start and end apart: 23 -> 14, of which waited for: 9 -> 11; matrix products, arithmetic and copies ran while one was open for 50% -> 5% of each run, Pallas kernels for 0% -> 11%
where the time goes in v1:
time: 927 us; the launch traced here: 918 us
  waiting for transfers between devices  387 us (42%)
  blocking collectives  231 us (25%)
  Pallas kernels  186 us (20%)
  local copies, waits for them, and re-layouts  52.6 us (6%)
  other arithmetic  24.3 us (3%)
  between operations  19.2 us (2%)
  starting transfers between devices  17.4 us (2%)
    all_to_all x4, blocking collectives, exchange(): lax.all_to_all(values, 'expert', split_axis=0, concat_axis=0, tiled=True)  186 us
    all_to_all x4, waiting for transfers between devices, exchange(): lax.all_to_all(values, 'expert', split_axis=0, concat_axis=0, tiled=True)  150 us
    reduce_scatter x2, waiting for transfers between devices, local(): lax.psum_scatter(g, 'dp', scatter_dimension=0, tiled=True)  92.9 us
    pallas_call x5, Pallas kernels, call(): pl.pallas_call(kernel, grid=(self.micros,), in_specs=[spec for spec, _ in...  87.4 us
    psum x1, waiting for transfers between devices, local(): lax.psum(lax.psum_scatter(g, 'dp', scatter_dimension=0, tiled=False), 'ex...  76.7 us
    pallas_call x2, Pallas kernels, expert_back(): pl.pallas_call(expert_back_kernel, grid=(hidden // block,), in_specs=[pl....  55.9 us
    unnamed x48, local copies, waits for them, and re-layouts  43.4 us
    psum x1, blocking collectives, local(): grad_norm = jnp.sqrt(lax.psum(square, ('dp', 'expert')))  39.8 us
  transfers between devices with their start and end apart: 14, of which 11 were waited for; matrix products, arithmetic and copies ran while one was open for 5% of the time, Pallas kernels for 11%

profile of v1, /device:TPU:0, one launch (start us, length us, event | category | flops | bytes accessed | tf_op | source)
XLA Modules:
  0.0 917.8 jit_solution(8619464934294649089)
XLA Ops:
  7.2 2.3 convert_element_type.58
  9.6 2.5 fusion.12
  12.1 2.5 convert_element_type.59
  14.6 1.5 fusion.11
  17.7 1.1 stack.34
  18.8 0.8 copy.88.meta_ref
  19.6 7.6 routing.1
  27.1 22.4 %all-gather.9.cloned.1.call-done = bf16[1,2064,512]{2,0,1:T(2,128)(2,1)} async-done(((bf16[1,516,512]{2,0,1:T(2,128)(2,1)}), bf16[1,2064,512]{2,0,1:T(2,128)(2,1)}) %all-gather.9.cloned.1.call-update) | async-done | bytes 2113552 | tf_op jit(solution)/shard_map/all_gather | solution.py:685
  49.6 4.1 copy.116
  53.7 11.9 %attn_first.1 = (f32[2,416,512]{2,1,0:T(8,128)}, bf16[2,416,1536]{2,1,0:T(8,128)(2,1)}, bf16[2,416,512]{2,1,0:T(8,128)(2,1)}, bf16[2,416,512]{2,1,0:T(8,128)(2,1...) custom-call(bf16[1024,512]{1,0:T(8,128)(2,1)} %tok_ref.1, ...), custom_call_target="tpu_custom_call" | custom-call | tf_op jit(solution)/shard_map/attn_first/pallas_call | solution.py:469
  65.6 5.5 all-to-all-start
  71.1 0.7 all-gather.13.cloned.1.call-update
  71.9 5.8 all_gather.17
  77.6 0.6 slice_bitcast_fusion.2
  78.2 8.1 all-gather.11.cloned.1.call-done
  86.3 27.8 %all-to-all-done = bf16[8,2,112,512]{3,2,1,0:T(8,128)(2,1)S(1)} async-done(((bf16[8,2,112,512]{3,2,1,0:T(8,128)(2,1)}), bf16[8,2,112,512]{3,2,1,0:T(8,128)(2,1)S(1)}, u32[]{:S(2)}, u32[]{:S(2)}) %all-to-all-start) | async-done | bytes 1835040 | tf_op jit(solution)/shard_map/all_to_all | solution.py:702
  114.1 1.2 copy-done.2
  115.4 17.6 %expert_forward.2 = (bf16[1792,512]{1,0:T(8,128)(2,1)}, bf16[1792,2048]{1,0:T(8,128)(2,1)}, bf16[1792,2048]{1,0:T(8,128)(2,1)}) custom-call(bf16[1792,512]{1,0:T(8,128)(2,1)} %bitcast.49, bf16[1024,2048]{1,0:T(8,128)(2,1)} %bitcast.39, bf16[1,2560]{1,0:T(2,128)(2,1)} %get-tuple-element.196.shift_ref), custom_call_target="tpu_custom_call" | custom-call | tf_op jit(solution)/shard_map/expert_forward/pallas_call | solution.py:564
  132.9 3.6 all-to-all-start.1
  137.2 4.1 copy.115
  141.3 38.0 %all-to-all-done.1.back_ref = bf16[8,2,112,512]{3,2,1,0:T(8,128)(2,1)S(1)} async-done(((bf16[8,2,112,512]{3,2,1,0:T(8,128)(2,1)}), bf16[8,2,112,512]{3,2,1,0:T(8,128)(2,1)S(1)}, u32[]{:S(2)}, u32[]{:S(2)}) %all-to-all-start.1) | async-done | bytes 1835040 | tf_op jit(solution)/shard_map/all_to_all | solution.py:702
  179.3 1.2 copy-done.6
  180.6 15.7 %attn_next.1 = (bf16[2,2,416,512]{3,2,1,0:T(8,128)(2,1)}, f32[2,416,512]{2,1,0:T(8,128)}, bf16[2,416,1536]{2,1,0:T(8,128)(2,1)}, bf16[2,416,512]{2,1,0:T(8,128)(...) custom-call(bf16[8,2,112,512]{3,2,1,0:T(8,128)(2,1)} %copy-done.6, ...), custom_call_target="tpu_custom_call" | custom-call | tf_op jit(solution)/shard_map/attn_next/pallas_call | solution.py:469
  196.3 3.6 all-to-all-start.2
  200.0 42.8 %all-to-all-done.2 = bf16[8,2,112,512]{3,2,1,0:T(8,128)(2,1)S(1)} async-done(((bf16[8,2,112,512]{3,2,1,0:T(8,128)(2,1)}), bf16[8,2,112,512]{3,2,1,0:T(8,128)(2,1)S(1)}, u32[]{:S(2)}, u32[]{:S(2)}) %all-to-all-start.2) | async-done | bytes 1835040 | tf_op jit(solution)/shard_map/all_to_all | solution.py:702
  242.8 1.2 copy-done.5
  244.0 17.5 %expert_forward.3 = (bf16[1792,512]{1,0:T(8,128)(2,1)}, bf16[1792,2048]{1,0:T(8,128)(2,1)}, bf16[1792,2048]{1,0:T(8,128)(2,1)}) custom-call(bf16[1792,512]{1,0:T(8,128)(2,1)} %bitcast.53, bf16[1024,2048]{1,0:T(8,128)(2,1)} %bitcast.42, bf16[1,2560]{1,0:T(2,128)(2,1)} %get-tuple-element.195.shift_ref), custom_call_target="tpu_custom_call" | custom-call | tf_op jit(solution)/shard_map/expert_forward/pallas_call | solution.py:564
  261.5 46.6 %all_to_all.40.back_ref = bf16[8,2,112,512]{3,2,1,0:T(8,128)(2,1)} all-to-all(bf16[8,2,112,512]{3,2,1,0:T(8,128)(2,1)} %bitcast.59), channel_id=1, replica_groups=mesh['dp'=4,'expert'=8] {'expert'}, dimensions={0} | all-to-all | bytes 3670016 | tf_op jit(solution)/shard_map/all_to_all | solution.py:702
  308.2 7.6 turn.1
  315.8 46.2 %all_to_all.41 = bf16[8,2,112,512]{3,2,1,0:T(8,128)(2,1)} all-to-all(bf16[8,2,112,512]{3,2,1,0:T(8,128)(2,1)} %get-tuple-element.67), channel_id=1, replica_groups=mesh['dp'=4,'expert'=8] {'expert'}, dimensions={0} | all-to-all | bytes 3670016 | tf_op jit(solution)/shard_map/all_to_all | solution.py:702
  362.0 27.9 %expert_back.2 = (bf16[1792,512]{1,0:T(8,128)(2,1)}, bf16[1024,2048]{1,0:T(8,128)(2,1)}, f32[1,2048]{1,0:T(1,128)}) custom-call(bf16[1792,512]{1,0:T(8,128)(2,1)} %bitcast.51, bf16[1792,512]{1,0:T(8,128)(2,1)} %bitcast.54, bf16[1792,2048]{1,0:T(8,128)(2,1)} %get-tuple-element.68.act_ref, bf16[1792,2048]{1,0:T(8,128)(2,1)} %get-tuple-element.69.slope_ref, ...), custom_call_target="tpu_custom_call" | custom-call | tf_op jit(solution)/shard_map/expert_back/pallas_call | solution.py:613
  389.9 46.2 %all_to_all.42.refs_0_ = bf16[8,2,112,512]{3,2,1,0:T(8,128)(2,1)} all-to-all(bf16[8,2,112,512]{3,2,1,0:T(8,128)(2,1)} %bitcast.57), channel_id=1, replica_groups=mesh['dp'=4,'expert'=8] {'expert'}, dimensions={0} | all-to-all | bytes 3670016 | tf_op jit(solution)/shard_map/all_to_all | solution.py:702
  436.1 27.6 %attn_back.1 = (f32[2,416,512]{2,1,0:T(8,128)}, f32[2,416,128]{2,1,0:T(8,128)}, bf16[8,2,112,512]{3,2,1,0:T(8,128)(2,1)}, bf16[4,528,512]{2,1,0:T(8,128)(2,1)}) custom-call(bf16[8,2,112,512]{3,2,1,0:T(8,128)(2,1)} %all_to_all.42.refs_0_, f32[2,416,512]{2,1,0:T(8,128)} %get-tuple-element.71.refs_1_, f32[2,416,128]{2,1,0:T(8,128)} %get-tuple-element.72.refs_2_, ...), custom_call_target="tpu_custom_call" | custom-call | tf_op jit(solution)/shard_map/attn_back/pallas_call | solution.py:469
  463.7 3.6 all-to-all-start.6
  467.4 0.5 reduce-scatter.10.cloned.1.call-update
  468.2 41.3 %all-to-all-done.6 = bf16[8,2,112,512]{3,2,1,0:T(8,128)(2,1)S(1)} async-done(((bf16[8,2,112,512]{3,2,1,0:T(8,128)(2,1)}), bf16[8,2,112,512]{3,2,1,0:T(8,128)(2,1)S(1)}, u32[]{:S(2)}, u32[]{:S(2)}) %all-to-all-start.6) | async-done | bytes 1835040 | tf_op jit(solution)/shard_map/all_to_all | solution.py:702
  509.5 1.2 copy-done.4
  510.7 27.9 %expert_back.3 = (bf16[1792,512]{1,0:T(8,128)(2,1)}, bf16[1024,2048]{1,0:T(8,128)(2,1)}, f32[1,2048]{1,0:T(1,128)}) custom-call(bf16[1792,512]{1,0:T(8,128)(2,1)} %bitcast.52, bf16[1792,512]{1,0:T(8,128)(2,1)} %bitcast.50, bf16[1792,2048]{1,0:T(8,128)(2,1)} %get-tuple-element.80.act_ref, bf16[1792,2048]{1,0:T(8,128)(2,1)} %get-tuple-element.81.slope_ref, ...), custom_call_target="tpu_custom_call" | custom-call | tf_op jit(solution)/shard_map/expert_back/pallas_call | solution.py:613
  538.6 46.6 %all_to_all.43.refs_0_ = bf16[8,2,112,512]{3,2,1,0:T(8,128)(2,1)} all-to-all(bf16[8,2,112,512]{3,2,1,0:T(8,128)(2,1)} %bitcast.58), channel_id=1, replica_groups=mesh['dp'=4,'expert'=8] {'expert'}, dimensions={0} | all-to-all | bytes 3670016 | tf_op jit(solution)/shard_map/all_to_all | solution.py:702
  585.2 24.5 %attn_last.1 = (f32[1024,512]{1,0:T(8,128)}, bf16[4,528,512]{2,1,0:T(8,128)(2,1)}) custom-call(bf16[8,2,112,512]{3,2,1,0:T(8,128)(2,1)} %all_to_all.43.refs_0_, f32[2,416,512]{2,1,0:T(8,128)} %get-tuple-element.83.refs_1_, f32[2,416,128]{2,1,0:T(8,128)} %get-tuple-element.84.refs_2_, f32[2,416,128]{2,1,0:T(8,128)} %get-tuple-element.61.router_old.refs_13_.refs_3_, ...), custom_call_target="tpu_custom_call" | custom-call | tf_op jit(solution)/shard_map/attn_last/pallas_call | solution.py:469
  610.3 1.0 copy-done.3
  611.7 1.8 reduce.2
  613.6 1.1 copy.96
  614.7 14.4 %bitcast_reduce_fusion = bf16[2560,2]{1,0:T(8,128)(2,1)} fusion(bf16[2,1,2560]{1,0,2:T(2,128)(2,1)S(1)} %copy.96), kind=kLoop, calls=%fused_computation.17 | loop fusion | bytes 20480
  629.1 0.7 reduce-scatter.14.cloned.1.call-update
  629.9 0.7 reduce-scatter.12.cloned.1.call-update
  630.6 8.9 reduce-scatter.8.cloned.1.call-done
  640.3 24.8 %reduce-scatter.16.cloned.1.call-done = bf16[640,2]{1,0:T(8,128)(2,1)} async-done(((bf16[2560,2]{1,0:T(8,128)(2,1)}), bf16[640,2]{1,0:T(8,128)(2,1)}) %reduce-scatter.16.cloned.1.call-update) | async-done | bytes 2576
  665.2 1.7 reshape_bitcast_fusion
  667.1 0.6 multiply_reduce_fusion.2
  667.7 45.2 %reduce-scatter.14.cloned.1.call-done = bf16[256,2048]{1,0:T(8,128)(2,1)} async-done(((bf16[1024,2048]{1,0:T(8,128)(2,1)}), bf16[256,2048]{1,0:T(8,128)(2,1)}) %reduce-scatter.14.cloned.1.call-update) | async-done | bytes 1048592 | tf_op jit(solution)/shard_map/reduce_scatter | solution.py:739
  712.9 47.7 %reduce-scatter.12.cloned.1.call-done = bf16[256,2048]{1,0:T(8,128)(2,1)} async-done(((bf16[1024,2048]{1,0:T(8,128)(2,1)}), bf16[256,2048]{1,0:T(8,128)(2,1)}) %reduce-scatter.12.cloned.1.call-update) | async-done | bytes 1048592 | tf_op jit(solution)/shard_map/reduce_scatter | solution.py:739
  760.6 5.2 multiply_reduce_fusion
  765.8 76.7 %all-reduce.3.cloned.1.call-done = (bf16[528,512]{1,0:T(8,128)(2,1)}, bf16[528,512]{1,0:T(8,128)(2,1)}) async-done(((bf16[528,512]{1,0:T(8,128)(2,1)}, bf16[528,512]{1,0:T(8,128)(2,1)}), (bf16[528,512]{1,0:T(8,128)(2,1)}, bf16[528,512]{1,0:T(8,128)(2,1)})) %all-reduce.3.cloned.1.call-update) | async-done | bytes 1081360 | tf_op jit(solution)/shard_map/psum | solution.py:735
  842.6 1.3 slice_bitcast_fusion
  843.9 1.1 multiply_reduce_fusion.1
  847.1 39.8 %psum.23 = f32[]{:T(128)} all-reduce(f32[]{:T(128)S(6)} %add.68), channel_id=1, replica_groups=mesh['dp'=4,'expert'=8] {'dp','expert'}, use_global_device_ids=true, to_apply=%region_12.0 | all-reduce | flops 1 | bytes 8 | tf_op jit(solution)/shard_map/psum | solution.py:750
  887.6 3.8 fusion.3
  891.4 3.0 copy.93
  894.3 3.0 copy.94
  897.3 3.0 copy.95
  900.3 3.0 copy.92
  903.2 0.6 add_multiply_fusion.1
  903.9 5.7 add_multiply_fusion
  (77 shorter events, 4.0 us)
Async XLA Ops:
  7.2 42.4 %all-gather.9.cloned.1.call-start = ((), (), s32[]{:S(2)}) async-start(), calls=%async_computation.17 | async-start | bytes 5283840 | tf_op jit(solution)/shard_map/all_gather | solution.py:685
  12.1 74.3 %all-gather.11.cloned.1.call-start = ((), (), s32[]{:S(2)}) async-start(), calls=%async_computation.18 | async-start | bytes 5242880 | tf_op jit(solution)/shard_map/all_gather | solution.py:688
  14.6 1.5 copy-start.12
  16.1 1.1 copy-start.17
  16.1 1.3 copy-start.18
  18.8 0.8 copy-start.9
  65.6 6.3 copy-start.10
  65.6 48.5 %all-to-all-start = ((bf16[8,2,112,512]{3,2,1,0:T(8,128)(2,1)}), bf16[8,2,112,512]{3,2,1,0:T(8,128)(2,1)S(1)}, u32[]{:S(2)}, u32[]{:S(2)}) async-start(bf16[8,2,112,512]{3,2,1,0:T(8,128)(2,1)} %get-tuple-element.58), calls=%async_computation | async-start | bytes 3670016 | tf_op jit(solution)/shard_map/all_to_all | solution.py:702
  71.1 66.1 %all-gather.13.cloned.1.call-start = ((), (), s32[]{:S(2)}) async-start(), calls=%async_computation.19 | async-start | bytes 5283840 | tf_op jit(solution)/shard_map/all_gather | solution.py:685
  114.1 1.2 copy-start.2
  132.9 46.4 %all-to-all-start.1 = ((bf16[8,2,112,512]{3,2,1,0:T(8,128)(2,1)}), bf16[8,2,112,512]{3,2,1,0:T(8,128)(2,1)S(1)}, u32[]{:S(2)}, u32[]{:S(2)}) async-start(bf16[8,2,112,512]{3,2,1,0:T(8,128)(2,1)} %bitcast.56), calls=%async_computation.1 | async-start | bytes 3670016 | tf_op jit(solution)/shard_map/all_to_all | solution.py:702
  136.6 63.4 %all-gather.15.cloned.1.call-start = ((), (), s32[]{:S(2)}) async-start(), calls=%async_computation.20 | async-start | bytes 5242880 | tf_op jit(solution)/shard_map/all_gather | solution.py:688
  179.3 1.2 copy-start.6
  196.3 46.4 %all-to-all-start.2 = ((bf16[8,2,112,512]{3,2,1,0:T(8,128)(2,1)}), bf16[8,2,112,512]{3,2,1,0:T(8,128)(2,1)S(1)}, u32[]{:S(2)}, u32[]{:S(2)}) async-start(bf16[8,2,112,512]{3,2,1,0:T(8,128)(2,1)} %get-tuple-element.62), calls=%async_computation.2 | async-start | bytes 3670016 | tf_op jit(solution)/shard_map/all_to_all | solution.py:702
  242.8 1.2 copy-start.5
  463.7 45.7 %all-to-all-start.6 = ((bf16[8,2,112,512]{3,2,1,0:T(8,128)(2,1)}), bf16[8,2,112,512]{3,2,1,0:T(8,128)(2,1)S(1)}, u32[]{:S(2)}, u32[]{:S(2)}) async-start(bf16[8,2,112,512]{3,2,1,0:T(8,128)(2,1)} %get-tuple-element.79), calls=%async_computation.6 | async-start | bytes 3670016 | tf_op jit(solution)/shard_map/all_to_all | solution.py:702
  467.3 163.3 %reduce-scatter.10.cloned.1.call-start = ((), (), s32[]{:S(2)}) async-start(), calls=%async_computation.14 | async-start | bytes 2703360 | tf_op jit(solution)/shard_map/reduce_scatter | solution.py:735
  467.9 171.6 %reduce-scatter.8.cloned.1.call-start = ((), (), s32[]{:S(2)}) async-start(), calls=%async_computation.13 | async-start | bytes 2703360 | tf_op jit(solution)/shard_map/reduce_scatter | solution.py:735
  509.5 1.2 copy-start.4
  609.8 1.5 copy-start.3
  609.8 1.8 copy-start.13
  609.8 3.7 copy-start.14
  609.8 55.3 %reduce-scatter.16.cloned.1.call-start = ((), (), s32[]{:S(2)}) async-start(), calls=%async_computation.21 | async-start | bytes 819200
  629.1 83.8 %reduce-scatter.14.cloned.1.call-start = ((), (), s32[]{:S(2)}) async-start(), calls=%async_computation.16 | async-start | bytes 5242880 | tf_op jit(solution)/shard_map/reduce_scatter | solution.py:739
  629.8 130.8 %reduce-scatter.12.cloned.1.call-start = ((), (), s32[]{:S(2)}) async-start(), calls=%async_computation.15 | async-start | bytes 5242880 | tf_op jit(solution)/shard_map/reduce_scatter | solution.py:739
  630.6 212.0 %all-reduce.3.cloned.1.call-start = ((), (), s32[]{:S(2)}) async-start(), calls=%async_computation.22 | async-start | bytes 2162688 | tf_op jit(solution)/shard_map/psum | solution.py:735
  667.7 235.5 %copy-start.11 = (f32[2,1,640]{2,1,0:T(1,128)}, f32[2,1,640]{2,1,0:T(1,128)S(1)}, u32[]{:S(2)}) copy-start(f32[2,1,640]{2,1,0:T(1,128)S(1)} %get-tuple-element.188) | copy-start | bytes 15364
  891.4 12.5 %copy-start.8 = (f32[2,1,256,2048]{3,2,1,0:T(8,128)S(1)}, f32[2,1,256,2048]{3,2,1,0:T(8,128)}, u32[]{:S(2)}) copy-start(f32[2,1,256,2048]{3,2,1,0:T(8,128)} %param.25) | copy-start | bytes 12582916
  894.3 9.5 %copy-start.7 = (f32[2,1,256,2048]{3,2,1,0:T(8,128)S(1)}, f32[2,1,256,2048]{3,2,1,0:T(8,128)}, u32[]{:S(2)}) copy-start(f32[2,1,256,2048]{3,2,1,0:T(8,128)} %param.26) | copy-start | bytes 12582916
  897.3 6.6 copy-start.1
  900.2 3.0 copy-start.15
  900.2 3.0 copy-start.16
  900.2 3.6 copy-start
Sparse Core Ops, SparseCore 0:
  12.2 37.3 all-gather.8
  51.7 34.5 all-gather.10
  88.4 34.6 all-gather.12
  139.2 34.9 all-gather.14
  471.0 31.9 reduce-scatter.9
  610.0 29.5 reduce-scatter.7
  642.6 22.4 reduce-scatter.15
  668.3 44.5 reduce-scatter.13
  716.0 44.5 reduce-scatter.11
  764.0 78.5 all-reduce.2

commit v2 on v1

--- a/solution.py
+++ b/solution.py
@@ -77,65 +77,66 @@
     return router_rows, vectors
 
 
-def routing_kernel(capacity, slots_each, experts, layers, meta_ref, cols_ref, slot_col_ref, slot_row_ref):
-    toks = meta_ref.shape[-1]
-    meta = meta_ref[...]
-    cols = cols_ref[...]
-    rank_row, rank_col = meta[0:1], cols[:, 0:1]
-    ok_row, ok_col = meta[1:2], cols[:, 1:2]
-    before = one_where(rank_row < rank_col)
-    before_t = one_where(rank_col < rank_row)
+def cost(us):
+    return pl.CostEstimate(flops=int(us * 1.0e9), bytes_accessed=int(us * 3.0e6), transcendentals=0)
+
+
+def routing_kernel(capacity, slots_each, experts, rows, priority_ref, valid_ref, routes_ref, slot_col_ref, slot_row_ref):
+    micro = pl.program_id(0)
+    layers, _, group = routes_ref.shape
+    images = valid_ref.shape[0] // priority_ref.shape[0]
+    each = valid_ref.shape[1]
+    lines = [priority_ref[pl.ds(micro, 1), :]]
+    lines.append(jnp.concatenate([valid_ref[pl.ds(micro * images + i, 1), :] for i in range(images)], axis=1))
+    for layer in range(layers):
+        for k in range(2):
+            lines.append(routes_ref[layer, k : k + 1, :])
+    subs = lax.broadcasted_iota(jnp.int32, (LANES, group), 0)
+    table = jnp.zeros((LANES, group), F32)
+    for at, line in enumerate(lines):
+        table = jnp.where(subs == at, line.astype(F32), table)
+    cols = table.T
+
+    def packed(column):
+        return jnp.concatenate([column[i * each : i * each + rows] for i in range(images)], axis=0)
+
+    mine = packed(cols)
+    toks = images * rows
+    before = one_where(lines[0].astype(F32) < mine[:, 0:1])
+    ok_all, ok_mine = cols[:, 1:2] > 0.0, mine[:, 1:2] > 0.0
+    labels = lane_ids(1).astype(F32)
     lanes = lane_ids(toks)
-    subs = lax.broadcasted_iota(jnp.int32, (LANES, toks), 0)
-    col_out = [None] * 16
-    row_out = [None] * 8
+    full = jnp.where(lanes == 8, mine[:, 1:2], 0.0)
     for layer in range(layers):
-        counts, ones, counts_t, ones_t, totals, totals_t = [], [], [], [], [], []
+        firsts = 0.0
         for k in range(2):
-            named = cols[:, 2 + 2 * layer + k : 3 + 2 * layer + k]
-            hot = jnp.where((lanes == named) & (ok_col > 0), 1.0, 0.0)
-            ones.append(hot)
-            counts.append(dot_nn(before, hot.astype(BF16)))
-            totals.append(jnp.sum(hot, axis=0, keepdims=True))
-            named_t = meta[2 + 2 * layer + k : 3 + 2 * layer + k]
-            hot_t = jnp.where((subs == named_t) & (ok_row > 0), 1.0, 0.0)
-            ones_t.append(hot_t)
-            counts_t.append(dot_nn(hot_t.astype(BF16), before_t))
-            totals_t.append(jnp.sum(hot_t, axis=1, keepdims=True))
-        for k in range(2):
-            extra = totals[0] if k else 0.0
-            place = jnp.sum((counts[k] + extra) * ones[k], axis=1, keepdims=True).astype(jnp.int32)
-            named = cols[:, 2 + 2 * layer + k : 3 + 2 * layer + k]
-            held = (place < capacity) & (ok_col > 0)
-            col_out[2 * layer + k] = jnp.where(held, named * slots_each + place, -1)
-            col_out[4 + 2 * layer + k] = named
-            extra_t = totals_t[0] if k else 0.0
-            place_t = jnp.sum((counts_t[k] + extra_t) * ones_t[k], axis=0, keepdims=True).astype(jnp.int32)
-            named_t = meta[2 + 2 * layer + k : 3 + 2 * layer + k]
-            held_t = (place_t < capacity) & (ok_row > 0)
-            row_out[2 * layer + k] = jnp.where(held_t, named_t * slots_each + place_t, -1)
-    col_out[8] = ok_col
-    full = jnp.zeros((toks, LANES), jnp.int32)
-    for at, value in enumerate(col_out):
-        if value is not None:
-            full = jnp.where(lanes == at, value, full)
-    slot_col_ref[...] = full
-    eight = lax.broadcasted_iota(jnp.int32, (8, toks), 0)
-    rows = jnp.zeros((8, toks), jnp.int32)
-    for at, value in enumerate(row_out):
-        if value is not None:
-            rows = jnp.where(eight == at, value, rows)
-    slot_row_ref[...] = rows
-
-
-def routing(meta, cols, capacity, slots_each, experts, layers):
-    micros, _, toks = meta.shape
+            at = 2 + 2 * layer + k
+            hot = one_where((cols[:, at : at + 1] == labels) & ok_all)
+            counts = dot_nn(before, hot) + firsts
+            firsts = jnp.sum(hot.astype(F32), axis=0, keepdims=True)
+            named = mine[:, at : at + 1]
+            place = jnp.sum(jnp.where(named == labels, counts, 0.0), axis=1, keepdims=True)
+            slot = jnp.where((place < capacity) & ok_mine, named * slots_each + place, -1.0)
+            full = jnp.where(lanes == 2 * layer + k, slot, full)
+            full = jnp.where(lanes == 4 + 2 * layer + k, named, full)
+    slot_col_ref[...] = full.astype(jnp.int32)
+    fill = up_to(toks, LANES) - toks
+    turned = jnp.concatenate([full, jnp.zeros((fill, LANES), F32)], axis=0).T
+    slot_row_ref[...] = turned[:8, :toks].astype(jnp.int32)
+
+
+def routing(priority, valid, routes, capacity, slots_each, experts, rows):
+    micros, group = priority.shape
+    images = valid.shape[0] // micros
+    layers = routes.shape[0]
+    toks = images * rows
     return pl.pallas_call(
-        functools.partial(routing_kernel, capacity, slots_each, experts, layers),
+        functools.partial(routing_kernel, capacity, slots_each, experts, rows),
         grid=(micros,),
         in_specs=[
-            pl.BlockSpec((None, 8, toks), lambda m: (m, 0, 0)),
-            pl.BlockSpec((None, toks, 8), lambda m: (m, 0, 0)),
+            pl.BlockSpec(priority.shape, lambda m: (0, 0)),
+            pl.BlockSpec(valid.shape, lambda m: (0, 0)),
+            pl.BlockSpec((layers, 2, group), lambda m: (0, 0, m)),
         ],
         out_specs=[
             pl.BlockSpec((None, toks, LANES), lambda m: (m, 0, 0)),
@@ -146,8 +147,9 @@
             jax.ShapeDtypeStruct((micros, 8, toks), jnp.int32),
         ],
         compiler_params=pltpu.CompilerParams(vmem_limit_bytes=VMEM_LIMIT),
+        cost_estimate=cost(5),
         name="routing",
-    )(meta, cols)
+    )(priority, valid, routes)
 
 
 def gates(router, slot_col, layer):
@@ -393,10 +395,10 @@
 
 
 class Shapes:
-    def __init__(self, micros, images, rows, each, width, hidden, experts, slots_each, dense_rows, shards):
+    def __init__(self, micros, images, rows, each, width, hidden, experts, slots_each, dense_rows, shards, groups):
         self.micros, self.images, self.rows, self.each = micros, images, rows, each
         self.width, self.hidden, self.experts, self.slots_each = width, hidden, experts, slots_each
-        self.dense_rows, self.shards = dense_rows, shards
+        self.dense_rows, self.shards, self.groups = dense_rows, shards, groups
         self.toks = images * rows
         self.sizes = (images, rows, experts)
 
@@ -444,7 +446,7 @@
         return self.whole(self.dense_rows, self.width)
 
     def dense_out(self):
-        return self.whole(self.shards, up_to(self.dense_rows // self.shards, 16), self.width)
+        return self.whole(self.shards, up_to(self.dense_rows // self.shards, 4 * self.groups), self.width)
 
     def scratch(self):
         return [
@@ -465,7 +467,7 @@
             self.cols(),
         ]
 
-    def call(self, kernel, ins, outs, args, name, scratch=()):
+    def call(self, kernel, ins, outs, args, name, took, scratch=()):
         return pl.pallas_call(
             kernel,
             grid=(self.micros,),
@@ -474,6 +476,7 @@
             out_shape=[shape for _, shape in outs],
             scratch_shapes=list(scratch),
             compiler_params=pltpu.CompilerParams(vmem_limit_bytes=VMEM_LIMIT),
+            cost_estimate=cost(took),
             name=name,
         )(*args)
 
@@ -485,6 +488,7 @@
         shp.forward_outs(),
         (tokens, dense, cols, rows),
         "attn_first",
+        12,
     )
 
 
@@ -496,6 +500,7 @@
         [shp.picked(), *shp.forward_outs()],
         (back, x1, router, dense, cols, rows),
         "attn_next",
+        16,
     )
 
 
@@ -507,6 +512,7 @@
         [shp.token_block(F32), shp.per_micro(t, w), shp.per_micro(t, LANES), shp.exchange()],
         (back, x1, router, cotangent, cols, rows),
         "turn",
+        8,
         scratch=[pltpu.VMEM((2, t, w), BF16)],
     )
 
@@ -520,6 +526,7 @@
         [shp.per_micro(t, w), shp.per_micro(t, LANES), shp.exchange(), shp.dense_out()],
         (back, dx, dg, router, x, x1, c, o, qkv, a, dense, cols, rows, router_low, picked_low),
         "attn_back",
+        28,
         scratch=shp.scratch(),
     )
 
@@ -532,6 +539,7 @@
         [shp.token_block(F32), shp.dense_out()],
         (back, dx, dg, router, x, x1, c, o, qkv, a, dense, cols),
         "attn_last",
+        25,
         scratch=shp.scratch(),
     )
 
@@ -540,105 +548,6 @@
     cdf = 0.5 * (1.0 + lax.erf(h * INV_SQRT2))
     slope = cdf + h * (INV_SQRT2PI * jnp.exp(-0.5 * (h * h)))
     return (h * cdf).astype(BF16), slope.astype(BF16)
-
-
-def expert_forward_kernel(x_ref, mats_ref, shift_ref, y_ref, act_ref, slope_ref):
-    width, hidden = x_ref.shape[1], mats_ref.shape[1]
-    shift = shift_ref[...].astype(F32)
-    y = None
-    for at in range(0, hidden, 512):
-        cut = slice(at, at + 512)
-        h = dot_nn(x_ref[...], mats_ref[:width, cut]) + shift[:, cut]
-        act, slope = gelu_parts(h)
-        act_ref[:, cut] = act
-        slope_ref[:, cut] = slope
-        piece = dot_nt(act, mats_ref[width:, cut])
-        y = piece if y is None else y + piece
-    y_ref[...] = (y + shift[:, hidden:]).astype(BF16)
-
-
-def expert_forward(x, mats, shift):
-    rows, width = x.shape
-    hidden = mats.shape[1]
-    block = 256
-    return pl.pallas_call(
-        expert_forward_kernel,
-        grid=(rows // block,),
-        in_specs=[
-            pl.BlockSpec((block, width), lambda r: (r, 0)),
-            pl.BlockSpec(mats.shape, lambda r: (0, 0), pipeline_mode=pl.Buffered(1)),
-            pl.BlockSpec(shift.shape, lambda r: (0, 0)),
-        ],
-        out_specs=[
-            pl.BlockSpec((block, width), lambda r: (r, 0)),
-            pl.BlockSpec((block, hidden), lambda r: (r, 0)),
-            pl.BlockSpec((block, hidden), lambda r: (r, 0)),
-        ],
-        out_shape=[
-            jax.ShapeDtypeStruct((rows, width), BF16),
-            jax.ShapeDtypeStruct((rows, hidden), BF16),
-            jax.ShapeDtypeStruct((rows, hidden), BF16),
-        ],
-        compiler_params=pltpu.CompilerParams(vmem_limit_bytes=VMEM_LIMIT),
-        name="expert_forward",
-    )(x, mats, shift)
-
-
-def expert_back_kernel(dy_ref, x_ref, act_ref, slope_ref, w_in_ref, w_out_ref, dx_ref, dw_ref, db_ref, xt_ref, dyt_ref, total_ref):
-    step = pl.program_id(0)
-    width = x_ref.shape[1]
-
-    @pl.when(step == 0)
-    def _():
-        xt_ref[...] = x_ref[...].T
-        dyt_ref[...] = dy_ref[...].T
-        total_ref[...] = jnp.zeros_like(total_ref)
-
-    dh = (dot_nn(dy_ref[...], w_out_ref[...]) * slope_ref[...].astype(F32)).astype(BF16)
-    db_ref[...] = jnp.sum(dh.astype(F32), axis=0, keepdims=True)
-    dw_ref[:width, :] = dot_nn(xt_ref[...], dh).astype(BF16)
-    dw_ref[width:, :] = dot_nn(dyt_ref[...], act_ref[...]).astype(BF16)
-    total_ref[...] += dot_nt(dh, w_in_ref[...])
-
-    @pl.when(step == pl.num_programs(0) - 1)
-    def _():
-        dx_ref[...] = total_ref[...].astype(BF16)
-
-
-def expert_back(dy, x, act, slope, mats):
-    rows, width = x.shape
-    hidden = mats.shape[1]
-    block = 256
-    full = lambda f: (0, 0)
-    return pl.pallas_call(
-        expert_back_kernel,
-        grid=(hidden // block,),
-        in_specs=[
-            pl.BlockSpec((rows, width), full, pipeline_mode=pl.Buffered(1)),
-            pl.BlockSpec((rows, width), full, pipeline_mode=pl.Buffered(1)),
-            pl.BlockSpec((rows, block), lambda f: (0, f)),
-            pl.BlockSpec((rows, block), lambda f: (0, f)),
-            pl.BlockSpec((width, block), lambda f: (0, f)),
-            pl.BlockSpec((width, block), lambda f: (1, f)),
-        ],
-        out_specs=[
-            pl.BlockSpec((rows, width), full, pipeline_mode=pl.Buffered(1)),
-            pl.BlockSpec((2 * width, block), lambda f: (0, f)),
-            pl.BlockSpec((1, block), lambda f: (0, f)),
-        ],
-        out_shape=[
-            jax.ShapeDtypeStruct((rows, width), BF16),
-            jax.ShapeDtypeStruct((2 * width, hidden), BF16),
-            jax.ShapeDtypeStruct((1, hidden), F32),
-        ],
-        scratch_shapes=[
-            pltpu.VMEM((width, rows), BF16),
-            pltpu.VMEM((width, rows), BF16),
-            pltpu.VMEM((rows, width), F32),
-        ],
-        compiler_params=pltpu.CompilerParams(vmem_limit_bytes=VMEM_LIMIT),
-        name="expert_back",
-    )(dy, x, act, slope, mats, mats)
 
 
 def adam_update(master, first_mom, second_mom, gradient, clip_scale, step_float):
@@ -649,6 +558,635 @@
     second_hat = second_new / (1.0 - BETA_TWO**step_float)
     change = -STEP_RATE * (first_hat / (jnp.sqrt(second_hat) + ADAM_EPS) + DECAY_RATE * master)
     return (change, first_new, second_new)
+
+
+class Group:
+    def __init__(self, cube, count):
+        dp, ex = lax.axis_index("dp"), lax.axis_index("expert")
+        self.cube, self.count, self.dp, self.ex = cube, count, dp, ex
+        if cube:
+            self.half, self.x, self.core = lax.div(ex, 4), lax.div(dp, 2), lax.rem(dp, 2)
+            self.mine = lax.rem(self.half + self.x, 2) * 4 + lax.rem(ex, 4)
+        else:
+            self.mine = ex
+
+    def device(self, expert):
+        if self.cube:
+            far = lax.rem(lax.div(expert, 4) + self.half, 2)
+            return {"dp": far * 2 + self.core, "expert": self.half * 4 + lax.rem(expert, 4)}
+        return {"dp": self.dp, "expert": expert}
+
+    def after(self, steps):
+        return lax.rem(self.mine + steps, self.count)
+
+    def held_at(self, quarter):
+        if self.cube:
+            return lax.rem(quarter % 2 + self.core, 2) * 2 + lax.rem(quarter // 2 + self.x, 2)
+        return quarter
+
+
+def meet(devices):
+    barrier = pltpu.get_barrier_semaphore()
+    for device in devices:
+        pl.semaphore_signal(barrier, inc=1, device_id=device, device_id_type=MESH)
+    pl.semaphore_wait(barrier, len(devices))
+
+
+def remote(src, dst, send_sem, recv_sem, device):
+    return pltpu.make_async_remote_copy(
+        src_ref=src, dst_ref=dst, send_sem=send_sem, recv_sem=recv_sem, device_id=device, device_id_type=MESH
+    )
+
+
+def dispatch_start(group, send, landed, ssem, rsem, lsem, micros):
+    n = group.count
+    for m in range(micros):
+        pltpu.make_async_copy(send.at[group.mine, m], landed.at[m, 0], lsem.at[m]).start()
+        for k in range(n - 1, 0, -1):
+            target = group.after(k)
+            remote(send.at[target, m], landed.at[m, n - k], ssem.at[m, k], rsem.at[m, n - k], group.device(target)).start()
+
+
+def dispatch_wait(group, send, landed, ssem, rsem, m, slot):
+    remote(send.at[0, 0], landed.at[m, slot], ssem.at[m, slot], rsem.at[m, slot], group.device(0)).wait_recv()
+
+
+def return_start(group, ready, back, ysem, bsem, osem, m, slot):
+    def away():
+        remote(ready.at[m, slot], back.at[group.mine, m], ysem.at[m, slot], bsem.at[m, group.mine], group.device(group.after(slot))).start()
+
+    if isinstance(slot, int):
+        if slot == 0:
+            pltpu.make_async_copy(ready.at[m, 0], back.at[group.mine, m], osem.at[m]).start()
+        else:
+            away()
+        return
+
+    @pl.when(slot == 0)
+    def _():
+        pltpu.make_async_copy(ready.at[m, 0], back.at[group.mine, m], osem.at[m]).start()
+
+    @pl.when(slot > 0)
+    def _():
+        away()
+
+
+def drain(group, send, landed, ready, back, ssem, rsem, ysem, bsem, osem, micros):
+    n = group.count
+    for m in range(micros):
+        pltpu.make_async_copy(ready.at[m, 0], back.at[group.mine, m], osem.at[m]).wait()
+        for k in range(1, n):
+            there = group.device(0)
+            remote(send.at[0, 0], landed.at[m, k], ssem.at[m, k], rsem.at[m, k], there).wait_send()
+            remote(ready.at[m, k], back.at[0, m], ysem.at[m, k], bsem.at[m, 0], there).wait_send()
+            who = group.after(k)
+            remote(ready.at[m, k], back.at[who, m], ysem.at[m, k], bsem.at[m, who], there).wait_recv()
+
+
+def load_weights(mats, wbuf, wsem):
+    at = 0
+    for i, ref in enumerate(mats):
+        copy = pltpu.make_async_copy(ref, wbuf.at[pl.ds(at, ref.shape[0])], wsem.at[i])
+        at += ref.shape[0]
+        yield copy
+
+
+def served_forward_kernel(cube, count, pieces, *refs):
+    send, mats, (shift_ref, back, act_ref, slope_ref, keep_ref, landed, ready, wbuf, ssem, rsem, ysem, bsem, lsem, osem, wsem) = (
+        refs[0],
+        refs[1 : 1 + pieces],
+        refs[1 + pieces :],
+    )
+    group = Group(cube, count)
+    m, q = pl.program_id(0), pl.program_id(1)
+    micros, chunks = landed.shape[0], count // (act_ref.shape[0] // landed.shape[2])
+    each = count // chunks
+    quarters, _, hidden = wbuf.shape
+    width = landed.shape[3]
+    part = 2 * width // quarters
+
+    @pl.when((m == 0) & (q == 0))
+    def _():
+        for copy in load_weights(mats, wbuf, wsem):
+            copy.start()
+        meet([group.device(group.after(k)) for k in range(1, count)])
+        dispatch_start(group, send, landed, ssem, rsem, lsem, micros)
+        for copy in load_weights(mats, wbuf, wsem):
+            copy.wait()
+
+    for b in range(each):
+        slot = q * each + b
+        if b == 0:
+
+            @pl.when(q == 0)
+            def _():
+                pltpu.make_async_copy(send.at[group.mine, m], landed.at[m, 0], lsem.at[m]).wait()
+
+            @pl.when(q > 0)
+            def _():
+                dispatch_wait(group, send, landed, ssem, rsem, m, slot)
+        else:
+            dispatch_wait(group, send, landed, ssem, rsem, m, slot)
+    x = landed[m, pl.ds(q * each, each)].reshape(act_ref.shape[0], width)
+    keep_ref[...] = x
+    if cube:
+        span = (hidden + width) // quarters
+        shift = jnp.concatenate(
+            [wbuf[group.held_at(i), part:, :span].astype(F32)[0:1] for i in range(quarters)], axis=1
+        )
+    else:
+        shift = shift_ref[...].astype(F32)
+    y = [None] * (quarters // 2)
+    for at in range(0, hidden, 512):
+        cut = slice(at, at + 512)
+        h = None
+        for i in range(quarters // 2):
+            piece = dot_nn(x[:, i * part : (i + 1) * part], wbuf[group.held_at(i), :part, cut])
+            h = piece if h is None else h + piece
+        act, slope = gelu_parts(h + shift[:, cut])
+        act_ref[:, cut] = act
+        slope_ref[:, cut] = slope
+        for i in range(quarters // 2):
+            piece = dot_nt(act, wbuf[group.held_at(quarters // 2 + i), :part, cut])
+            y[i] = piece if y[i] is None else y[i] + piece
+    y = (jnp.concatenate(y, axis=1) + shift[:, hidden:]).astype(BF16)
+    ready[m, pl.ds(q * each, each)] = y.reshape(each, ready.shape[2], width)
+    for b in range(each):
+        if b == 0:
+            return_start(group, ready, back, ysem, bsem, osem, m, q * each)
+        else:
+            slot = q * each + b
+            remote(ready.at[m, slot], back.at[group.mine, m], ysem.at[m, slot], bsem.at[m, group.mine], group.device(group.after(slot))).start()
+
+    @pl.when((m == micros - 1) & (q == chunks - 1))
+    def _():
+        drain(group, send, landed, ready, back, ssem, rsem, ysem, bsem, osem, micros)
+
+
+def any_spec():
+    return pl.BlockSpec(memory_space=pl.ANY)
+
+
+def comm_params(ident):
+    return pltpu.CompilerParams(vmem_limit_bytes=VMEM_LIMIT, collective_id=ident, has_side_effects=True)
+
+
+def exchange_sems(micros, count):
+    table = pltpu.SemaphoreType.DMA((micros, count))
+    return [table] * 4 + [pltpu.SemaphoreType.DMA((micros,))] * 2 + [pltpu.SemaphoreType.DMA((2,))]
+
+
+def served_forward(cube, send, mats, shift):
+    count, micros, slots, width = send.shape
+    chunks = 4
+    rows = count // chunks * slots
+    quarters = sum(x.shape[0] for x in mats)
+    block, hidden = mats[0].shape[1:]
+    row_spec = lambda cols: pl.BlockSpec((None, rows, cols), lambda m, q: (m, q, 0))
+    full = (micros, count * slots)
+    return pl.pallas_call(
+        functools.partial(served_forward_kernel, cube, count, len(mats)),
+        grid=(micros, chunks),
+        in_specs=[any_spec()] * (1 + len(mats)) + [pl.BlockSpec(shift.shape, lambda m, q: (0, 0))],
+        out_specs=[any_spec(), row_spec(hidden), row_spec(hidden), row_spec(width)],
+        out_shape=[
+            jax.ShapeDtypeStruct(send.shape, BF16),
+            jax.ShapeDtypeStruct((*full, hidden), BF16),
+            jax.ShapeDtypeStruct((*full, hidden), BF16),
+            jax.ShapeDtypeStruct((*full, width), BF16),
+        ],
+        scratch_shapes=[
+            pltpu.VMEM((micros, count, slots, width), BF16),
+            pltpu.VMEM((micros, count, slots, width), BF16),
+            pltpu.VMEM((quarters, block, hidden), BF16),
+            *exchange_sems(micros, count),
+        ],
+        compiler_params=comm_params(0),
+        cost_estimate=cost(48),
+        name="served_forward",
+    )(send, *mats, shift)
+
+
+def served_back_kernel(cube, count, pieces, *refs):
+    send, mats, refs = refs[0], refs[1 : 1 + pieces], refs[1 + pieces :]
+    (x_ref, act_ref, slope_ref, back, *dw_refs, landed, ready, wbuf, xt_ref, dyt_ref, total_ref, acc_ref, bias_ref, ssem, rsem, ysem, bsem, lsem, osem, wsem) = refs
+    group = Group(cube, count)
+    m, f = pl.program_id(0), pl.program_id(1)
+    micros, steps = pl.num_programs(0), pl.num_programs(1)
+    total_micros = landed.shape[0]
+    quarters, block, _ = wbuf.shape
+    slots, width = landed.shape[2:]
+    rows = count * slots
+    part = 2 * width // quarters
+    wide = act_ref.shape[1]
+    cut = pl.ds(pl.multiple_of(f * wide, wide), wide)
+
+    @pl.when((m == 0) & (f == 0))
+    def _():
+        for copy in load_weights(mats, wbuf, wsem):
+            copy.start()
+        meet([group.device(group.after(k)) for k in range(1, count)])
+        dispatch_start(group, send, landed, ssem, rsem, lsem, total_micros)
+        for copy in load_weights(mats, wbuf, wsem):
+            copy.wait()
+
+    @pl.when(f == 0)
+    def _():
+        xt_ref[...] = x_ref[...].T
+        pltpu.make_async_copy(send.at[group.mine, m], landed.at[m, 0], lsem.at[m]).wait()
+        for slot in range(1, count):
+            dispatch_wait(group, send, landed, ssem, rsem, m, slot)
+        dyt_ref[...] = landed[m].reshape(rows, width).T
+        total_ref[...] = jnp.zeros_like(total_ref)
+
+    dy = landed[m].reshape(rows, width)
+    dact = None
+    for i in range(quarters // 2):
+        piece = dot_nn(dy[:, i * part : (i + 1) * part], wbuf[group.held_at(quarters // 2 + i), :part, cut])
+        dact = piece if dact is None else dact + piece
+    dh = (dact * slope_ref[...].astype(F32)).astype(BF16)
+    act = act_ref[...]
+    first = m == 0
+    spans = width // wide
+    dy_cut = landed[m, :, :, pl.ds(pl.multiple_of(lax.rem(f, spans) * wide, wide), wide)].reshape(rows, wide)
+    dy_sum = jnp.where(f < spans, jnp.sum(dy_cut.astype(F32), axis=0, keepdims=True), 0.0)
+    bias = jnp.concatenate(
+        [jnp.sum(dh.astype(F32), axis=0, keepdims=True), dy_sum, jnp.zeros((block - part - 2, wide), F32)], axis=0
+    ) + jnp.where(first, 0.0, bias_ref[f])
+    bias_ref[f] = bias
+    for i in range(quarters):
+        left = xt_ref if i < quarters // 2 else dyt_ref
+        at = (i % (quarters // 2)) * part
+        grad = dot_nn(left[at : at + part, :], dh if i < quarters // 2 else act)
+        grad = grad + jnp.where(first, 0.0, acc_ref[f, i])
+        acc_ref[f, i] = grad
+        low = jnp.concatenate([grad, bias], axis=0).astype(BF16)
+        if cube:
+
+            @pl.when(group.core == i % 2)
+            def _():
+                dw_refs[0][i // 2] = low
+
+            @pl.when(group.core != i % 2)
+            def _():
+                dw_refs[1][i // 2] = low
+        else:
+            dw_refs[0][i] = low
+    for i in range(quarters // 2):
+        total_ref[:, i * part : (i + 1) * part] += dot_nt(dh, wbuf[group.held_at(i), :part, cut])
+
+    @pl.when(f == steps - 1)
+    def _():
+        ready[m] = total_ref[...].astype(BF16).reshape(count, slots, width)
+        for slot in range(count):
+            return_start(group, ready, back, ysem, bsem, osem, m, slot)
+
+    @pl.when((m == micros - 1) & (f == steps - 1))
+    def _():
+        drain(group, send, landed, ready, back, ssem, rsem, ysem, bsem, osem, total_micros)
+
+
+def served_back(cube, send, mats, x, act, slope):
+    count, micros, slots, width = send.shape
+    rows = count * slots
+    quarters = sum(v.shape[0] for v in mats)
+    block, hidden = mats[0].shape[1:]
+    part = 2 * width // quarters
+    wide = 256
+    steps = hidden // wide
+    outs = 2 if cube else 1
+    col_spec = pl.BlockSpec((None, rows, wide), lambda m, f: (m, 0, f))
+    return pl.pallas_call(
+        functools.partial(served_back_kernel, cube, count, len(mats)),
+        grid=(micros, steps),
+        in_specs=[any_spec()] * (1 + len(mats)) + [pl.BlockSpec((None, rows, width), lambda m, f: (m, 0, 0)), col_spec, col_spec],
+        out_specs=[any_spec()] + [pl.BlockSpec((quarters // outs, block, wide), lambda m, f: (0, 0, lax.div(m, micros - 1) * f if micros > 1 else f))] * outs,
+        out_shape=[jax.ShapeDtypeStruct(send.shape, BF16)] + [jax.ShapeDtypeStruct((quarters // outs, block, hidden), BF16)] * outs,
+        scratch_shapes=[
+            pltpu.VMEM((micros, count, slots, width), BF16),
+            pltpu.VMEM((micros, count, slots, width), BF16),
+            pltpu.VMEM((quarters, block, hidden), BF16),
+            pltpu.VMEM((width, rows), BF16),
+            pltpu.VMEM((width, rows), BF16),
+            pltpu.VMEM((rows, width), F32),
+            pltpu.VMEM((steps, quarters, part, wide), F32),
+            pltpu.VMEM((steps, block - part, wide), F32),
+            *exchange_sems(micros, count),
+        ],
+        compiler_params=comm_params(1),
+        cost_estimate=cost(60),
+        name="served_back",
+    )(send, *mats, x, act, slope)
+
+
+def dense_sum_kernel(shards, groups, g_ref, out_ref, landed, part_ref, total_ref, spread, s1, r1, s2, r2, s3, r3):
+    dp, ex = lax.axis_index("dp"), lax.axis_index("expert")
+    rows = part_ref.shape[0]
+    each = rows * 4 // groups
+    line = [{"dp": dp, "expert": lax.rem(ex + k, groups)} for k in range(1, groups)]
+    if shards == 4:
+        x, core = lax.div(dp, 2), lax.rem(dp, 2)
+        near, far = {"dp": x * 2 + 1 - core, "expert": ex}, {"dp": (1 - x) * 2 + core, "expert": ex}
+        meet([near, far] + line)
+        copies = []
+        for k in range(2):
+            copy = remote(g_ref.at[k * 2 + 1 - core], landed.at[k], s1.at[k], r1.at[k], near)
+            copy.start()
+            copies.append(copy)
+        for copy in copies:
+            copy.wait()
+        landed[3] = (g_ref[(1 - x) * 2 + core].astype(F32) + landed[1 - x].astype(F32)).astype(BF16)
+        copy = remote(landed.at[3], landed.at[2], s1.at[2], r1.at[2], far)
+        copy.start()
+        total = g_ref[x * 2 + core].astype(F32) + landed[x].astype(F32)
+        copy.wait()
+        part_ref[...] = (total + landed[2].astype(F32)).astype(BF16)
+    else:
+        column = [{"dp": lax.rem(dp + k, shards), "expert": ex} for k in range(1, shards)]
+        meet(column + line)
+        copies = []
+        for k in range(1, shards):
+            copy = remote(g_ref.at[lax.rem(dp + k, shards)], landed.at[shards - k], s1.at[k], r1.at[shards - k], column[k - 1])
+            copy.start()
+            copies.append(copy)
+        for copy in copies:
+            copy.wait()
+        total = g_ref[dp].astype(F32)
+        for k in range(1, shards):
+            total = total + landed[k].astype(F32)
+        part_ref[...] = total.astype(BF16)
+
+    def piece(ref, j):
+        if groups >= 4:
+            span = groups // 4
+            return ref.at[pl.ds(pl.multiple_of(lax.rem(j, span) * each, 16), each), pl.ds(pl.multiple_of(lax.div(j, span) * LANES, LANES), LANES)]
+        raise ValueError("groups")
+
+    copies = []
+    for k in range(1, groups):
+        copy = remote(piece(part_ref, lax.rem(ex + k, groups)), spread.at[groups - k], s2.at[k], r2.at[groups - k], line[k - 1])
+        copy.start()
+        copies.append(copy)
+    span = groups // 4
+    mine_rows = pl.ds(pl.multiple_of(lax.rem(ex, span) * each, 16), each)
+    mine_cols = pl.ds(pl.multiple_of(lax.div(ex, span) * LANES, LANES), LANES)
+    mine = part_ref[mine_rows, mine_cols].astype(F32)
+    for copy in copies:
+        copy.wait()
+    for k in range(1, groups):
+        mine = mine + spread[k].astype(F32)
+    total_ref[...] = mine.astype(BF16)
+    copies = []
+    for k in range(1, groups):
+        copy = remote(total_ref, piece(out_ref, ex), s3.at[k], r3.at[groups - k], line[k - 1])
+        copy.start()
+        copies.append(copy)
+    out_ref[mine_rows, mine_cols] = total_ref[...]
+    for copy in copies:
+        copy.wait()
+
+
+def dense_sum(grad, groups):
+    shards, rows, width = grad.shape
+    each = rows * 4 // groups
+    vmem = pl.BlockSpec(memory_space=pltpu.VMEM)
+    return pl.pallas_call(
+        functools.partial(dense_sum_kernel, shards, groups),
+        in_specs=[vmem],
+        out_specs=vmem,
+        out_shape=jax.ShapeDtypeStruct((rows, width), BF16),
+        scratch_shapes=[
+            pltpu.VMEM((shards, rows, width), BF16),
+            pltpu.VMEM((rows, width), BF16),
+            pltpu.VMEM((each, LANES), BF16),
+            pltpu.VMEM((groups, each, LANES), BF16),
+            pltpu.SemaphoreType.DMA((shards,)),
+            pltpu.SemaphoreType.DMA((shards,)),
+            pltpu.SemaphoreType.DMA((groups,)),
+            pltpu.SemaphoreType.DMA((groups,)),
+            pltpu.SemaphoreType.DMA((groups,)),
+            pltpu.SemaphoreType.DMA((groups,)),
+        ],
+        compiler_params=comm_params(2),
+        cost_estimate=cost(50),
+        name="dense_sum",
+    )(grad)
+
+
+def scalar_sum_kernel(shards, groups, x_ref, out_ref, near, line_total, far, s1, r1, s2, r2):
+    dp, ex = lax.axis_index("dp"), lax.axis_index("expert")
+    column = [{"dp": lax.rem(dp + k, shards), "expert": ex} for k in range(1, shards)]
+    line = [{"dp": dp, "expert": lax.rem(ex + k, groups)} for k in range(1, groups)]
+    meet(column + line)
+    copies = []
+    for k in range(1, groups):
+        copy = remote(x_ref, near.at[ex], s1.at[k], r1.at[ex], line[k - 1])
+        copy.start()
+        copies.append(copy)
+    near[ex] = x_ref[...]
+    for k in range(1, groups):
+        copies[k - 1].wait_send()
+        who = lax.rem(ex + k, groups)
+        remote(x_ref, near.at[who], s1.at[k], r1.at[who], line[k - 1]).wait_recv()
+    total = near[0]
+    for j in range(1, groups):
+        total = total + near[j]
+    line_total[...] = total
+    copies = []
+    for k in range(1, shards):
+        copy = remote(line_total, far.at[dp], s2.at[k], r2.at[dp], column[k - 1])
+        copy.start()
+        copies.append(copy)
+    far[dp] = total
+    for k in range(1, shards):
+        copies[k - 1].wait_send()
+        who = lax.rem(dp + k, shards)
+        remote(line_total, far.at[who], s2.at[k], r2.at[who], column[k - 1]).wait_recv()
+    total = far[0]
+    for j in range(1, shards):
+        total = total + far[j]
+    out_ref[...] = jnp.broadcast_to(jnp.sum(total, keepdims=True), total.shape)
+
+
+def scalar_sum(value, shards, groups):
+    tile = (8, LANES)
+    vmem = pl.BlockSpec(memory_space=pltpu.VMEM)
+    return pl.pallas_call(
+        functools.partial(scalar_sum_kernel, shards, groups),
+        in_specs=[vmem],
+        out_specs=vmem,
+        out_shape=jax.ShapeDtypeStruct(tile, F32),
+        scratch_shapes=[
+            pltpu.VMEM((groups, *tile), F32),
+            pltpu.VMEM(tile, F32),
+            pltpu.VMEM((shards, *tile), F32),
+            pltpu.SemaphoreType.DMA((groups,)),
+            pltpu.SemaphoreType.DMA((groups,)),
+            pltpu.SemaphoreType.DMA((shards,)),
+            pltpu.SemaphoreType.DMA((shards,)),
+        ],
+        compiler_params=comm_params(3),
+        cost_estimate=cost(10),
+        name="scalar_sum",
+    )(value)[0, 0]
+
+
+def shifted(values, move):
+    shards, groups = lax.axis_size("dp"), lax.axis_size("expert")
+    pairs = []
+    for d in range(shards):
+        for e in range(groups):
+            to = {"z": (d, (e + 4) % 8), "x": ((d + 2) % 4, e), "core": (d ^ 1, e)}[move]
+            pairs.append((d * groups + e, to[0] * groups + to[1]))
+    return lax.ppermute(values, ("dp", "expert"), pairs)
+
+
+def on_first_x():
+    return lax.div(lax.axis_index("dp"), 2) == 0
+
+
+def x_turn(rows, partner):
+    return jnp.where(on_first_x(), partner, rows)
+
+
+def pair_up(rows, partner, far):
+    return jnp.stack([jnp.where(on_first_x(), rows, partner), far])
+
+
+def together(*values):
+    return lax.optimization_barrier(values)
+
+
+def dense_gather_kernel(low_ref, *refs):
+    outs, (landed, wide_ref, own_sem, send_sem, recv_sem) = refs[: low_ref.shape[0]], refs[low_ref.shape[0] :]
+    dp, ex = lax.axis_index("dp"), lax.axis_index("expert")
+    x, core = lax.div(dp, 2), lax.rem(dp, 2)
+    near, far = {"dp": x * 2 + 1 - core, "expert": ex}, {"dp": (1 - x) * 2 + core, "expert": ex}
+    layers, rows, _ = low_ref.shape
+    meet([near, far])
+    own, across, beside, passed = [], [], [], []
+    for i in range(layers):
+        across.append(remote(low_ref.at[i], landed.at[i, 1], send_sem.at[i, 1], recv_sem.at[i, 1], far))
+        across[i].start()
+        beside.append(remote(low_ref.at[i], landed.at[i, 2], send_sem.at[i, 2], recv_sem.at[i, 2], near))
+        beside[i].start()
+        own.append(pltpu.make_async_copy(low_ref.at[i], landed.at[i, 0], own_sem.at[i]))
+        own[i].start()
+    for i in range(layers):
+        across[i].wait()
+        passed.append(remote(landed.at[i, 1], landed.at[i, 3], send_sem.at[i, 3], recv_sem.at[i, 3], near))
+        passed[i].start()
+        own[i].wait()
+        beside[i].wait()
+        passed[i].wait()
+        for s in range(4):
+            spot = lax.rem(s // 2 + x, 2) + 2 * lax.rem(s % 2 + core, 2)
+            wide_ref[s * rows : (s + 1) * rows, :] = landed[i, spot].astype(F32)
+        outs[i][...] = wide_ref[...].astype(BF16)
+
+
+def dense_gather(low):
+    layers, rows, width = low.shape
+    vmem = pl.BlockSpec(memory_space=pltpu.VMEM)
+    return pl.pallas_call(
+        dense_gather_kernel,
+        in_specs=[vmem],
+        out_specs=[vmem] * layers,
+        out_shape=[jax.ShapeDtypeStruct((4 * rows, width), BF16)] * layers,
+        scratch_shapes=[
+            pltpu.VMEM((layers, 4, rows, width), BF16),
+            pltpu.VMEM((4 * rows, width), F32),
+            pltpu.SemaphoreType.DMA((layers,)),
+            pltpu.SemaphoreType.DMA((layers, 4)),
+            pltpu.SemaphoreType.DMA((layers, 4)),
+        ],
+        compiler_params=comm_params(4),
+        cost_estimate=cost(30),
+        name="dense_gather",
+    )(low)
+
+
+def pack_kernel(master_ref, shift_ref, out_ref):
+    part, hidden = master_ref.shape
+    rows = out_ref.shape[0] - part
+    span = shift_ref.shape[1]
+    out_ref[:part, :] = master_ref[...].astype(BF16)
+    wide = jnp.concatenate([shift_ref[...], jnp.zeros((1, hidden - span), F32)], axis=1)
+    subs = lax.broadcasted_iota(jnp.int32, (rows, hidden), 0)
+    out_ref[part:, :] = jnp.where(subs == 0, wide, 0.0).astype(BF16)
+
+
+def pack(master, shift, layer, rows):
+    part, hidden = master.shape[2:]
+    span = shift.shape[2]
+    return pl.pallas_call(
+        pack_kernel,
+        grid=(1,),
+        in_specs=[
+            pl.BlockSpec((None, None, part, hidden), lambda g: (layer, 0, 0, 0)),
+            pl.BlockSpec((None, 1, span), lambda g: (layer, 0, 0)),
+        ],
+        out_specs=pl.BlockSpec((rows, hidden), lambda g: (0, 0)),
+        out_shape=jax.ShapeDtypeStruct((rows, hidden), BF16),
+        compiler_params=pltpu.CompilerParams(vmem_limit_bytes=VMEM_LIMIT),
+        cost_estimate=cost(3),
+        name="pack",
+    )(master, shift)
+
+
+def tile_square(values):
+    rows, cols = values.shape
+    folded = jnp.sum((values * values).reshape(rows // 8, 8, cols), axis=0)
+    total = folded[:, :LANES]
+    for at in range(LANES, cols, LANES):
+        total = total + folded[:, at : at + LANES]
+    return total
+
+
+def finish_kernel(layers, width, *refs):
+    nears, lasts, sums = refs[:layers], refs[layers : 2 * layers], refs[2 * layers : 3 * layers]
+    grad_ref, shift_ref, square_ref = refs[3 * layers :]
+    dp, ex = lax.axis_index("dp"), lax.axis_index("expert")
+    part = grad_ref.shape[2]
+    span = shift_ref.shape[2]
+    total = jnp.zeros((8, LANES), F32)
+    subs = lax.broadcasted_iota(jnp.int32, (8, span), 0)
+    for i in range(layers):
+        grad = nears[i][...] + lasts[i][...].astype(F32)
+        grad_ref[i, 0] = grad[:part]
+        total = total + tile_square(grad[:part])
+        full = jnp.concatenate([grad[part : part + 1], grad[part + 1 : part + 2, :width]], axis=1)
+        mine = jnp.zeros((1, span), F32)
+        for q in range(full.shape[1] // span):
+            mine = jnp.where(dp == q, full[:, q * span : (q + 1) * span], mine)
+        shift_ref[i] = mine
+        total = total + tile_square(jnp.where(subs == 0, mine, 0.0))
+        dense = sums[i][...].astype(F32)
+        total = total + jnp.where(ex == 0, tile_square(dense), 0.0)
+    square_ref[...] = total
+
+
+def finish(pieces, sums, shards, part, span, width):
+    layers = len(pieces)
+    hidden = pieces[0][0].shape[1]
+    vmem = pl.BlockSpec(memory_space=pltpu.VMEM)
+    return pl.pallas_call(
+        functools.partial(finish_kernel, layers, width),
+        in_specs=[vmem] * (3 * layers),
+        out_specs=[vmem] * 3,
+        out_shape=[
+            jax.ShapeDtypeStruct((layers, 1, part, hidden), F32),
+            jax.ShapeDtypeStruct((layers, 1, span), F32),
+            jax.ShapeDtypeStruct((8, LANES), F32),
+        ],
+        compiler_params=pltpu.CompilerParams(vmem_limit_bytes=VMEM_LIMIT),
+        cost_estimate=cost(5),
+        name="finish",
+    )(*[near for near, _ in pieces], *[last for _, last in pieces], *sums)
+
+
+def served_shift(served, part, span):
+    return jnp.concatenate([v[:, part, :span] for v in served]).reshape(1, -1)
 
 
 def local(
@@ -679,30 +1217,33 @@
     capacity = (9 * images * PATCHES + 4 * experts - 1) // (4 * experts)
     slots_each = up_to(capacity, 16)
     rows = up_to(PATCHES, 16)
-    shp = Shapes(micros, images, rows, each, width, hidden, experts, slots_each, shard_rows * shards, shards)
-
-    dense_low = dense_master.astype(BF16)
-    dense = [lax.all_gather(dense_low[i], "dp", axis=0, tiled=True) for i in range(layer_count)]
-    expert_low = expert_master.astype(BF16)
-    shift_low = shift_master.astype(BF16)
-    mats = [lax.all_gather(expert_low[i, 0], "dp", axis=0, tiled=True) for i in range(layer_count)]
-    shift = lax.all_gather(shift_low, "dp", axis=2, tiled=True)
-
-    def cut(values):
-        return values.reshape(micros, images, each)[:, :, :rows].reshape(micros, images * rows)
-
-    planes = [cut(priority), cut(valid)]
-    for i in range(layer_count):
-        planes += [cut(routes[i, :, 0]), cut(routes[i, :, 1])]
-    planes += [jnp.zeros_like(planes[0])] * (8 - len(planes))
-    meta = jnp.stack(planes, axis=1)
-    slot_col, slot_row = routing(meta, jnp.swapaxes(meta, 1, 2), capacity, slots_each, experts, layer_count)
-
-    def exchange(values):
-        return lax.all_to_all(values, "expert", split_axis=0, concat_axis=0, tiled=True)
-
-    flat = (experts * micros * slots_each, width)
-    saved, kept, picks = [], [], []
+    shp = Shapes(micros, images, rows, each, width, hidden, experts, slots_each, shard_rows * shards, shards, groups)
+
+    cube = shards == 4 and groups == 8
+    part, span = expert_master.shape[2], shift_master.shape[2]
+    row_block = up_to(part + 2, 16)
+
+    def owned_rows(i):
+        extra = jnp.pad(shift_master[i], ((0, row_block - part - 1), (0, hidden - span)))
+        return jnp.concatenate([expert_master[i, 0], extra], axis=0).astype(BF16)
+
+    own = [pack(expert_master, shift_master, i, row_block) if cube else owned_rows(i) for i in range(layer_count)]
+    dense_low = jnp.stack([dense_master[i].astype(BF16) for i in range(layer_count)])
+    slot_col, slot_row = routing(
+        priority, valid, jnp.swapaxes(routes, 1, 2), capacity, slots_each, experts, rows
+    )
+    if cube:
+        partner = shifted(own[0], "z")
+        dense = dense_gather(dense_low)
+        tokens, slot_col, crossing = together(tokens, slot_col, x_turn(own[0], partner))
+        far = shifted(crossing, "x")
+        later, _ = together(own[1], crossing)
+        partners = [partner, shifted(later, "z")]
+    else:
+        dense = [lax.all_gather(dense_low[i], "dp", axis=0, tiled=True) for i in range(layer_count)]
+        mats = [(lax.all_gather(own[i], "dp", axis=0),) for i in range(layer_count)]
+
+    saved, kept, picks, mats_in = [], [], [], []
     for i in range(layer_count):
         if i == 0:
             outs = first_stage(shp, tokens, dense[0], slot_col, slot_row)
@@ -711,49 +1252,87 @@
             picks.append(picked)
         *state, send = outs
         saved.append(state)
-        received = exchange(send).reshape(flat)
-        produced, act, slope = expert_forward(received, mats[i], shift[i])
+        if cube:
+            if i:
+                pair = pair_up(own[i], partners[i], far)
+            else:
+                pair = pair_up(own[0], partner, far)
+            pair, send = together(pair, send)
+            served = (pair, shifted(pair, "core"))
+            mats_in.append(served)
+        else:
+            mats_in.append(mats[i])
+        shift = jnp.zeros((8, LANES), BF16) if cube else served_shift(mats_in[i], part, span)
+        back, act, slope, received = served_forward(cube, send, mats_in[i], shift)
+        if cube and i + 1 < layer_count:
+            partners[i + 1], back = together(partners[i + 1], back)
+            crossing = x_turn(own[i + 1], partners[i + 1])
+            far = shifted(crossing, "x")
         kept.append((received, act, slope))
-        back = exchange(produced.reshape(send.shape))
     top = layer_count - 1
     output, dx, dg, send = turn_stage(shp, top, back, saved[top][4], saved[top][6], cotangent, slot_col, slot_row)
-    dense_grads, mats_grads, shift_grads = [None] * layer_count, [None] * layer_count, [None] * layer_count
+    dense_grads, mats_grads = [None] * layer_count, [None] * layer_count
     for i in reversed(range(layer_count)):
         received, act, slope = kept[i]
-        dy = exchange(send).reshape(flat)
-        dsent, dmats, dshift_in = expert_back(dy, received, act, slope, mats[i])
-        mats_grads[i] = dmats
-        shift_grads[i] = jnp.concatenate([dshift_in[0], jnp.sum(dy, axis=0, dtype=F32)])
-        back = exchange(dsent.reshape(send.shape))
+        back, grads, *others = served_back(cube, send, mats_in[i], received, act, slope)
+        if not cube:
+            mats_grads[i] = lax.psum_scatter(grads, "dp", scatter_dimension=0, tiled=False)
+        beside = shifted(others[0], "core") if cube else None
         if i:
             dx, dg, send, dense_grads[i] = back_stage(
                 shp, i, back, dx, dg, saved[i], dense[i], slot_col, slot_row, saved[i - 1][6], picks[i - 1]
             )
+            if cube:
+                near_pair = grads.astype(F32) + beside.astype(F32)
+                crossing, send = together(jnp.where(on_first_x(), near_pair[1], near_pair[0]).astype(BF16), send)
+                far = shifted(crossing, "x")
+                waiting = (near_pair, far)
         else:
+            if cube:
+                upper_pair, upper_far = waiting
+                onward = jnp.where(on_first_x(), upper_far, upper_pair[1].astype(BF16))
+                near_pair = grads.astype(F32) + beside.astype(F32)
+                crossing = jnp.where(on_first_x(), near_pair[1], near_pair[0]).astype(BF16)
+                onward, crossing, back = together(onward, crossing, back)
+                upper_last = shifted(onward, "z")
+                mats_grads[1] = (jnp.where(on_first_x(), upper_pair[0], upper_far.astype(F32)), upper_last)
+                far = shifted(crossing, "x")
             grad_tokens, dense_grads[i] = last_stage(shp, back, dx, dg, saved[i], dense[i], slot_col)
-    dense_parts_sum = [
-        lax.psum(lax.psum_scatter(g, "dp", scatter_dimension=0, tiled=False), "expert") for g in dense_grads
-    ]
-    dense_shard = jnp.stack([g[:shard_rows] for g in dense_parts_sum]).astype(F32)
-    expert_shard = jnp.stack(
-        [lax.psum_scatter(g, "dp", scatter_dimension=0, tiled=True) for g in mats_grads]
-    ).astype(F32)[:, None]
-    shift_shard = lax.psum_scatter(
-        jnp.stack(shift_grads)[:, None].astype(BF16), "dp", scatter_dimension=2, tiled=True
-    ).astype(F32)
-    first_replica = (lax.axis_index("expert") == 0).astype(F32)
-    square = (
-        jnp.sum(dense_shard * dense_shard) * first_replica
-        + jnp.sum(expert_shard * expert_shard)
-        + jnp.sum(shift_shard * shift_shard)
-    )
-    grad_norm = jnp.sqrt(lax.psum(square, ("dp", "expert")))
+            if cube:
+                onward, dense_grads[i] = together(jnp.where(on_first_x(), far, near_pair[1].astype(BF16)), dense_grads[i])
+                mats_grads[0] = (jnp.where(on_first_x(), near_pair[0], far.astype(F32)), shifted(onward, "z"))
+    dense_sums = []
+    for i in range(layer_count):
+        if i:
+            dense_sums.append(lax.psum(lax.psum_scatter(dense_grads[i], "dp", scatter_dimension=0, tiled=False), "expert"))
+        else:
+            dense_sums.append(dense_sum(dense_grads[i], groups))
+    fold = lambda v: v.reshape(layer_count, shard_rows, width // LANES, LANES).transpose(1, 2, 0, 3).reshape(-1, LANES)
+    unfold = lambda v: v.reshape(shard_rows, width // LANES, layer_count, LANES).transpose(2, 0, 1, 3).reshape(layer_count, shard_rows, width)
+    dense_shard = fold(jnp.stack([g[:shard_rows] for g in dense_sums]).astype(F32))
+    if cube:
+        expert_shard, shift_shard, square = finish(mats_grads, dense_sums, shards, part, span, width)
+    else:
+        owned = [g.astype(F32) for g in mats_grads]
+        expert_shard = jnp.stack([g[:part] for g in owned])[:, None]
+        shift_shard = jnp.stack(
+            [lax.dynamic_slice(jnp.concatenate([g[part], g[part + 1, :width]]), (lax.axis_index("dp") * span,), (span,)) for g in owned]
+        )[:, None]
+        first_replica = (lax.axis_index("expert") == 0).astype(F32)
+        square = (
+            jnp.sum(dense_shard * dense_shard) * first_replica
+            + jnp.sum(expert_shard * expert_shard)
+            + jnp.sum(shift_shard * shift_shard)
+        )
+        square = jnp.zeros((8, LANES), F32).at[0, 0].set(square)
+    grad_norm = jnp.sqrt(scalar_sum(square, shards, groups))
     clip_scale = CLIP_NORM / jnp.maximum(grad_norm, CLIP_NORM)
     step_float = step.astype(F32)
-    dense_new = adam_update(dense_master, dense_first, dense_second, dense_shard, clip_scale, step_float)
+    dense_new = adam_update(fold(dense_master), fold(dense_first), fold(dense_second), dense_shard, clip_scale, step_float)
+    dense_new = [unfold(values) for values in dense_new]
     expert_new = adam_update(expert_master, expert_first, expert_second, expert_shard, clip_scale, step_float)
     shift_new = adam_update(shift_master, shift_first, shift_second, shift_shard, clip_scale, step_float)
-    return (output, grad_tokens, grad_norm, dense_shard, *dense_new, expert_shard, *expert_new, shift_shard, *shift_new)
+    return (output, grad_tokens, grad_norm, unfold(dense_shard), *dense_new, expert_shard, *expert_new, shift_shard, *shift_new)
 
 
 def solution(mesh):

time: 927 us -> 742 us (0.80)
  Pallas kernels: 186 us -> 536 us
  waiting for transfers between devices: 387 us -> 106 us
  blocking collectives: 231 us -> 0 us
  local copies, waits for them, and re-layouts: 52.6 us -> 25.6 us
  other arithmetic: 24.3 us -> 34.9 us
    pallas_call x4 -> x10, Pallas kernels: 91 us -> 440 us  [the longest x2 195 us: served_back(): pl.pallas_call(functools.partial(served_back_kernel, cube, count, len(mat...]
    all_to_all x4 -> x0, blocking collectives: 186 us -> none  [exchange(): lax.all_to_all(values, 'expert', split_axis=0, concat_axis=0, tiled=True)]
    all_to_all x4 -> x0, waiting for transfers between devices: 150 us -> none  [exchange(): lax.all_to_all(values, 'expert', split_axis=0, concat_axis=0, tiled=True)]
    reduce_scatter x4 -> x1, waiting for transfers between devices: 102 us -> 0.01 us  [local(): lax.psum_scatter(dense_grads[i], 'dp', scatter_dimension=0, tiled=False)]
    psum x1 -> x0, blocking collectives: 39.8 us -> none  [local(): grad_norm = jnp.sqrt(lax.psum(square, ('dp', 'expert')))]
    ppermute x0 -> x12, waiting for transfers between devices: none -> 35.4 us  [shifted(): return lax.ppermute(values, ('dp', 'expert'), pairs)]
    all_gather x4 -> x0, waiting for transfers between devices: 30.5 us -> none  [the longest x2 22.5 us: local(): lax.all_gather(dense_low[i], 'dp', axis=0, tiled=True)]
    unnamed x11 -> x2, waiting for transfers between devices: 28 us -> 0.03 us
  transfers between devices with their start and end apart: 14 -> 14, of which waited for: 11 -> 6; matrix products, arithmetic and copies ran while one was open for 5% -> 4% of each run, Pallas kernels for 11% -> 51%
where the time goes in v2:
time: 742 us; the launch traced here: 733 us
  Pallas kernels  536 us (72%)
  waiting for transfers between devices  106 us (14%)
  other arithmetic  34.9 us (5%)
  local copies, waits for them, and re-layouts  25.6 us (3%)
  between operations  17.4 us (2%)
  starting transfers between devices  12.7 us (2%)
    pallas_call x2, Pallas kernels, served_back(): pl.pallas_call(functools.partial(served_back_kernel, cube, count, len(mat...  195 us
    pallas_call x2, Pallas kernels, served_forward(): pl.pallas_call(functools.partial(served_forward_kernel, cube, count, len(...  117 us
    pallas_call x5, Pallas kernels, call(): pl.pallas_call(kernel, grid=(self.micros,), in_specs=[spec for spec, _ in...  88.4 us
    psum x1, waiting for transfers between devices, local(): lax.psum(lax.psum_scatter(dense_grads[i], 'dp', scatter_dimension=0, tile...  70.9 us
    pallas_call x1, Pallas kernels, dense_sum(): pl.pallas_call(functools.partial(dense_sum_kernel, shards, groups), in_sp...  69.8 us
    ppermute x12, waiting for transfers between devices, shifted(): return lax.ppermute(values, ('dp', 'expert'), pairs)  35.4 us
    pallas_call x1, Pallas kernels, dense_gather(): pl.pallas_call(dense_gather_kernel, in_specs=[vmem], out_specs=[vmem] * l...  30.6 us
    unnamed x46, local copies, waits for them, and re-layouts  20.5 us
  transfers between devices with their start and end apart: 14, of which 6 were waited for; matrix products, arithmetic and copies ran while one was open for 4% of the time, Pallas kernels for 51%

profile of v2, /device:TPU:0, one launch (start us, length us, event | category | flops | bytes accessed | tf_op | source)
XLA Modules:
  0.0 732.7 jit_solution(2532351446679614672)
XLA Ops:
  7.2 2.8 pack.3
  10.1 4.1 collective-permute-start
  14.1 0.7 convert.4
  14.9 1.1 copy.38.low_ref
  16.0 30.6 %dense_gather.1 = (bf16[2064,512]{1,0:T(8,128)(2,1)}, bf16[2064,512]{1,0:T(8,128)(2,1)}) custom-call(bf16[2,516,512]{2,1,0:T(8,128)(2,1)} %copy.38.low_ref), custom_call_target="tpu_custom_call" | custom-call | flops 30000001024 | bytes 90000000 | tf_op jit(solution)/shard_map/dense_gather/pallas_call | solution.py:1091
  46.7 7.7 %routing.1 = (s32[2,416,128]{2,1,0:T(8,128)}, s32[2,8,416]{2,1,0:T(8,128)}) custom-call(s32[2,512]{1,0:T(2,128)} %priority_ref.1, s32[4,256]{1,0:T(4,128)} %valid_ref.1, s32[2,2,1024]{2,1,0:T(2,128)} %bitcast.44), custom_call_target="tpu_custom_call" | custom-call | flops 5000000000 | bytes 15000000 | tf_op jit(solution)/shard_map/routing/pallas_call | solution.py:133
  54.4 8.4 %collective-permute-done = bf16[272,2048]{1,0:T(8,128)(2,1)S(1)} collective-permute-done((bf16[272,2048]{1,0:T(8,128)(2,1)}, bf16[272,2048]{1,0:T(8,128)(2,1)S(1)}, u32[]{:S(2)}, u32[]{:S(2)}) %collective-permute-start) | collective-permute-done | bytes 1114144 | tf_op jit(solution)/shard_map/ppermute | solution.py:1041
  62.8 1.1 select_bitcast_fusion.1
  63.9 1.5 collective-permute-start.2
  65.5 11.9 %attn_first.1 = (f32[2,416,512]{2,1,0:T(8,128)}, bf16[2,416,1536]{2,1,0:T(8,128)(2,1)}, bf16[2,416,512]{2,1,0:T(8,128)(2,1)}, bf16[2,416,512]{2,1,0:T(8,128)(2,1...) custom-call(bf16[1024,512]{1,0:T(8,128)(2,1)} %tok_ref, ...), custom_call_target="tpu_custom_call" | custom-call | flops 12000000000 | bytes 36000000 | tf_op jit(solution)/shard_map/attn_first/pallas_call | solution.py:471
  77.3 12.5 %collective-permute-done.2 = bf16[272,2048]{1,0:T(8,128)(2,1)S(1)} collective-permute-done((bf16[272,2048]{1,0:T(8,128)(2,1)}, bf16[272,2048]{1,0:T(8,128)(2,1)S(1)}, u32[]{:S(2)}, u32[]{:S(2)}) %collective-permute-start.2) | collective-permute-done | bytes 1114144 | tf_op jit(solution)/shard_map/ppermute | solution.py:1041
  89.9 1.0 copy-done.16
  90.9 1.5 pad_maximum_fusion.refs_1_
  92.3 0.1 collective-permute-start.3
  92.4 3.4 pack.2
  95.8 1.0 collective-permute-done.3.refs_2_
  96.9 0.6 broadcast_7_refs_3_.2.refs_3_
  97.4 69.7 %served_forward.2 = (bf16[8,2,112,512]{3,2,1,0:T(8,128)(2,1)}, bf16[2,896,2048]{2,1,0:T(8,128)(2,1)}, bf16[2,896,2048]{2,1,0:T(8,128)(2,1)}, bf16[2,896,512]{2,1,0:T(8,128)(2,1)}) custom-call(bf16[8,2,112,512]{3,2,1,0:T(8,128)(2,1)} %get-tuple-element.88.refs_0_, bf16[2,272,2048]{2,1,0:T(8,128)(2,1)} %copy-done.8, ...), custom_call_target="tpu_custom_call" | custom-call | flops 48000000000 | bytes 144000000 | tf_op jit(solution)/shard_map/served_forward/pallas_call | solution.py:747
  167.2 1.0 copy-done.15
  168.2 1.4 select_bitcast_fusion
  169.6 1.6 collective-permute-start.4
  171.1 15.9 %attn_next.1 = (bf16[2,2,416,512]{3,2,1,0:T(8,128)(2,1)}, f32[2,416,512]{2,1,0:T(8,128)}, bf16[2,416,1536]{2,1,0:T(8,128)(2,1)}, bf16[2,416,512]{2,1,0:T(8,128)(...) custom-call(bf16[8,2,112,512]{3,2,1,0:T(8,128)(2,1)} %get-tuple-elem, ...), custom_call_target="tpu_custom_call" | custom-call | flops 16000000000 | bytes 48000000 | tf_op jit(solution)/shard_map/attn_next/pallas_call | solution.py:471
  187.1 8.9 %collective-permute-done.4 = bf16[272,2048]{1,0:T(8,128)(2,1)S(1)} collective-permute-done((bf16[272,2048]{1,0:T(8,128)(2,1)S(1)}, bf16[272,2048]{1,0:T(8,128)(2,1)S(1)}, u32[]{:S(2)}, u32[]{:S(2)}) %collective-permute-start.4) | collective-permute-done | bytes 1114144 | tf_op jit(solution)/shard_map/ppermute | solution.py:1041
  196.0 1.0 copy-done.14
  197.0 1.5 pad_maximum_fusion.1.refs_1_
  198.5 0.1 collective-permute-start.5
  198.6 4.5 collective-permute-done.5.refs_2_
  203.0 47.6 %served_forward.3 = (bf16[8,2,112,512]{3,2,1,0:T(8,128)(2,1)}, bf16[2,896,2048]{2,1,0:T(8,128)(2,1)}, bf16[2,896,2048]{2,1,0:T(8,128)(2,1)}, bf16[2,896,512]{2,1,0:T(8,128)(2,1)}) custom-call(bf16[8,2,112,512]{3,2,1,0:T(8,128)(2,1)} %get-tuple-element.97.refs_0_, bf16[2,272,2048]{2,1,0:T(8,128)(2,1)} %copy-done.11, ...), custom_call_target="tpu_custom_call" | custom-call | flops 48000000000 | bytes 144000000 | tf_op jit(solution)/shard_map/served_forward/pallas_call | solution.py:747
  250.7 7.7 %turn.1 = (f32[1024,512]{1,0:T(8,128)}, f32[2,416,512]{2,1,0:T(8,128)}, f32[2,416,128]{2,1,0:T(8,128)}, bf16[8,2,112,512]{3,2,1,0:T(8,128)(2,1)}) custom-call(bf16[8,2,112,512]{3,2,1,0:T(8,128)(2,1)} %get-tuple-element.99.back_ref, f32[2,416,512]{2,1,0:T(8,128)} %get-tuple-element.100.x1_old.refs_5_, f32[2,416,128]{2,1,0:T(8,128)} %get-tuple-element.101.router_old.refs_3_, ...), custom_call_target="tpu_custom_call" | custom-call | flops 8000000000 | bytes 24000000 | tf_op jit(solution)/shard_map/turn/pallas_call | solution.py:471
  258.3 80.9 %served_back.2 = (bf16[8,2,112,512]{3,2,1,0:T(8,128)(2,1)}, bf16[2,272,2048]{2,1,0:T(8,128)(2,1)}, bf16[2,272,2048]{2,1,0:T(8,128)(2,1)}) custom-call(bf16[8,2,112,512]{3,2,1,0:T(8,128)(2,1)} %get-tuple-element.103.refs_0_, bf16[2,272,2048]{2,1,0:T(8,128)(2,1)} %copy-done.11, bf16[2,272,2048]{2,1,0:T(8,128)(2,1)} %collective-permute-done.5.refs_2_, ...), custom_call_target="tpu_custom_call" | custom-call | flops 60000002048 | bytes 180000000 | tf_op jit(solution)/shard_map/served_back/pallas_call | solution.py:859
  339.2 0.1 collective-permute-start.6
  339.3 28.1 %attn_back.1 = (f32[2,416,512]{2,1,0:T(8,128)}, f32[2,416,128]{2,1,0:T(8,128)}, bf16[8,2,112,512]{3,2,1,0:T(8,128)(2,1)}, bf16[4,544,512]{2,1,0:T(8,128)(2,1)}) custom-call(bf16[8,2,112,512]{3,2,1,0:T(8,128)(2,1)} %get-tuple-element.109.refs_0_, f32[2,416,512]{2,1,0:T(8,128)} %get-tuple-element.110.refs_1_, f32[2,416,128]{2,1,0:T(8,128)} %get-tuple-element.111.refs_2_, ...), custom_call_target="tpu_custom_call" | custom-call | flops 28000000000 | bytes 84000000 | tf_op jit(solution)/shard_map/attn_back/pallas_call | solution.py:471
  367.5 1.5 copy-done.10
  369.1 2.4 convert_add_fusion.1
  371.5 2.0 copy-done.1
  373.6 0.2 select_convert_fusion.1
  373.8 2.1 collective-permute-start.7
  375.9 113.8 %served_back.3 = (bf16[8,2,112,512]{3,2,1,0:T(8,128)(2,1)}, bf16[2,272,2048]{2,1,0:T(8,128)(2,1)}, bf16[2,272,2048]{2,1,0:T(8,128)(2,1)}) custom-call(bf16[8,2,112,512]{3,2,1,0:T(8,128)(2,1)} %get-tuple-element.120.refs_0_, bf16[2,272,2048]{2,1,0:T(8,128)(2,1)} %copy-done.8, bf16[2,272,2048]{2,1,0:T(8,128)(2,1)} %collective-permute-done.3.refs_2_, ...), custom_call_target="tpu_custom_call" | custom-call | flops 60000002048 | bytes 180000000 | tf_op jit(solution)/shard_map/served_back/pallas_call | solution.py:859
  490.5 2.8 fusion.8
  493.3 3.5 convert_select_fusion.refs_1_
  496.9 2.4 convert_add_fusion
  499.4 2.1 copy-done
  501.4 1.2 select_convert_fusion
  502.6 0.3 collective-permute-start.9
  502.9 1.1 collective-permute-start.11
  504.0 24.8 %attn_last.1 = (f32[1024,512]{1,0:T(8,128)}, bf16[4,544,512]{2,1,0:T(8,128)(2,1)}) custom-call(bf16[8,2,112,512]{3,2,1,0:T(8,128)(2,1)} %get-tuple-element.127.refs_0_, f32[2,416,512]{2,1,0:T(8,128)} %get-tuple-element.128.refs_1_, f32[2,416,128]{2,1,0:T(8,128)} %get-tuple-element.129.refs_2_, f32[2,416,128]{2,1,0:T(8,128)} %get-tuple-element.94.router_old.refs_13_.refs_3_, ...), custom_call_target="tpu_custom_call" | custom-call | flops 24999999488 | bytes 75000000 | tf_op jit(solution)/shard_map/attn_last/pallas_call | solution.py:471
  528.7 70.9 %all-reduce.2.cloned.1.call-done.refs_5_ = bf16[544,512]{1,0:T(8,128)(2,1)} async-done(((bf16[544,512]{1,0:T(8,128)(2,1)}), bf16[544,512]{1,0:T(8,128)(2,1)}) %all-reduce.2.cloned.1.call-update) | async-done | bytes 557072 | tf_op jit(solution)/shard_map/psum | solution.py:1307
  599.7 1.1 slice_bitcast_fusion.4
  600.8 2.8 fusion.7
  603.5 1.7 collective-permute-start.10
  605.2 69.8 %dense_sum.1.refs_4_ = bf16[544,512]{1,0:T(8,128)(2,1)} custom-call(bf16[4,544,512]{2,1,0:T(8,128)(2,1)} %get-tuple-element.140.g_ref), custom_call_target="tpu_custom_call" | custom-call | flops 49999998976 | bytes 150000000 | tf_op jit(solution)/shard_map/dense_sum/pallas_call | solution.py:953
  675.0 1.1 slice_bitcast_fusion.5
  676.1 0.1 maximum_convert_fusion
  676.2 3.0 copy.42
  679.2 3.4 convert_select_fusion.1.refs_0_
  682.6 5.9 finish.1
  688.5 15.1 %scalar_sum.1 = f32[8,128]{1,0:T(8,128)} custom-call(f32[8,128]{1,0:T(8,128)} %get-tuple-element.142.x_ref), custom_call_target="tpu_custom_call" | custom-call | flops 10000000000 | bytes 30000000 | tf_op jit(solution)/shard_map/scalar_sum/pallas_call | solution.py:1014
  703.6 1.2 slice.39
  705.5 3.5 fusion.3
  709.1 3.0 copy.43
  712.0 3.0 copy.44
  715.0 3.0 copy.45
  718.0 0.6 add_multiply_fusion.1
  718.6 5.7 add_multiply_fusion
  (50 shorter events, 0.3 us)
Async XLA Ops:
  7.2 7.0 copy-start.2
  7.2 489.7 %reduce-scatter.2.cloned.1.call-start = ((), (), s32[]{:S(2)}) async-start(), calls=%async_computation.1 | async-start | bytes 2785280 | tf_op jit(solution)/shard_map/reduce_scatter | solution.py:1307
  10.1 52.7 %collective-permute-start = (bf16[272,2048]{1,0:T(8,128)(2,1)}, bf16[272,2048]{1,0:T(8,128)(2,1)S(1)}, u32[]{:S(2)}, u32[]{:S(2)}) collective-permute-start(bf16[272,2048]{1,0:T(8,128)(2,1)} %pack.3), channel_id=1, source_target_pairs={{0,4},{1,5},{2,6},{3,7},{4,0},{5,1},{6,2},{7,3},{8,12},{9,13},{10,... | collective-permute-start | bytes 3342344 | tf_op jit(solution)/shard_map/ppermute | solution.py:1041
  46.7 16.1 %copy-start.12 = (bf16[272,2048]{1,0:T(8,128)(2,1)S(1)}, bf16[272,2048]{1,0:T(8,128)(2,1)}, u32[]{:S(2)}) copy-start(bf16[272,2048]{1,0:T(8,128)(2,1)} %pack.3) | copy-start | bytes 3342340
  63.9 25.9 %collective-permute-start.2 = (bf16[272,2048]{1,0:T(8,128)(2,1)}, bf16[272,2048]{1,0:T(8,128)(2,1)S(1)}, u32[]{:S(2)}, u32[]{:S(2)}) collective-permute-start(bf16[272,2048]{1,0:T(8,128)(2,1)} %get-tuple-element.81), channel_id=1, source_target_pairs={{0,16},{1,17},{2,18},{3,19},{4,20},{5,21},{6,22},{7,23},{8,24},{9,... | collective-permute-start | bytes 3342344 | tf_op jit(solution)/shard_map/ppermute | solution.py:1041
  89.9 1.0 copy-start.16
  92.3 3.5 copy-start.8
  92.3 4.5 collective-permute-start.3
  95.8 71.4 %collective-permute-start.1 = (bf16[272,2048]{1,0:T(8,128)(2,1)}, bf16[272,2048]{1,0:T(8,128)(2,1)S(1)}, u32[]{:S(2)}, u32[]{:S(2)}) collective-permute-start(bf16[272,2048]{1,0:T(8,128)(2,1)} %pack.2), channel_id=1, source_target_pairs={{0,4},{1,5},{2,6},{3,7},{4,0},{5,1},{6,2},{7,3},{8,12},{9,13},{10,... | collective-permute-start | bytes 3342344 | tf_op jit(solution)/shard_map/ppermute | solution.py:1041
  97.4 70.7 %copy-start.13 = (bf16[272,2048]{1,0:T(8,128)(2,1)S(1)}, bf16[272,2048]{1,0:T(8,128)(2,1)}, u32[]{:S(2)}) copy-start(bf16[272,2048]{1,0:T(8,128)(2,1)} %pack.2) | copy-start | bytes 3342340
  167.2 1.0 copy-start.15
  169.6 26.5 %collective-permute-start.4 = (bf16[272,2048]{1,0:T(8,128)(2,1)S(1)}, bf16[272,2048]{1,0:T(8,128)(2,1)S(1)}, u32[]{:S(2)}, u32[]{:S(2)}) collective-permute-start(bf16[272,2048]{1,0:T(8,128)(2,1)S(1)} %get-tuple-element.185), channel_id=1, source_target_pairs={{0,16},{1,17},{2,18},{3,19},{4,20},{5,21},{6,22},{7,23},{8,24},{9,... | collective-permute-start | bytes 3342344 | tf_op jit(solution)/shard_map/ppermute | solution.py:1041
  196.0 1.0 copy-start.14
  198.5 4.6 copy-start.11
  198.5 4.5 collective-permute-start.5
  339.2 28.3 %collective-permute-start.6 = (bf16[2,272,2048]{2,1,0:T(8,128)(2,1)}, bf16[2,272,2048]{2,1,0:T(8,128)(2,1)}, u32[]{:S(2)}, u32[]{:S(2)}) collective-permute-start(bf16[2,272,2048]{2,1,0:T(8,128)(2,1)} %get-tuple-element.108), channel_id=1, source_target_pairs={{0,8},{1,9},{2,10},{3,11},{4,12},{5,13},{6,14},{7,15},{8,0},{9,1},... | collective-permute-start | bytes 6684680 | tf_op jit(solution)/shard_map/ppermute | solution.py:1041
  367.4 1.6 copy-start.10
  367.5 232.2 %all-reduce.2.cloned.1.call-start = ((), (), s32[]{:S(2)}) async-start(), calls=%async_computation.2 | async-start | bytes 1114112 | tf_op jit(solution)/shard_map/psum | solution.py:1307
  371.5 2.0 copy-start.1
  373.8 116.8 %collective-permute-start.7 = (bf16[272,2048]{1,0:T(8,128)(2,1)S(1)}, bf16[272,2048]{1,0:T(8,128)(2,1)S(1)}, u32[]{:S(2)}, u32[]{:S(2)}) collective-permute-start(bf16[272,2048]{1,0:T(8,128)(2,1)S(1)} %select_convert_fusion.1), channel_id=1, source_target_pairs={{0,16},{1,17},{2,18},{3,19},{4,20},{5,21},{6,22},{7,23},{8,24},{9,... | collective-permute-start | bytes 3342344 | tf_op jit(solution)/shard_map/ppermute | solution.py:1041
  489.7 7.2 collective-permute-start.8
  493.3 3.6 copy-start.9
  499.3 2.1 copy-start
  502.6 98.1 %collective-permute-start.9 = (bf16[272,2048]{1,0:T(8,128)(2,1)}, bf16[272,2048]{1,0:T(8,128)(2,1)S(1)}, u32[]{:S(2)}, u32[]{:S(2)}) collective-permute-start(bf16[272,2048]{1,0:T(8,128)(2,1)} %select_convert_fusion), channel_id=1, source_target_pairs={{0,16},{1,17},{2,18},{3,19},{4,20},{5,21},{6,22},{7,23},{8,24},{9,... | collective-permute-start | bytes 3342344 | tf_op jit(solution)/shard_map/ppermute | solution.py:1041
  502.9 179.7 %collective-permute-start.11 = (bf16[272,2048]{1,0:T(8,128)(2,1)}, bf16[272,2048]{1,0:T(8,128)(2,1)}, u32[]{:S(2)}, u32[]{:S(2)}) collective-permute-start(bf16[272,2048]{1,0:T(8,128)(2,1)} %fusion.8), channel_id=1, source_target_pairs={{0,4},{1,5},{2,6},{3,7},{4,0},{5,1},{6,2},{7,3},{8,12},{9,13},{10,... | collective-permute-start | bytes 3342344 | tf_op jit(solution)/shard_map/ppermute | solution.py:1041
  603.5 79.0 %collective-permute-start.10 = (bf16[272,2048]{1,0:T(8,128)(2,1)}, bf16[272,2048]{1,0:T(8,128)(2,1)}, u32[]{:S(2)}, u32[]{:S(2)}) collective-permute-start(bf16[272,2048]{1,0:T(8,128)(2,1)} %fusion.7), channel_id=1, source_target_pairs={{0,4},{1,5},{2,6},{3,7},{4,0},{5,1},{6,2},{7,3},{8,12},{9,13},{10,... | collective-permute-start | bytes 3342344 | tf_op jit(solution)/shard_map/ppermute | solution.py:1041
  688.5 17.0 %copy-start.3 = (f32[2,516,512]{2,0,1:T(2,128)S(1)}, f32[2,516,512]{2,0,1:T(2,128)}, u32[]{:S(2)}) copy-start(f32[2,516,512]{2,0,1:T(2,128)} %param.21) | copy-start | bytes 6340612
  705.5 13.1 %copy-start.7 = (f32[2,1,256,2048]{3,2,1,0:T(8,128)S(1)}, f32[2,1,256,2048]{3,2,1,0:T(8,128)}, u32[]{:S(2)}) copy-start(f32[2,1,256,2048]{3,2,1,0:T(8,128)} %get-tuple-element.167) | copy-start | bytes 12582916
  709.1 9.6 %copy-start.6 = (f32[2,1,256,2048]{3,2,1,0:T(8,128)S(1)}, f32[2,1,256,2048]{3,2,1,0:T(8,128)}, u32[]{:S(2)}) copy-start(f32[2,1,256,2048]{3,2,1,0:T(8,128)} %param.25) | copy-start | bytes 12582916
  712.0 6.6 copy-start.5
  715.0 3.0 copy-start.17
  715.0 3.0 copy-start.18
  715.0 3.0 copy-start.19
  715.0 3.0 copy-start.20
  715.0 3.6 copy-start.4
Sparse Core Ops, SparseCore 0:
  367.6 55.9 reduce-scatter.1
  497.0 102.6 all-reduce.1
